TPU v7x, 128 devices: a whole 4x4x4 slice. The times are simulated.
128 devices in a mesh: tile: 64 (over x, z, y_lo, core), split: 2 (over y_hi).
Axes of the slice: x: 4, y: 4 (y_hi: 2, y_lo: 2; y = y_hi * 2 + y_lo), z: 4, core: 2. Of those that a mesh axis runs over, the one named last changes fastest.
Arguments:
- noisy_image: bfloat16 [64, 45, 128, 128], P('tile', None, 'split'), may hold values from -60 to 60
- seam_codes: int32 [64, 4], replicated, may hold values from 0 to 3
- timestep: int32 [1], replicated, may hold values from 0 to 999
- time_weight: float32 [48, 192], replicated, may hold values from -0.875 to 0.875
- bias_upper: float32 [192, 48], replicated, may hold values from -0.875 to 0.875
- bias_lower: float32 [192, 96], replicated, may hold values from -0.875 to 0.875
- kernel_upper_first: bfloat16 [3, 3, 48, 45], replicated, may hold values from -0.3125 to 0.3125
- kernel_upper_second: bfloat16 [3, 3, 48, 48], replicated, may hold values from -0.3125 to 0.3125
- kernel_lower_first: bfloat16 [3, 3, 96, 48], replicated, may hold values from -0.3125 to 0.3125
- kernel_lower_second: bfloat16 [3, 3, 96, 96], replicated, may hold values from -0.21875 to 0.21875
- kernel_decode_first: bfloat16 [3, 3, 48, 144], replicated, may hold values from -0.15625 to 0.15625
- kernel_decode_second: bfloat16 [3, 3, 48, 48], replicated, may hold values from -0.3125 to 0.3125
- output_weight: bfloat16 [45, 48], replicated, may hold values from -0.875 to 0.875
- gains_upper: float32 [4, 48], replicated, may hold values from 0.25 to 1.75
- shifts_upper: float32 [4, 48], replicated, may hold values from -1 to 1
- gains_lower: float32 [2, 96], replicated, may hold values from 0.25 to 1.75
- shifts_lower: float32 [2, 96], replicated, may hold values from -1 to 1
Outputs:
- predicted_noise: bfloat16 [64, 45, 128, 128], P('tile', None, 'split')
All inputs are finite; a program needn't handle non-finite values.
Results may differ from a plain program's by a relative error of at most 0.018.
Values may be sent and summed in bfloat16 or wider, within the bound.
No kernel may reach another device: no remote copies, remote signals or barrier semaphores. Data moves between devices by JAX's collectives and lax.ppermute only.
A program may use at most 128 MiB of HBM per device.

v0:
```python
import math

import jax
import jax.numpy as jnp
from jax import lax
from jax.experimental import pallas as pl
from jax.experimental.pallas import tpu as pltpu
from jax.sharding import Mesh
from jax.sharding import PartitionSpec as P

GROUPS = 8
ROW_TILES = 4
TILE = ("tile_0", "tile_1", "tile_2", "tile_3")
TILE_SPLIT = ("tile_0", "tile_1", "tile_2", "tile_3", "split")
EPSILON = 1e-05
LANES = 128
F32 = jnp.float32
BF16 = jnp.bfloat16


def lane_index(shape):
    return lax.broadcasted_iota(jnp.int32, shape, 1)


def turn(value, amount):
    return pltpu.roll(value, amount, 1)


def group_index(channels, shape):
    row = lax.broadcasted_iota(jnp.int32, shape, 0)
    return (row * 43) >> (8 if channels == 48 else 9)


def column_of(row_value, channels):
    shape = (channels, row_value.shape[1])
    on_diagonal = lax.broadcasted_iota(jnp.int32, shape, 0) == lane_index(shape)
    return jnp.sum(jnp.where(on_diagonal, jnp.broadcast_to(row_value, shape), 0.0), axis=1, keepdims=True)


def coefficients(stats, gain_row, shift_row, bias_row, channels, pixels):
    devices = stats.shape[0]
    count = pixels * (channels // GROUPS)
    mean_row = jnp.sum(stats, axis=0, keepdims=True) * (1.0 / devices)
    apart = jnp.sum(jnp.square(stats - mean_row), axis=0, keepdims=True) * (1.0 / devices)
    shape = (channels, LANES)
    group = group_index(channels, shape)
    lane = lane_index(shape)

    def pick(row_value, first):
        return jnp.sum(jnp.where(lane == group + first, jnp.broadcast_to(row_value, shape), 0.0), axis=1, keepdims=True)

    mean = pick(mean_row, 0)
    spread = pick(mean_row, GROUPS) * (1.0 / count) + pick(apart, 0)
    slope = lax.rsqrt(spread + EPSILON) * column_of(gain_row, channels)
    offset = column_of(shift_row, channels) - mean * slope
    if bias_row is not None:
        offset = offset + column_of(bias_row, channels) * slope
    return jnp.broadcast_to(slope * 0.5, shape), jnp.broadcast_to(offset * 0.5, shape)


def activate(value, coef):
    half = value.astype(F32) * coef[0] + coef[1]
    return (half + half * jnp.tanh(half)).astype(BF16)


def group_stats(sums, squares, bias_row, channels, pixels, width):
    shape = (channels, LANES)
    lane = lane_index(shape)
    group = group_index(channels, shape)
    inside = lane < width
    mean = jnp.sum(jnp.where(inside, sums, 0.0), axis=1, keepdims=True) * (1.0 / pixels)
    second = jnp.sum(jnp.where(inside, squares, 0.0), axis=1, keepdims=True)
    spread = jnp.maximum(second - pixels * jnp.square(mean), 0.0)
    if bias_row is not None:
        mean = mean + column_of(bias_row, channels)
    group_size = channels // GROUPS
    mean_row = jnp.sum(jnp.where(lane == group, mean, 0.0), axis=0, keepdims=True) * (1.0 / group_size)
    group_mean = jnp.sum(jnp.where(lane == group, mean_row, 0.0), axis=1, keepdims=True)
    total = spread + pixels * jnp.square(mean - group_mean)
    return mean_row + jnp.sum(jnp.where(lane == group + GROUPS, total, 0.0), axis=0, keepdims=True)


def frame_rows(taps, first, channels, width, block_rows, rows_of, upper, lower, west, east, place, together=4):
    stride = taps.shape[1] // 3
    lane = lane_index((channels, LANES))
    base = place * block_rows
    hold_west = turn(west, (LANES + 1 - base) % LANES)
    hold_east = turn(east, (LANES + width - base) % LANES)

    def put(row, value, hw, he):
        taps[row, pl.ds(first, channels)] = jnp.where(lane == 0, hw, turn(value, 1))
        taps[row, pl.ds(stride + first, channels)] = value
        taps[row, pl.ds(2 * stride + first, channels)] = jnp.where(lane == width - 1, he, turn(value, LANES - 1))

    zero = jnp.zeros((channels, LANES), BF16)
    put(0, upper, jnp.where(place == 0, zero, hold_west), jnp.where(place == 0, zero, hold_east))

    def body(step, carry):
        hw, he = carry
        for k in range(together):
            row = step * together + k
            hw, he = turn(hw, LANES - 1), turn(he, LANES - 1)
            put(row + 1, rows_of(row), hw, he)
        return hw, he

    hw, he = lax.fori_loop(0, block_rows // together, body, (hold_west, hold_east))
    hw, he = turn(hw, LANES - 1), turn(he, LANES - 1)
    put(block_rows + 1, lower, jnp.where(place == 1, zero, hw), jnp.where(place == 1, zero, he))


def convolve_rows(taps, weight_ref, raw_ref, block_rows, together=4):
    outputs = weight_ref.shape[0]
    depth = taps.shape[1] * 3
    weight = weight_ref[...]
    zero = jnp.zeros((outputs, LANES), F32)

    def body(step, carry):
        sums, squares = carry
        row = step * together
        for k in range(0, together, 2):
            window = jnp.concatenate(
                [taps[pl.ds(row + k + j, 3)].reshape(depth, LANES) for j in range(2)], axis=1
            )
            both = jnp.dot(weight, window, preferred_element_type=F32)
            for j in range(2):
                value = both[:, j * LANES : (j + 1) * LANES]
                raw_ref[row + k + j] = value
                sums = sums + value
                squares = squares + value * value
        return sums, squares

    return lax.fori_loop(0, block_rows // together, body, (zero, zero))


def pack_edges(raw_ref, pack_ref, block_rows, channels, width, depth, place, together=8):
    size = depth * channels
    lane = lane_index((channels, LANES))
    last = block_rows - 1
    for d in range(depth):
        outer = jnp.where(place == 0, d, last - d)
        pack_ref[pl.ds(d * channels, channels)] = raw_ref[outer].astype(BF16)
        pack_ref[pl.ds(size + d * channels, channels)] = raw_ref[last - outer].astype(BF16)

    def body(step, carry):
        carry = list(carry)
        for k in range(together):
            row = step * together + k
            value = raw_ref[row].astype(F32)
            for d in range(depth):
                line = jnp.where(lane == row, jnp.broadcast_to(value[:, d : d + 1], lane.shape), carry[d])
                right = width - 1 - d
                carry[d] = jnp.where(
                    lane == block_rows + row, jnp.broadcast_to(value[:, right : right + 1], lane.shape), line
                )
        return tuple(carry)

    zero = jnp.zeros((channels, LANES), F32)
    columns = lax.fori_loop(0, block_rows // together, body, (zero,) * depth)
    for d in range(depth):
        pack_ref[pl.ds(2 * size + d * channels, channels)] = columns[d].astype(BF16)


def finish(taps, weight_ref, raw_ref, pack_ref, stat_ref, bias_row, block_rows, channels, width, depth, place):
    sums, squares = convolve_rows(taps, weight_ref, raw_ref, block_rows)
    stat_ref[...] = group_stats(sums, squares, bias_row, channels, float(block_rows * width), width)
    if pack_ref is not None:
        pack_edges(raw_ref, pack_ref, block_rows, channels, width, depth, place)


WHOLE = pl.BlockSpec(memory_space=pltpu.VMEM)
SCALARS = pl.BlockSpec(memory_space=pltpu.SMEM)


def call(body, operands, outs, scratch=()):
    return pl.pallas_call(
        body,
        in_specs=[SCALARS] + [WHOLE] * (len(operands) - 1),
        out_specs=[WHOLE] * len(outs),
        out_shape=[jax.ShapeDtypeStruct(s, d) for s, d in outs],
        scratch_shapes=list(scratch),
        compiler_params=pltpu.CompilerParams(vmem_limit_bytes=48 * 1024 * 1024),
    )(*operands)


def edges_of_image(scalars, image):
    block_rows, channels, width = image.shape

    def body(sc, image_ref, pack_ref):
        pack_edges(image_ref, pack_ref, block_rows, channels, width, 1, sc[0])

    return call(body, (scalars, image), [((3 * channels, LANES), BF16)])[0]


def strips(scalars, pack, partner, width):
    size = pack.shape[0] // 3
    half = width // 2

    def body(sc, mine_ref, their_ref, ns_ref, east_ref, west_ref, side_ref):
        place = sc[0]
        lane = lane_index((size, LANES))

        def ordered(first):
            mine, theirs = mine_ref[pl.ds(first, size)], their_ref[pl.ds(first, size)]
            return jnp.where(place == 0, mine, theirs), jnp.where(place == 0, theirs, mine)

        low, high = ordered(0)
        side_ref[0] = low
        side_ref[2] = high
        low, high = ordered(2 * size)
        side_ref[3] = jnp.where(lane < half, low, turn(high, half))
        side_ref[1] = jnp.where(lane < half, turn(low, LANES - half), high)
        shape = (LANES, LANES)
        row, column = lax.broadcasted_iota(jnp.int32, shape, 0), lane_index(shape)
        for k, out in enumerate((ns_ref, east_ref, west_ref)):
            reverse = sc[2 + 2 * k]
            hit = jnp.where(reverse == 1, width - 1 - row, row) == column
            order = jnp.where(hit & (column < width), 1.0, 0.0).astype(BF16)
            strip = jnp.where(lane < width, side_ref[sc[1 + 2 * k]], jnp.zeros((size, LANES), BF16))
            out[...] = jnp.dot(strip, order, preferred_element_type=F32).astype(BF16)

    outs = [((size, LANES), BF16)] * 3
    return call(body, (scalars, pack, partner), outs, [pltpu.VMEM((4, size, LANES), BF16)])


def above_below(place, facing, inner):
    return jnp.where(place == 0, facing, inner), jnp.where(place == 0, inner, facing)


def first_stage(scalars, image, partner, ns, east, west, weight, bias):
    block_rows, channels, width = image.shape
    outputs = weight.shape[0]

    def body(sc, image_ref, partner_ref, ns_ref, east_ref, west_ref, weight_ref, bias_ref, raw_ref, pack_ref, stat_ref, taps):
        place = sc[0]
        upper, lower = above_below(place, ns_ref[...], partner_ref[pl.ds(channels, channels)])
        frame_rows(
            taps, 0, channels, width, block_rows, lambda r: image_ref[r], upper, lower, west_ref[...], east_ref[...], place
        )
        finish(taps, weight_ref, raw_ref, pack_ref, stat_ref, bias_ref[...], block_rows, outputs, width, 1, place)

    return call(
        body,
        (scalars, image, partner, ns, east, west, weight, bias),
        [((block_rows, outputs, LANES), F32), ((3 * outputs, LANES), BF16), ((1, LANES), F32)],
        [pltpu.VMEM((block_rows + 2, 3 * channels, LANES), BF16)],
    )


def plain_stage(scalars, raw, stats, partner, ns, east, west, weight, gain, shift, bias, width, depth):
    block_rows, channels, _ = raw.shape
    outputs = weight.shape[0]
    biased = bias is not None

    def body(sc, raw_in, stats_ref, partner_ref, ns_ref, east_ref, west_ref, weight_ref, gain_ref, shift_ref, *rest):
        bias_row = None
        if biased:
            bias_row, rest = rest[0][...], rest[1:]
        if depth:
            raw_ref, stat_ref, pack_ref, taps = rest
        else:
            raw_ref, stat_ref, taps = rest
            pack_ref = None
        place = sc[0]
        coef = coefficients(
            stats_ref[...], gain_ref[...], shift_ref[...], bias_row, channels, float(block_rows * width)
        )
        lane = lane_index((channels, LANES))
        clear = jnp.zeros((channels, LANES), BF16)

        def strip(ref):
            return jnp.where(lane < width, activate(ref[...], coef), clear)

        upper, lower = above_below(place, strip(ns_ref), activate(partner_ref[pl.ds(channels, channels)], coef))
        frame_rows(
            taps,
            0,
            channels,
            width,
            block_rows,
            lambda r: activate(raw_in[r], coef),
            upper,
            lower,
            strip(west_ref),
            strip(east_ref),
            place,
        )
        finish(taps, weight_ref, raw_ref, pack_ref, stat_ref, None, block_rows, outputs, width, depth, place)

    outs = [((block_rows, outputs, LANES), F32), ((1, LANES), F32)]
    if depth:
        outs.append(((3 * depth * outputs, LANES), BF16))
    operands = (scalars, raw, stats, partner, ns, east, west, weight, gain, shift)
    if biased:
        operands += (bias,)
    return call(body, operands, outs, [pltpu.VMEM((block_rows + 2, 3 * channels, LANES), BF16)])


def pool_stage(scalars, raw, stats, partner, ns, east, west, weight, gain, shift, bias):
    block_rows, channels, width = raw.shape
    low_rows, low_width = block_rows // 2, width // 2
    outputs = weight.shape[0]

    def body(
        sc, raw_in, stats_ref, partner_ref, ns_ref, east_ref, west_ref, weight_ref, gain_ref, shift_ref, bias_ref,
        skip_ref, side_ref, raw_ref, pack_ref, stat_ref, taps, pooled,
    ):
        place = sc[0]
        coef = coefficients(stats_ref[...], gain_ref[...], shift_ref[...], None, channels, float(block_rows * width))
        shape = (2 * LANES, LANES)
        row, column = lax.broadcasted_iota(jnp.int32, shape, 0), lane_index(shape)
        gather = jnp.where(((row & (LANES - 1)) >> 1) == column, 0.25, 0.0).astype(BF16)

        def pool(outer, second):
            both = jnp.concatenate([outer, second], axis=1)
            return jnp.dot(both, gather, preferred_element_type=F32).astype(BF16)

        def lines(ref, first):
            return activate(ref[pl.ds(first, channels)], coef), activate(ref[pl.ds(first + channels, channels)], coef)

        ns_lines, east_lines, west_lines = lines(ns_ref, 0), lines(east_ref, 0), lines(west_ref, 0)
        inner_lines = lines(partner_ref, 2 * channels)
        upper, lower = above_below(place, ns_lines[0], inner_lines[0])
        side_ref[0] = upper
        side_ref[1] = lower
        side_ref[2] = west_lines[0]
        side_ref[3] = east_lines[0]

        def make(step, carry):
            for k in range(2):
                row = step * 2 + k
                first = activate(raw_in[2 * row], coef)
                second = activate(raw_in[2 * row + 1], coef)
                skip_ref[2 * row] = first
                skip_ref[2 * row + 1] = second
                pooled[row] = pool(first, second)
            return carry

        lax.fori_loop(0, low_rows // 2, make, 0)
        upper, lower = above_below(place, pool(*ns_lines), pool(*inner_lines))
        frame_rows(
            taps,
            0,
            channels,
            low_width,
            low_rows,
            lambda r: pooled[r],
            upper,
            lower,
            pool(*west_lines),
            pool(*east_lines),
            place,
        )
        finish(taps, weight_ref, raw_ref, pack_ref, stat_ref, bias_ref[...], low_rows, outputs, low_width, 1, place)

    return call(
        body,
        (scalars, raw, stats, partner, ns, east, west, weight, gain, shift, bias),
        [
            ((block_rows, channels, LANES), BF16),
            ((4, channels, LANES), BF16),
            ((low_rows, outputs, LANES), F32),
            ((3 * outputs, LANES), BF16),
            ((1, LANES), F32),
        ],
        [pltpu.VMEM((low_rows + 2, 3 * channels, LANES), BF16), pltpu.VMEM((low_rows, channels, LANES), BF16)],
    )


def decode_stage(scalars, raw, stats, partner, ns, east, west, skip, sides, weight, gain, shift):
    low_rows, channels, _ = raw.shape
    block_rows, skip_channels, width = skip.shape
    low_width = width // 2
    joined = channels + skip_channels
    outputs = weight.shape[0]

    def body(
        sc, raw_in, stats_ref, partner_ref, ns_ref, east_ref, west_ref, skip_ref, side_ref, weight_ref, gain_ref, shift_ref,
        raw_ref, pack_ref, stat_ref, taps, wide,
    ):
        place = sc[0]
        coef = coefficients(
            stats_ref[...], gain_ref[...], shift_ref[...], None, channels, float(low_rows * low_width)
        )
        shape = (LANES, LANES)
        row, column = lax.broadcasted_iota(jnp.int32, shape, 0), lane_index(shape)
        spread = jnp.where(row == column >> 1, 1.0, 0.0).astype(BF16)

        lane = lane_index((channels, LANES))

        def widen(value):
            kept = jnp.where(lane < low_width, activate(value, coef), jnp.zeros((channels, LANES), BF16))
            return jnp.dot(kept, spread, preferred_element_type=F32).astype(BF16)

        def make(step, carry):
            for k in range(4):
                row = step * 4 + k
                wide[row] = widen(raw_in[row])
            return carry

        lax.fori_loop(0, low_rows // 4, make, 0)
        upper, lower = above_below(place, widen(ns_ref[...]), widen(partner_ref[pl.ds(channels, channels)]))
        frame_rows(
            taps,
            0,
            channels,
            width,
            block_rows,
            lambda r: wide[r >> 1],
            upper,
            lower,
            widen(west_ref[...]),
            widen(east_ref[...]),
            place,
            2,
        )
        frame_rows(
            taps,
            channels,
            skip_channels,
            width,
            block_rows,
            lambda r: skip_ref[r],
            side_ref[0],
            side_ref[1],
            side_ref[2],
            side_ref[3],
            place,
        )
        finish(taps, weight_ref, raw_ref, pack_ref, stat_ref, None, block_rows, outputs, width, 1, place)

    return call(
        body,
        (scalars, raw, stats, partner, ns, east, west, skip, sides, weight, gain, shift),
        [((block_rows, outputs, LANES), F32), ((3 * outputs, LANES), BF16), ((1, LANES), F32)],
        [pltpu.VMEM((block_rows + 2, 3 * joined, LANES), BF16), pltpu.VMEM((low_rows, channels, LANES), BF16)],
    )


def project_stage(scalars, raw, stats, weight, gain, shift, kept):
    block_rows, channels, width = raw.shape

    def body(sc, raw_in, stats_ref, weight_ref, gain_ref, shift_ref, out_ref):
        coef = coefficients(stats_ref[...], gain_ref[...], shift_ref[...], None, channels, float(block_rows * width))
        project = weight_ref[...]

        def make(step, carry):
            for k in range(0, 4, 2):
                row = step * 4 + k
                both = jnp.concatenate([activate(raw_in[row], coef), activate(raw_in[row + 1], coef)], axis=1)
                result = jnp.dot(project, both, preferred_element_type=F32).astype(BF16)
                out_ref[row] = result[:kept, :LANES]
                out_ref[row + 1] = result[:kept, LANES:]
            return carry

        lax.fori_loop(0, block_rows // 4, make, 0)

    return call(body, (scalars, raw, stats, weight, gain, shift), [((block_rows, kept, LANES), BF16)])[0]


def shift_tiles(value, steps):
    count = lax.axis_size(TILE)
    return lax.ppermute(value, TILE, [(t, (t + steps) % count) for t in range(count)])


def vertical(value):
    count = lax.axis_size(TILE)
    pairs = []
    for t in range(count):
        pairs.append((2 * t, 2 * ((t + ROW_TILES) % count)))
        pairs.append((2 * t + 1, 2 * ((t - ROW_TILES) % count) + 1))
    return lax.ppermute(value, TILE_SPLIT, pairs)


def exchange(scalars, pack, width):
    partner = lax.ppermute(pack, "split", [(0, 1), (1, 0)])
    ns, east, west = strips(scalars, pack, partner, width)
    return partner, vertical(ns), shift_tiles(east, -1), shift_tiles(west, 1)


def share(stat):
    devices = lax.axis_size(TILE) * lax.axis_size("split")
    copies = jnp.broadcast_to(stat[None], (devices, 1, LANES))
    return lax.all_to_all(copies, TILE_SPLIT, 0, 0).reshape(devices, LANES)


def embedding(timestep, time_weight, bias_upper, bias_lower):
    moment = timestep[0].astype(F32)
    half_width = time_weight.shape[0] // 2
    frequencies = jnp.exp(-math.log(10000.0) * jnp.arange(half_width, dtype=F32) / half_width)
    angles = moment * frequencies
    features = jnp.concatenate([jnp.sin(angles), jnp.cos(angles)])[None, :]
    embedded = jax.nn.silu(jnp.dot(features, time_weight, precision=lax.Precision.HIGHEST))
    both = jnp.concatenate([bias_upper, bias_lower], axis=1)
    biases = jnp.dot(embedded, both, precision=lax.Precision.HIGHEST)
    return biases[:, : bias_upper.shape[1]], biases[:, bias_upper.shape[1] :]


def flat_kernel(kernel):
    return jnp.transpose(kernel, (2, 0, 1, 3)).reshape(kernel.shape[2], -1)


def seam_scalars(seam_codes):
    count = lax.axis_size(TILE)
    tile, place = lax.axis_index(TILE), lax.axis_index("split")

    def facing(target, side):
        k = (side + 2 + seam_codes[target % count, side]) % 4
        reverse = (k < 2) == (side < 2)
        return k, reverse.astype(jnp.int32)

    north = facing(tile + ROW_TILES, 0)
    south = facing(tile - ROW_TILES, 2)
    up = place == 0
    vertical_pick = (jnp.where(up, north[0], south[0]), jnp.where(up, north[1], south[1]))
    picks = vertical_pick + facing(tile - 1, 1) + facing(tile + 1, 3)
    return jnp.stack([place] + [p.astype(jnp.int32) for p in picks])


def per_device(
    noisy_image,
    seam_codes,
    timestep,
    time_weight,
    bias_upper,
    bias_lower,
    kernel_upper_first,
    kernel_upper_second,
    kernel_lower_first,
    kernel_lower_second,
    kernel_decode_first,
    kernel_decode_second,
    output_weight,
    gains_upper,
    shifts_upper,
    gains_lower,
    shifts_lower,
):
    scalars = seam_scalars(seam_codes)
    first_bias, second_bias = embedding(timestep, time_weight, bias_upper, bias_lower)
    channels, block_rows, width = noisy_image.shape[1:]
    padding = kernel_upper_first.shape[2] - channels
    image = jnp.transpose(jnp.pad(noisy_image[0], ((0, padding), (0, 0), (0, 0))), (1, 0, 2))
    upper_first = flat_kernel(jnp.pad(kernel_upper_first, ((0, 0), (0, 0), (0, 0), (0, padding))))
    low_width = width // 2

    pack = edges_of_image(scalars, image)
    received = exchange(scalars, pack, width)
    raw, pack, stat = first_stage(scalars, image, *received, upper_first, first_bias)

    stats, received = share(stat), exchange(scalars, pack, width)
    raw, stat, pack = plain_stage(
        scalars, raw, stats, *received, flat_kernel(kernel_upper_second), gains_upper[0:1], shifts_upper[0:1], first_bias,
        width, 2,
    )

    stats, received = share(stat), exchange(scalars, pack, width)
    skip, sides, raw, pack, stat = pool_stage(
        scalars, raw, stats, *received, flat_kernel(kernel_lower_first), gains_upper[1:2], shifts_upper[1:2], second_bias
    )

    stats, received = share(stat), exchange(scalars, pack, low_width)
    raw, stat, pack = plain_stage(
        scalars, raw, stats, *received, flat_kernel(kernel_lower_second), gains_lower[0:1], shifts_lower[0:1], second_bias,
        low_width, 1,
    )

    stats, received = share(stat), exchange(scalars, pack, low_width)
    raw, pack, stat = decode_stage(
        scalars, raw, stats, *received, skip, sides, flat_kernel(kernel_decode_first), gains_lower[1:2], shifts_lower[1:2]
    )

    stats, received = share(stat), exchange(scalars, pack, width)
    raw, stat = plain_stage(
        scalars, raw, stats, *received, flat_kernel(kernel_decode_second), gains_upper[2:3], shifts_upper[2:3], None, width, 0
    )

    project = jnp.pad(output_weight, ((0, padding), (0, 0)))
    result = project_stage(scalars, raw, share(stat), project, gains_upper[3:4], shifts_upper[3:4], channels)
    return jnp.transpose(result, (1, 0, 2))[None]


def solution(mesh):
    torus = Mesh(
        mesh.devices.reshape(4, 4, 2, 2, mesh.shape["split"]),
        ("tile_0", "tile_1", "tile_2", "tile_3", "split"),
    )
    return jax.shard_map(
        per_device,
        mesh=torus,
        in_specs=(P(TILE, None, "split", None),) + (P(),) * 16,
        out_specs=P(TILE, None, "split", None),
        check_vma=False,
    )
```

profile of v0, /device:TPU:1, one launch (start us, length us, event | category | flops | bytes accessed | tf_op | source)
XLA Modules:
  0.0 241.6 jit_solution(5497328129980942839)
XLA Ops:
  0.0 1.5 constant_dynamic-slice_fusion.1
  4.1 1.6 copy.48
  5.9 1.7 shard_map.163.mine_ref
  7.7 3.8 %collective-permute-start = (bf16[144,128]{1,0:T(8,128)(2,1)S(1)}, bf16[144,128]{1,0:T(8,128)(2,1)S(1)}, u32[]{:S(2)}, u32[]{:S(2)}) collective-permute-start(bf16[144,128]{1,0:T(8,128)(2,1)S(1)} %shard_map.163.mine_ref), channel_id=1, source_target_pairs={{0,1},{1,0},{2,3},{3,2},{4,5},{5,4},{6,7},{7,6},{8,9},{9,8},{10,11... | collective-permute-start | bytes 110600 | tf_op jit(solution)/shard_map/ppermute | solution.py:475
  12.8 0.8 shard_map.164
  13.6 1.7 collective-permute-start.1
  15.3 2.1 collective-permute-start.2
  17.4 1.2 collective-permute-start.3
  18.9 1.9 collective-permute-done.1.ns_ref
  20.7 1.1 collective-permute-done.3.west_ref
  21.8 10.1 %shard_map.165 = (f32[64,48,128]{2,1,0:T(8,128)S(1)}, bf16[144,128]{1,0:T(8,128)(2,1)S(1)}, f32[1,128]{1,0:T(1,128)S(1)}) custom-call(s32[7]{0:T(128)S(1)} %stack.39.sc, bf16[64,48,128]{2,1,0:T(8,128)(2,1)S(1)} %pad_bitcast_fusion.image_ref, bf16[144,128]{1,0:T(8,128)(2,1)S(1)} %collective-permute-done.their_ref.partner_ref, ...), custom_call_target="tpu_custom_call" | custom-call | tf_op jit(solution)/shard_map/pallas_call | solution.py:175
  31.9 5.2 %collective-permute-start.4 = (bf16[144,128]{1,0:T(8,128)(2,1)S(1)}, bf16[144,128]{1,0:T(8,128)(2,1)S(1)}, u32[]{:S(2)}, u32[]{:S(2)}) collective-permute-start(bf16[144,128]{1,0:T(8,128)(2,1)S(1)} %get-tuple-element.47.mine_ref), channel_id=1, source_target_pairs={{0,1},{1,0},{2,3},{3,2},{4,5},{5,4},{6,7},{7,6},{8,9},{9,8},{10,11... | collective-permute-start | bytes 110600 | tf_op jit(solution)/shard_map/ppermute | solution.py:475
  37.8 8.7 %all-to-all-start = ((f32[128,1,128]{2,1,0:T(1,128)}), f32[128,1,128]{2,1,0:T(1,128)S(1)}, u32[]{:S(2)}, u32[]{:S(2)}) async-start(f32[128,1,128]{2,1,0:T(1,128)} %broadcast_in_dim.53), calls=%async_computation | async-start | bytes 131072 | tf_op jit(solution)/shard_map/all_to_all | solution.py:483
  46.5 0.8 shard_map.166
  47.3 1.7 collective-permute-start.5
  49.7 1.1 collective-permute-start.7
  51.0 3.3 %collective-permute-done.5.ns_ref = bf16[48,128]{1,0:T(8,128)(2,1)S(1)} collective-permute-done((bf16[48,128]{1,0:T(8,128)(2,1)S(1)}, bf16[48,128]{1,0:T(8,128)(2,1)S(1)}, u32[]{:S(2)}, u32[]{:S(2)}) %collective-permute-start.5) | collective-permute-done | bytes 12320 | tf_op jit(solution)/shard_map/ppermute | solution.py:471
  55.0 1.4 all-to-all-done
  56.4 11.3 %shard_map.167 = (f32[64,48,128]{2,1,0:T(8,128)S(1)}, f32[1,128]{1,0:T(1,128)S(1)}, bf16[288,128]{1,0:T(8,128)(2,1)S(1)}) custom-call(s32[7]{0:T(128)S(1)} %stack.39.sc, f32[64,48,128]{2,1,0:T(8,128)S(1)} %get-tuple-element.45.raw_in, f32[128,128]{1,0:T(8,128)S(1)} %bitcast.56, bf16[144,128]{1,0:T(8,128)(2,1)S(1)} %collective-permute-done.4.their_ref.partner_ref, ...), custom_call_target="tpu_custom_call" | custom-call | tf_op jit(solution)/shard_map/pallas_call | solution.py:175
  67.7 1.1 copy-done.1
  68.9 2.4 %collective-permute-start.8 = (bf16[288,128]{1,0:T(8,128)(2,1)S(1)}, bf16[288,128]{1,0:T(8,128)(2,1)S(1)}, u32[]{:S(2)}, u32[]{:S(2)}) collective-permute-start(bf16[288,128]{1,0:T(8,128)(2,1)S(1)} %get-tuple-element.53.mine_ref), channel_id=1, source_target_pairs={{0,1},{1,0},{2,3},{3,2},{4,5},{5,4},{6,7},{7,6},{8,9},{9,8},{10,11... | collective-permute-start | bytes 221192 | tf_op jit(solution)/shard_map/ppermute | solution.py:475
  72.0 9.3 %all-to-all-start.1 = ((f32[128,1,128]{2,1,0:T(1,128)}), f32[128,1,128]{2,1,0:T(1,128)S(1)}, u32[]{:S(2)}, u32[]{:S(2)}) async-start(f32[128,1,128]{2,1,0:T(1,128)} %broadcast_in_dim.55), calls=%async_computation.1 | async-start | bytes 131072 | tf_op jit(solution)/shard_map/all_to_all | solution.py:483
  81.2 0.8 shard_map.168
  82.0 1.3 collective-permute-start.10
  83.9 1.6 collective-permute-start.9
  85.6 5.5 %all-to-all-done.1 = f32[128,1,128]{2,1,0:T(1,128)S(1)} async-done(((f32[128,1,128]{2,1,0:T(1,128)}), f32[128,1,128]{2,1,0:T(1,128)S(1)}, u32[]{:S(2)}, u32[]{:S(2)}) %all-to-all-start.1) | async-done | bytes 65568 | tf_op jit(solution)/shard_map/all_to_all | solution.py:483
  91.2 1.4 copy-done.2
  92.6 8.9 %shard_map.169 = (bf16[64,48,128]{2,1,0:T(8,128)(2,1)S(1)}, bf16[4,48,128]{2,1,0:T(8,128)(2,1)S(1)}, f32[32,96,128]{2,1,0:T(8,128)S(1)}, bf16[288,128]{1,0:T(8,128)(2,1)S(1)}, f32[1,128]{1,0:T(1,128)S(1)}) custom-call(s32[7]{0:T(128)S(1)} %stack.39.sc, f32[64,48,128]{2,1,0:T(8,128)S(1)} %copy-done.2, f32[128,128]{1,0:T(8,128)S(1)} %bitcast.54, ...), custom_call_target="tpu_custom_call" | custom-call | tf_op jit(solution)/shard_map/pallas_call | solution.py:175
  101.5 0.9 copy-done.3
  103.0 2.0 collective-permute-start.12
  105.7 10.6 %all-to-all-start.2 = ((f32[128,1,128]{2,1,0:T(1,128)}), f32[128,1,128]{2,1,0:T(1,128)S(1)}, u32[]{:S(2)}, u32[]{:S(2)}) async-start(f32[128,1,128]{2,1,0:T(1,128)} %broadcast_in_dim.57), calls=%async_computation.2 | async-start | bytes 131072 | tf_op jit(solution)/shard_map/all_to_all | solution.py:483
  116.3 0.8 shard_map.170
  117.0 1.5 collective-permute-start.13
  119.2 1.1 collective-permute-start.15
  121.3 4.7 %all-to-all-done.2 = f32[128,1,128]{2,1,0:T(1,128)S(1)} async-done(((f32[128,1,128]{2,1,0:T(1,128)}), f32[128,1,128]{2,1,0:T(1,128)S(1)}, u32[]{:S(2)}, u32[]{:S(2)}) %all-to-all-start.2) | async-done | bytes 65568 | tf_op jit(solution)/shard_map/all_to_all | solution.py:483
  127.2 0.7 copy-done.10
  128.0 0.7 copy-done.14
  130.0 7.7 %shard_map.171 = (f32[32,96,128]{2,1,0:T(8,128)S(1)}, f32[1,128]{1,0:T(1,128)S(1)}, bf16[288,128]{1,0:T(8,128)(2,1)}) custom-call(s32[7]{0:T(128)S(1)} %stack.39.sc, f32[32,96,128]{2,1,0:T(8,128)S(1)} %get-tuple-element.57.raw_in, f32[128,128]{1,0:T(8,128)S(1)} %bitcast.53, bf16[288,128]{1,0:T(8,128)(2,1)S(1)} %collective-permute-done.12.their_ref.partner_ref, ...), custom_call_target="tpu_custom_call" | custom-call | tf_op jit(solution)/shard_map/pallas_call | solution.py:175
  137.6 2.5 %collective-permute-start.16 = (bf16[288,128]{1,0:T(8,128)(2,1)}, bf16[288,128]{1,0:T(8,128)(2,1)S(1)}, u32[]{:S(2)}, u32[]{:S(2)}) collective-permute-start(bf16[288,128]{1,0:T(8,128)(2,1)} %get-tuple-element.65.mine_ref), channel_id=1, source_target_pairs={{0,1},{1,0},{2,3},{3,2},{4,5},{5,4},{6,7},{7,6},{8,9},{9,8},{10,11... | collective-permute-start | bytes 221192 | tf_op jit(solution)/shard_map/ppermute | solution.py:475
  140.8 8.6 %all-to-all-start.3 = ((f32[128,1,128]{2,1,0:T(1,128)}), f32[128,1,128]{2,1,0:T(1,128)S(1)}, u32[]{:S(2)}, u32[]{:S(2)}) async-start(f32[128,1,128]{2,1,0:T(1,128)} %broadcast_in_dim.59), calls=%async_computation.3 | async-start | bytes 131072 | tf_op jit(solution)/shard_map/all_to_all | solution.py:483
  149.4 1.1 shard_map.172
  150.6 1.7 collective-permute-start.17
  152.9 1.1 collective-permute-start.19
  154.1 1.1 copy.44
  155.4 4.0 %all-to-all-done.3 = f32[128,1,128]{2,1,0:T(1,128)S(1)} async-done(((f32[128,1,128]{2,1,0:T(1,128)}), f32[128,1,128]{2,1,0:T(1,128)S(1)}, u32[]{:S(2)}, u32[]{:S(2)}) %all-to-all-start.3) | async-done | bytes 65568 | tf_op jit(solution)/shard_map/all_to_all | solution.py:483
  160.6 1.1 copy-done.4
  161.8 0.8 copy-done.6
  162.6 0.7 copy-done.8
  165.4 19.5 %shard_map.173 = (f32[64,48,128]{2,1,0:T(8,128)S(1)}, bf16[144,128]{1,0:T(8,128)(2,1)S(1)}, f32[1,128]{1,0:T(1,128)S(1)}) custom-call(s32[7]{0:T(128)S(1)} %stack.39.sc, f32[32,96,128]{2,1,0:T(8,128)S(1)} %get-tuple-element.63.raw_in, f32[128,128]{1,0:T(8,128)S(1)} %bitcast.52, bf16[288,128]{1,0:T(8,128)(2,1)S(1)} %collective-permute-done.16.their_ref.partner_ref, ...), custom_call_target="tpu_custom_call" | custom-call | tf_op jit(solution)/shard_map/pallas_call | solution.py:175
  185.5 9.0 %all-to-all-start.4 = ((f32[128,1,128]{2,1,0:T(1,128)}), f32[128,1,128]{2,1,0:T(1,128)S(1)}, u32[]{:S(2)}, u32[]{:S(2)}) async-start(f32[128,1,128]{2,1,0:T(1,128)} %broadcast_in_dim.61), calls=%async_computation.4 | async-start | bytes 131072 | tf_op jit(solution)/shard_map/all_to_all | solution.py:483
  194.5 2.9 %collective-permute-start.20 = (bf16[144,128]{1,0:T(8,128)(2,1)S(1)}, bf16[144,128]{1,0:T(8,128)(2,1)S(1)}, u32[]{:S(2)}, u32[]{:S(2)}) collective-permute-start(bf16[144,128]{1,0:T(8,128)(2,1)S(1)} %get-tuple-element.73.mine_ref), channel_id=1, source_target_pairs={{0,1},{1,0},{2,3},{3,2},{4,5},{5,4},{6,7},{7,6},{8,9},{9,8},{10,11... | collective-permute-start | bytes 110600 | tf_op jit(solution)/shard_map/ppermute | solution.py:475
  197.5 1.8 collective-permute-done.20.their_ref.partner_ref
  199.3 0.8 shard_map.174
  200.1 1.6 collective-permute-start.21
  201.6 1.5 collective-permute-start.22
  203.1 1.3 collective-permute-start.23
  204.4 1.0 copy.45
  205.5 1.3 collective-permute-done.21.ns_ref
  206.8 0.8 collective-permute-done.23.west_ref
  207.6 8.7 %shard_map.175 = (f32[64,48,128]{2,1,0:T(8,128)S(1)}, f32[1,128]{1,0:T(1,128)S(1)}) custom-call(s32[7]{0:T(128)S(1)} %stack.39.sc, f32[64,48,128]{2,1,0:T(8,128)S(1)} %get-tuple-element.71.raw_in, f32[128,128]{1,0:T(8,128)S(1)} %bitcast.51, bf16[144,128]{1,0:T(8,128)(2,1)S(1)} %collective-permute-done.20.their_ref.partner_ref, ...), custom_call_target="tpu_custom_call" | custom-call | tf_op jit(solution)/shard_map/pallas_call | solution.py:175
  217.0 10.7 %all-to-all-start.5 = ((f32[128,1,128]{2,1,0:T(1,128)}), f32[128,1,128]{2,1,0:T(1,128)S(1)}, u32[]{:S(2)}, u32[]{:S(2)}) async-start(f32[128,1,128]{2,1,0:T(1,128)} %broadcast_in_dim.63), calls=%async_computation.5 | async-start | bytes 131072 | tf_op jit(solution)/shard_map/all_to_all | solution.py:483
  227.7 9.7 %all-to-all-done.5 = f32[128,1,128]{2,1,0:T(1,128)S(1)} async-done(((f32[128,1,128]{2,1,0:T(1,128)}), f32[128,1,128]{2,1,0:T(1,128)S(1)}, u32[]{:S(2)}, u32[]{:S(2)}) %all-to-all-start.5) | async-done | bytes 65568 | tf_op jit(solution)/shard_map/all_to_all | solution.py:483
  237.4 3.1 %shard_map.176 = bf16[64,45,128]{2,1,0:T(8,128)(2,1)S(1)} custom-call(s32[7]{0:T(128)S(1)} %stack.39.sc, f32[64,48,128]{2,1,0:T(8,128)S(1)} %get-tuple-element.77.raw_in, f32[128,128]{1,0:T(8,128)S(1)} %bitcast.55, bf16[48,48]{1,0:T(8,128)(2,1)S(1)} %pad.14.weight_ref, f32[1,48]{1,0:T(1,128)S(1)} %get-tuple-element.100.gain_ref, ...), custom_call_target="tpu_custom_call" | custom-call | tf_op jit(solution)/shard_map/pallas_call | solution.py:175
  240.5 1.1 copy.46
  (103 shorter events, 16.4 us)
Async XLA Ops:
  0.0 12.2 %copy-start = (f32[48,192]{1,0:T(8,128)S(1)}, f32[48,192]{1,0:T(8,128)}, u32[]{:S(2)}) copy-start(f32[48,192]{1,0:T(8,128)} %param.20) | copy-start | bytes 110596
  5.7 6.7 %copy-start.24 = (f32[192,48]{0,1:T(8,128)S(1)}, f32[192,48]{0,1:T(8,128)}, u32[]{:S(2)}) copy-start(f32[192,48]{0,1:T(8,128)} %param.21) | copy-start | bytes 110596
  5.7 6.8 %copy-start.23 = (f32[192,96]{1,0:T(8,128)S(1)}, f32[192,96]{1,0:T(8,128)}, u32[]{:S(2)}) copy-start(f32[192,96]{1,0:T(8,128)} %param.22) | copy-start | bytes 221188
  5.7 12.9 %copy-start.20 = (bf16[3,3,48,45]{3,2,1,0:T(8,128)(2,1)S(1)}, bf16[3,3,48,45]{3,2,1,0:T(8,128)(2,1)}, u32[]{:S(2)}) copy-start(bf16[3,3,48,45]{3,2,1,0:T(8,128)(2,1)} %param.23) | copy-start | bytes 116644
  5.9 44.9 %copy-start.26 = (f32[4,48]{1,0:T(4,128)S(1)}, f32[4,48]{1,0:T(4,128)}, u32[]{:S(2)}) copy-start(f32[4,48]{1,0:T(4,128)} %param.31) | copy-start | bytes 2308
  5.9 44.9 %copy-start.27 = (f32[4,48]{1,0:T(4,128)S(1)}, f32[4,48]{1,0:T(4,128)}, u32[]{:S(2)}) copy-start(f32[4,48]{1,0:T(4,128)} %param.30) | copy-start | bytes 2308
  5.9 44.9 %copy-start.22 = (bf16[3,3,48,48]{3,2,1,0:T(8,128)(2,1)S(1)}, bf16[3,3,48,48]{3,2,1,0:T(8,128)(2,1)}, u32[]{:S(2)}) copy-start(bf16[3,3,48,48]{3,2,1,0:T(8,128)(2,1)} %param.24) | copy-start | bytes 124420
  7.7 5.1 %collective-permute-start = (bf16[144,128]{1,0:T(8,128)(2,1)S(1)}, bf16[144,128]{1,0:T(8,128)(2,1)S(1)}, u32[]{:S(2)}, u32[]{:S(2)}) collective-permute-start(bf16[144,128]{1,0:T(8,128)(2,1)S(1)} %shard_map.163.mine_ref), channel_id=1, source_target_pairs={{0,1},{1,0},{2,3},{3,2},{4,5},{5,4},{6,7},{7,6},{8,9},{9,8},{10,11... | collective-permute-start | bytes 110600 | tf_op jit(solution)/shard_map/ppermute | solution.py:475
  13.6 7.1 %collective-permute-start.1 = (bf16[48,128]{1,0:T(8,128)(2,1)S(1)}, bf16[48,128]{1,0:T(8,128)(2,1)S(1)}, u32[]{:S(2)}, u32[]{:S(2)}) collective-permute-start(bf16[48,128]{1,0:T(8,128)(2,1)S(1)} %get-tuple-element.42), channel_id=1, source_target_pairs={{0,8},{1,121},{2,10},{3,123},{4,12},{5,125},{6,14},{7,127},{8,16},... | collective-permute-start | bytes 36872 | tf_op jit(solution)/shard_map/ppermute | solution.py:471
  15.3 5.4 %collective-permute-start.2 = (bf16[48,128]{1,0:T(8,128)(2,1)S(1)}, bf16[48,128]{1,0:T(8,128)(2,1)S(1)}, u32[]{:S(2)}, u32[]{:S(2)}) collective-permute-start(bf16[48,128]{1,0:T(8,128)(2,1)S(1)} %get-tuple-element.43), channel_id=1, source_target_pairs={{0,126},{2,0},{4,2},{6,4},{8,6},{10,8},{12,10},{14,12},{16,14},{18... | collective-permute-start | bytes 36872 | tf_op jit(solution)/shard_map/ppermute | solution.py:462
  17.4 4.4 %collective-permute-start.3 = (bf16[48,128]{1,0:T(8,128)(2,1)S(1)}, bf16[48,128]{1,0:T(8,128)(2,1)S(1)}, u32[]{:S(2)}, u32[]{:S(2)}) collective-permute-start(bf16[48,128]{1,0:T(8,128)(2,1)S(1)} %get-tuple-element.44), channel_id=1, source_target_pairs={{0,2},{2,4},{4,6},{6,8},{8,10},{10,12},{12,14},{14,16},{16,18},{18... | collective-permute-start | bytes 36872 | tf_op jit(solution)/shard_map/ppermute | solution.py:462
  31.9 53.6 %copy-start.21 = (bf16[3,3,96,48]{2,3,1,0:T(8,128)(2,1)S(1)}, bf16[3,3,96,48]{2,3,1,0:T(8,128)(2,1)}, u32[]{:S(2)}) copy-start(bf16[3,3,96,48]{2,3,1,0:T(8,128)(2,1)} %param.25) | copy-start | bytes 248836
  31.9 14.6 %collective-permute-start.4 = (bf16[144,128]{1,0:T(8,128)(2,1)S(1)}, bf16[144,128]{1,0:T(8,128)(2,1)S(1)}, u32[]{:S(2)}, u32[]{:S(2)}) collective-permute-start(bf16[144,128]{1,0:T(8,128)(2,1)S(1)} %get-tuple-element.47.mine_ref), channel_id=1, source_target_pairs={{0,1},{1,0},{2,3},{3,2},{4,5},{5,4},{6,7},{7,6},{8,9},{9,8},{10,11... | collective-permute-start | bytes 110600 | tf_op jit(solution)/shard_map/ppermute | solution.py:475
  37.8 18.7 %all-to-all-start = ((f32[128,1,128]{2,1,0:T(1,128)}), f32[128,1,128]{2,1,0:T(1,128)S(1)}, u32[]{:S(2)}, u32[]{:S(2)}) async-start(f32[128,1,128]{2,1,0:T(1,128)} %broadcast_in_dim.53), calls=%async_computation | async-start | bytes 131072 | tf_op jit(solution)/shard_map/all_to_all | solution.py:483
  47.3 7.0 %collective-permute-start.5 = (bf16[48,128]{1,0:T(8,128)(2,1)S(1)}, bf16[48,128]{1,0:T(8,128)(2,1)S(1)}, u32[]{:S(2)}, u32[]{:S(2)}) collective-permute-start(bf16[48,128]{1,0:T(8,128)(2,1)S(1)} %get-tuple-element.48), channel_id=1, source_target_pairs={{0,8},{1,121},{2,10},{3,123},{4,12},{5,125},{6,14},{7,127},{8,16},... | collective-permute-start | bytes 36872 | tf_op jit(solution)/shard_map/ppermute | solution.py:471
  49.0 5.3 %collective-permute-start.6 = (bf16[48,128]{1,0:T(8,128)(2,1)S(1)}, bf16[48,128]{1,0:T(8,128)(2,1)S(1)}, u32[]{:S(2)}, u32[]{:S(2)}) collective-permute-start(bf16[48,128]{1,0:T(8,128)(2,1)S(1)} %get-tuple-element.49), channel_id=1, source_target_pairs={{0,126},{2,0},{4,2},{6,4},{8,6},{10,8},{12,10},{14,12},{16,14},{18... | collective-permute-start | bytes 36872 | tf_op jit(solution)/shard_map/ppermute | solution.py:462
  49.7 5.4 %collective-permute-start.7 = (bf16[48,128]{1,0:T(8,128)(2,1)S(1)}, bf16[48,128]{1,0:T(8,128)(2,1)S(1)}, u32[]{:S(2)}, u32[]{:S(2)}) collective-permute-start(bf16[48,128]{1,0:T(8,128)(2,1)S(1)} %get-tuple-element.50), channel_id=1, source_target_pairs={{0,2},{2,4},{4,6},{6,8},{8,10},{10,12},{12,14},{14,16},{16,18},{18... | collective-permute-start | bytes 36872 | tf_op jit(solution)/shard_map/ppermute | solution.py:462
  67.7 1.2 copy-start.1
  68.9 51.5 %copy-start.28 = (f32[2,96]{1,0:T(2,128)S(1)}, f32[2,96]{1,0:T(2,128)}, u32[]{:S(2)}) copy-start(f32[2,96]{1,0:T(2,128)} %param.33) | copy-start | bytes 2308
  68.9 51.5 %copy-start.29 = (f32[2,96]{1,0:T(2,128)S(1)}, f32[2,96]{1,0:T(2,128)}, u32[]{:S(2)}) copy-start(f32[2,96]{1,0:T(2,128)} %param.32) | copy-start | bytes 2308
  68.9 52.1 %copy-start.19 = (bf16[3,3,96,96]{3,2,1,0:T(8,128)(2,1)S(1)}, bf16[3,3,96,96]{3,2,1,0:T(8,128)(2,1)}, u32[]{:S(2)}) copy-start(bf16[3,3,96,96]{3,2,1,0:T(8,128)(2,1)} %param.26) | copy-start | bytes 497668
  68.9 12.3 %collective-permute-start.8 = (bf16[288,128]{1,0:T(8,128)(2,1)S(1)}, bf16[288,128]{1,0:T(8,128)(2,1)S(1)}, u32[]{:S(2)}, u32[]{:S(2)}) collective-permute-start(bf16[288,128]{1,0:T(8,128)(2,1)S(1)} %get-tuple-element.53.mine_ref), channel_id=1, source_target_pairs={{0,1},{1,0},{2,3},{3,2},{4,5},{5,4},{6,7},{7,6},{8,9},{9,8},{10,11... | collective-permute-start | bytes 221192 | tf_op jit(solution)/shard_map/ppermute | solution.py:475
  72.0 19.2 %all-to-all-start.1 = ((f32[128,1,128]{2,1,0:T(1,128)}), f32[128,1,128]{2,1,0:T(1,128)S(1)}, u32[]{:S(2)}, u32[]{:S(2)}) async-start(f32[128,1,128]{2,1,0:T(1,128)} %broadcast_in_dim.55), calls=%async_computation.1 | async-start | bytes 131072 | tf_op jit(solution)/shard_map/all_to_all | solution.py:483
  82.0 9.1 %collective-permute-start.10 = (bf16[96,128]{1,0:T(8,128)(2,1)S(1)}, bf16[96,128]{1,0:T(8,128)(2,1)S(1)}, u32[]{:S(2)}, u32[]{:S(2)}) collective-permute-start(bf16[96,128]{1,0:T(8,128)(2,1)S(1)} %get-tuple-element.55), channel_id=1, source_target_pairs={{0,126},{2,0},{4,2},{6,4},{8,6},{10,8},{12,10},{14,12},{16,14},{18... | collective-permute-start | bytes 73736 | tf_op jit(solution)/shard_map/ppermute | solution.py:462
  83.3 7.8 %collective-permute-start.11 = (bf16[96,128]{1,0:T(8,128)(2,1)S(1)}, bf16[96,128]{1,0:T(8,128)(2,1)S(1)}, u32[]{:S(2)}, u32[]{:S(2)}) collective-permute-start(bf16[96,128]{1,0:T(8,128)(2,1)S(1)} %get-tuple-element.56), channel_id=1, source_target_pairs={{0,2},{2,4},{4,6},{6,8},{8,10},{10,12},{12,14},{14,16},{16,18},{18... | collective-permute-start | bytes 73736 | tf_op jit(solution)/shard_map/ppermute | solution.py:462
  83.9 7.3 %collective-permute-start.9 = (bf16[96,128]{1,0:T(8,128)(2,1)S(1)}, bf16[96,128]{1,0:T(8,128)(2,1)S(1)}, u32[]{:S(2)}, u32[]{:S(2)}) collective-permute-start(bf16[96,128]{1,0:T(8,128)(2,1)S(1)} %get-tuple-element.54), channel_id=1, source_target_pairs={{0,8},{1,121},{2,10},{3,123},{4,12},{5,125},{6,14},{7,127},{8,16},... | collective-permute-start | bytes 73736 | tf_op jit(solution)/shard_map/ppermute | solution.py:471
  91.1 1.4 copy-start.2
  101.5 0.9 copy-start.3
  102.4 0.6 copy-start.5
  103.0 13.2 %collective-permute-start.12 = (bf16[288,128]{1,0:T(8,128)(2,1)S(1)}, bf16[288,128]{1,0:T(8,128)(2,1)S(1)}, u32[]{:S(2)}, u32[]{:S(2)}) collective-permute-start(bf16[288,128]{1,0:T(8,128)(2,1)S(1)} %get-tuple-element.59.mine_ref), channel_id=1, source_target_pairs={{0,1},{1,0},{2,3},{3,2},{4,5},{5,4},{6,7},{7,6},{8,9},{9,8},{10,11... | collective-permute-start | bytes 221192 | tf_op jit(solution)/shard_map/ppermute | solution.py:475
  105.7 20.4 %all-to-all-start.2 = ((f32[128,1,128]{2,1,0:T(1,128)}), f32[128,1,128]{2,1,0:T(1,128)S(1)}, u32[]{:S(2)}, u32[]{:S(2)}) async-start(f32[128,1,128]{2,1,0:T(1,128)} %broadcast_in_dim.57), calls=%async_computation.2 | async-start | bytes 131072 | tf_op jit(solution)/shard_map/all_to_all | solution.py:483
  117.0 9.0 %collective-permute-start.13 = (bf16[96,128]{1,0:T(8,128)(2,1)S(1)}, bf16[96,128]{1,0:T(8,128)(2,1)S(1)}, u32[]{:S(2)}, u32[]{:S(2)}) collective-permute-start(bf16[96,128]{1,0:T(8,128)(2,1)S(1)} %get-tuple-element.60), channel_id=1, source_target_pairs={{0,8},{1,121},{2,10},{3,123},{4,12},{5,125},{6,14},{7,127},{8,16},... | collective-permute-start | bytes 73736 | tf_op jit(solution)/shard_map/ppermute | solution.py:471
  118.6 7.4 %collective-permute-start.14 = (bf16[96,128]{1,0:T(8,128)(2,1)S(1)}, bf16[96,128]{1,0:T(8,128)(2,1)S(1)}, u32[]{:S(2)}, u32[]{:S(2)}) collective-permute-start(bf16[96,128]{1,0:T(8,128)(2,1)S(1)} %get-tuple-element.61), channel_id=1, source_target_pairs={{0,126},{2,0},{4,2},{6,4},{8,6},{10,8},{12,10},{14,12},{16,14},{18... | collective-permute-start | bytes 73736 | tf_op jit(solution)/shard_map/ppermute | solution.py:462
  119.2 7.4 %collective-permute-start.15 = (bf16[96,128]{1,0:T(8,128)(2,1)S(1)}, bf16[96,128]{1,0:T(8,128)(2,1)S(1)}, u32[]{:S(2)}, u32[]{:S(2)}) collective-permute-start(bf16[96,128]{1,0:T(8,128)(2,1)S(1)} %get-tuple-element.62), channel_id=1, source_target_pairs={{0,2},{2,4},{4,6},{6,8},{8,10},{10,12},{12,14},{14,16},{16,18},{18... | collective-permute-start | bytes 73736 | tf_op jit(solution)/shard_map/ppermute | solution.py:462
  126.0 0.6 copy-start.9
  126.6 0.6 copy-start.13
  127.2 0.7 copy-start.10
  128.0 0.7 copy-start.14
  128.7 0.7 copy-start.15
  129.4 0.6 copy-start.16
  137.6 11.8 %collective-permute-start.16 = (bf16[288,128]{1,0:T(8,128)(2,1)}, bf16[288,128]{1,0:T(8,128)(2,1)S(1)}, u32[]{:S(2)}, u32[]{:S(2)}) collective-permute-start(bf16[288,128]{1,0:T(8,128)(2,1)} %get-tuple-element.65.mine_ref), channel_id=1, source_target_pairs={{0,1},{1,0},{2,3},{3,2},{4,5},{5,4},{6,7},{7,6},{8,9},{9,8},{10,11... | collective-permute-start | bytes 221192 | tf_op jit(solution)/shard_map/ppermute | solution.py:475
  140.8 18.6 %all-to-all-start.3 = ((f32[128,1,128]{2,1,0:T(1,128)}), f32[128,1,128]{2,1,0:T(1,128)S(1)}, u32[]{:S(2)}, u32[]{:S(2)}) async-start(f32[128,1,128]{2,1,0:T(1,128)} %broadcast_in_dim.59), calls=%async_computation.3 | async-start | bytes 131072 | tf_op jit(solution)/shard_map/all_to_all | solution.py:483
  150.6 8.8 %collective-permute-start.17 = (bf16[96,128]{1,0:T(8,128)(2,1)S(1)}, bf16[96,128]{1,0:T(8,128)(2,1)S(1)}, u32[]{:S(2)}, u32[]{:S(2)}) collective-permute-start(bf16[96,128]{1,0:T(8,128)(2,1)S(1)} %get-tuple-element.66), channel_id=1, source_target_pairs={{0,8},{1,121},{2,10},{3,123},{4,12},{5,125},{6,14},{7,127},{8,16},... | collective-permute-start | bytes 73736 | tf_op jit(solution)/shard_map/ppermute | solution.py:471
  152.3 7.1 %collective-permute-start.18 = (bf16[96,128]{1,0:T(8,128)(2,1)S(1)}, bf16[96,128]{1,0:T(8,128)(2,1)S(1)}, u32[]{:S(2)}, u32[]{:S(2)}) collective-permute-start(bf16[96,128]{1,0:T(8,128)(2,1)S(1)} %get-tuple-element.67), channel_id=1, source_target_pairs={{0,126},{2,0},{4,2},{6,4},{8,6},{10,8},{12,10},{14,12},{16,14},{18... | collective-permute-start | bytes 73736 | tf_op jit(solution)/shard_map/ppermute | solution.py:462
  152.9 7.1 %collective-permute-start.19 = (bf16[96,128]{1,0:T(8,128)(2,1)S(1)}, bf16[96,128]{1,0:T(8,128)(2,1)S(1)}, u32[]{:S(2)}, u32[]{:S(2)}) collective-permute-start(bf16[96,128]{1,0:T(8,128)(2,1)S(1)} %get-tuple-element.68), channel_id=1, source_target_pairs={{0,2},{2,4},{4,6},{6,8},{8,10},{10,12},{12,14},{14,16},{16,18},{18... | collective-permute-start | bytes 73736 | tf_op jit(solution)/shard_map/ppermute | solution.py:462
  159.4 0.6 copy-start.7
  160.0 0.6 copy-start.11
  160.6 1.1 copy-start.4
  161.8 0.8 copy-start.6
  162.6 0.7 copy-start.8
  163.3 0.7 copy-start.12
  164.0 0.7 copy-start.17
  164.7 0.7 copy-start.18
  184.9 42.8 %copy-start.25 = (bf16[45,48]{1,0:T(8,128)(2,1)S(1)}, bf16[45,48]{1,0:T(8,128)(2,1)}, u32[]{:S(2)}) copy-start(bf16[45,48]{1,0:T(8,128)(2,1)} %param.29) | copy-start | bytes 12964
  185.5 22.1 %all-to-all-start.4 = ((f32[128,1,128]{2,1,0:T(1,128)}), f32[128,1,128]{2,1,0:T(1,128)S(1)}, u32[]{:S(2)}, u32[]{:S(2)}) async-start(f32[128,1,128]{2,1,0:T(1,128)} %broadcast_in_dim.61), calls=%async_computation.4 | async-start | bytes 131072 | tf_op jit(solution)/shard_map/all_to_all | solution.py:483
  194.5 4.8 %collective-permute-start.20 = (bf16[144,128]{1,0:T(8,128)(2,1)S(1)}, bf16[144,128]{1,0:T(8,128)(2,1)S(1)}, u32[]{:S(2)}, u32[]{:S(2)}) collective-permute-start(bf16[144,128]{1,0:T(8,128)(2,1)S(1)} %get-tuple-element.73.mine_ref), channel_id=1, source_target_pairs={{0,1},{1,0},{2,3},{3,2},{4,5},{5,4},{6,7},{7,6},{8,9},{9,8},{10,11... | collective-permute-start | bytes 110600 | tf_op jit(solution)/shard_map/ppermute | solution.py:475
  200.1 6.7 %collective-permute-start.21 = (bf16[48,128]{1,0:T(8,128)(2,1)S(1)}, bf16[48,128]{1,0:T(8,128)(2,1)S(1)}, u32[]{:S(2)}, u32[]{:S(2)}) collective-permute-start(bf16[48,128]{1,0:T(8,128)(2,1)S(1)} %get-tuple-element.74), channel_id=1, source_target_pairs={{0,8},{1,121},{2,10},{3,123},{4,12},{5,125},{6,14},{7,127},{8,16},... | collective-permute-start | bytes 36872 | tf_op jit(solution)/shard_map/ppermute | solution.py:471
  201.6 5.2 %collective-permute-start.22 = (bf16[48,128]{1,0:T(8,128)(2,1)S(1)}, bf16[48,128]{1,0:T(8,128)(2,1)S(1)}, u32[]{:S(2)}, u32[]{:S(2)}) collective-permute-start(bf16[48,128]{1,0:T(8,128)(2,1)S(1)} %get-tuple-element.75), channel_id=1, source_target_pairs={{0,126},{2,0},{4,2},{6,4},{8,6},{10,8},{12,10},{14,12},{16,14},{18... | collective-permute-start | bytes 36872 | tf_op jit(solution)/shard_map/ppermute | solution.py:462
  203.1 4.5 %collective-permute-start.23 = (bf16[48,128]{1,0:T(8,128)(2,1)S(1)}, bf16[48,128]{1,0:T(8,128)(2,1)S(1)}, u32[]{:S(2)}, u32[]{:S(2)}) collective-permute-start(bf16[48,128]{1,0:T(8,128)(2,1)S(1)} %get-tuple-element.76), channel_id=1, source_target_pairs={{0,2},{2,4},{4,6},{6,8},{8,10},{10,12},{12,14},{14,16},{16,18},{18... | collective-permute-start | bytes 36872 | tf_op jit(solution)/shard_map/ppermute | solution.py:462
  217.0 20.4 %all-to-all-start.5 = ((f32[128,1,128]{2,1,0:T(1,128)}), f32[128,1,128]{2,1,0:T(1,128)S(1)}, u32[]{:S(2)}, u32[]{:S(2)}) async-start(f32[128,1,128]{2,1,0:T(1,128)} %broadcast_in_dim.63), calls=%async_computation.5 | async-start | bytes 131072 | tf_op jit(solution)/shard_map/all_to_all | solution.py:483
where the time goes:
time: 243 us; the launch traced here: 242 us
  starting transfers between devices  98.8 us (41%)
  Pallas kernels  75.9 us (31%)
  waiting for transfers between devices  36.3 us (15%)
  local copies, waits for them, and re-layouts  26.3 us (11%)
  between operations  3.67 us (2%)
    pallas_call x14, Pallas kernels, call(): pl.pallas_call(body, in_specs=[SCALARS] + [WHOLE] * (len(operands) - 1),...  75.9 us
    all_to_all x6, starting transfers between devices, share(): return lax.all_to_all(copies, TILE_SPLIT, 0, 0).reshape(devices, LANES)  56.8 us
    all_to_all x6, waiting for transfers between devices, share(): return lax.all_to_all(copies, TILE_SPLIT, 0, 0).reshape(devices, LANES)  25.4 us
    ppermute x6, starting transfers between devices, exchange(): partner = lax.ppermute(pack, 'split', [(0, 1), (1, 0)])  18.9 us
    unnamed x62, local copies, waits for them, and re-layouts  15.7 us
    ppermute x12, starting transfers between devices, shift_tiles(): lax.ppermute(value, TILE, [(t, (t + steps) % count) for t in range(count)])  13.3 us
    ppermute x6, starting transfers between devices, vertical(): return lax.ppermute(value, TILE_SPLIT, pairs)  9.81 us
    ppermute x6, waiting for transfers between devices, vertical(): return lax.ppermute(value, TILE_SPLIT, pairs)  6.49 us
  transfers between devices with their start and end apart: 30, of which 12 were waited for; matrix products, arithmetic and copies ran while one was open for 3% of the time, Pallas kernels for 2%

commit v1 on v0

--- a/solution.py
+++ b/solution.py
@@ -8,12 +8,14 @@
 from jax.sharding import Mesh
 from jax.sharding import PartitionSpec as P
 
+
 GROUPS = 8
 ROW_TILES = 4
 TILE = ("tile_0", "tile_1", "tile_2", "tile_3")
 TILE_SPLIT = ("tile_0", "tile_1", "tile_2", "tile_3", "split")
 EPSILON = 1e-05
 LANES = 128
+DEVICES = 128
 F32 = jnp.float32
 BF16 = jnp.bfloat16
 
@@ -31,13 +33,13 @@
     return (row * 43) >> (8 if channels == 48 else 9)
 
 
-def column_of(row_value, channels):
+def column_of(row_value, channels, first=0):
     shape = (channels, row_value.shape[1])
-    on_diagonal = lax.broadcasted_iota(jnp.int32, shape, 0) == lane_index(shape)
+    on_diagonal = lax.broadcasted_iota(jnp.int32, shape, 0) + first == lane_index(shape)
     return jnp.sum(jnp.where(on_diagonal, jnp.broadcast_to(row_value, shape), 0.0), axis=1, keepdims=True)
 
 
-def coefficients(stats, gain_row, shift_row, bias_row, channels, pixels):
+def coefficients(stats, gain_row, shift_row, bias, channels, pixels):
     devices = stats.shape[0]
     count = pixels * (channels // GROUPS)
     mean_row = jnp.sum(stats, axis=0, keepdims=True) * (1.0 / devices)
@@ -53,8 +55,8 @@
     spread = pick(mean_row, GROUPS) * (1.0 / count) + pick(apart, 0)
     slope = lax.rsqrt(spread + EPSILON) * column_of(gain_row, channels)
     offset = column_of(shift_row, channels) - mean * slope
-    if bias_row is not None:
-        offset = offset + column_of(bias_row, channels) * slope
+    if bias is not None:
+        offset = offset + column_of(bias[0][...], channels, bias[1]) * slope
     return jnp.broadcast_to(slope * 0.5, shape), jnp.broadcast_to(offset * 0.5, shape)
 
 
@@ -63,7 +65,7 @@
     return (half + half * jnp.tanh(half)).astype(BF16)
 
 
-def group_stats(sums, squares, bias_row, channels, pixels, width):
+def group_stats(sums, squares, bias, channels, pixels, width):
     shape = (channels, LANES)
     lane = lane_index(shape)
     group = group_index(channels, shape)
@@ -71,8 +73,8 @@
     mean = jnp.sum(jnp.where(inside, sums, 0.0), axis=1, keepdims=True) * (1.0 / pixels)
     second = jnp.sum(jnp.where(inside, squares, 0.0), axis=1, keepdims=True)
     spread = jnp.maximum(second - pixels * jnp.square(mean), 0.0)
-    if bias_row is not None:
-        mean = mean + column_of(bias_row, channels)
+    if bias is not None:
+        mean = mean + column_of(bias[0][...], channels, bias[1])
     group_size = channels // GROUPS
     mean_row = jnp.sum(jnp.where(lane == group, mean, 0.0), axis=0, keepdims=True) * (1.0 / group_size)
     group_mean = jnp.sum(jnp.where(lane == group, mean_row, 0.0), axis=1, keepdims=True)
@@ -84,27 +86,27 @@
     stride = taps.shape[1] // 3
     lane = lane_index((channels, LANES))
     base = place * block_rows
-    hold_west = turn(west, (LANES + 1 - base) % LANES)
-    hold_east = turn(east, (LANES + width - base) % LANES)
 
     def put(row, value, hw, he):
         taps[row, pl.ds(first, channels)] = jnp.where(lane == 0, hw, turn(value, 1))
         taps[row, pl.ds(stride + first, channels)] = value
         taps[row, pl.ds(2 * stride + first, channels)] = jnp.where(lane == width - 1, he, turn(value, LANES - 1))
 
+    def sides(row):
+        return turn(west, (LANES - base - row) % LANES), turn(east, (2 * LANES + width - 1 - base - row) % LANES)
+
     zero = jnp.zeros((channels, LANES), BF16)
-    put(0, upper, jnp.where(place == 0, zero, hold_west), jnp.where(place == 0, zero, hold_east))
+    hw, he = sides(-1)
+    put(0, upper, jnp.where(place == 0, zero, hw), jnp.where(place == 0, zero, he))
 
     def body(step, carry):
-        hw, he = carry
         for k in range(together):
             row = step * together + k
-            hw, he = turn(hw, LANES - 1), turn(he, LANES - 1)
-            put(row + 1, rows_of(row), hw, he)
-        return hw, he
-
-    hw, he = lax.fori_loop(0, block_rows // together, body, (hold_west, hold_east))
-    hw, he = turn(hw, LANES - 1), turn(he, LANES - 1)
+            put(row + 1, rows_of(row), *sides(row))
+        return carry
+
+    lax.fori_loop(0, block_rows // together, body, 0)
+    hw, he = sides(block_rows)
     put(block_rows + 1, lower, jnp.where(place == 1, zero, hw), jnp.where(place == 1, zero, he))
 
 
@@ -124,7 +126,7 @@
             both = jnp.dot(weight, window, preferred_element_type=F32)
             for j in range(2):
                 value = both[:, j * LANES : (j + 1) * LANES]
-                raw_ref[row + k + j] = value
+                raw_ref[row + k + j] = value.astype(BF16)
                 sums = sums + value
                 squares = squares + value * value
         return sums, squares
@@ -141,28 +143,35 @@
         pack_ref[pl.ds(d * channels, channels)] = raw_ref[outer].astype(BF16)
         pack_ref[pl.ds(size + d * channels, channels)] = raw_ref[last - outer].astype(BF16)
 
+    spacing = 2 if width == LANES else 1
+
     def body(step, carry):
         carry = list(carry)
         for k in range(together):
             row = step * together + k
-            value = raw_ref[row].astype(F32)
+            value = raw_ref[row].astype(BF16)
             for d in range(depth):
-                line = jnp.where(lane == row, jnp.broadcast_to(value[:, d : d + 1], lane.shape), carry[d])
-                right = width - 1 - d
-                carry[d] = jnp.where(
-                    lane == block_rows + row, jnp.broadcast_to(value[:, right : right + 1], lane.shape), line
-                )
+                amount = spacing * row
+                west = (lane == amount)
+                east = lane == (amount + width - 1) % LANES
+                if d:
+                    left = turn(value, (amount + LANES - d) % LANES)
+                    right = turn(value, (amount + d) % LANES)
+                    carry[d] = jnp.where(west, left, jnp.where(east, right, carry[d]))
+                else:
+                    carry[d] = jnp.where(west | east, turn(value, amount), carry[d])
         return tuple(carry)
 
-    zero = jnp.zeros((channels, LANES), F32)
+    zero = jnp.zeros((channels, LANES), BF16)
     columns = lax.fori_loop(0, block_rows // together, body, (zero,) * depth)
     for d in range(depth):
-        pack_ref[pl.ds(2 * size + d * channels, channels)] = columns[d].astype(BF16)
-
-
-def finish(taps, weight_ref, raw_ref, pack_ref, stat_ref, bias_row, block_rows, channels, width, depth, place):
+        pack_ref[pl.ds(2 * size + d * channels, channels)] = columns[d]
+
+
+def finish(taps, weight_ref, raw_ref, pack_ref, stat_ref, bias, block_rows, channels, width, depth, place):
     sums, squares = convolve_rows(taps, weight_ref, raw_ref, block_rows)
-    stat_ref[...] = group_stats(sums, squares, bias_row, channels, float(block_rows * width), width)
+    stat = group_stats(sums, squares, bias, channels, float(block_rows * width), width)
+    stat_ref[...] = jnp.broadcast_to(stat, stat_ref.shape)
     if pack_ref is not None:
         pack_edges(raw_ref, pack_ref, block_rows, channels, width, depth, place)
 
@@ -171,14 +180,14 @@
 SCALARS = pl.BlockSpec(memory_space=pltpu.SMEM)
 
 
-def call(body, operands, outs, scratch=()):
+def call(body, operands, outs, scratch=(), limit=12):
     return pl.pallas_call(
         body,
         in_specs=[SCALARS] + [WHOLE] * (len(operands) - 1),
         out_specs=[WHOLE] * len(outs),
         out_shape=[jax.ShapeDtypeStruct(s, d) for s, d in outs],
         scratch_shapes=list(scratch),
-        compiler_params=pltpu.CompilerParams(vmem_limit_bytes=48 * 1024 * 1024),
+        compiler_params=pltpu.CompilerParams(vmem_limit_bytes=limit * 1024 * 1024),
     )(*operands)
 
 
@@ -206,11 +215,17 @@
         low, high = ordered(0)
         side_ref[0] = low
         side_ref[2] = high
-        low, high = ordered(2 * size)
-        side_ref[3] = jnp.where(lane < half, low, turn(high, half))
-        side_ref[1] = jnp.where(lane < half, turn(low, LANES - half), high)
         shape = (LANES, LANES)
         row, column = lax.broadcasted_iota(jnp.int32, shape, 0), lane_index(shape)
+        low, high = ordered(2 * size)
+        both = jnp.concatenate([low, high], axis=1)
+        spacing = 2 if width == LANES else 1
+        for side, start in ((3, 0), (1, width - 1)):
+            upper = (row == (start + spacing * column) % LANES) & (column < half)
+            under = (row == (start + spacing * (column - half)) % LANES) & (column >= half) & (column < width)
+            spread = jnp.concatenate([upper, under], axis=0)
+            spread = jnp.where(spread, 1.0, 0.0).astype(BF16)
+            side_ref[side] = jnp.dot(both, spread, preferred_element_type=F32).astype(BF16)
         for k, out in enumerate((ns_ref, east_ref, west_ref)):
             reverse = sc[2 + 2 * k]
             hit = jnp.where(reverse == 1, width - 1 - row, row) == column
@@ -236,17 +251,17 @@
         frame_rows(
             taps, 0, channels, width, block_rows, lambda r: image_ref[r], upper, lower, west_ref[...], east_ref[...], place
         )
-        finish(taps, weight_ref, raw_ref, pack_ref, stat_ref, bias_ref[...], block_rows, outputs, width, 1, place)
+        finish(taps, weight_ref, raw_ref, pack_ref, stat_ref, (bias_ref, 0), block_rows, outputs, width, 1, place)
 
     return call(
         body,
         (scalars, image, partner, ns, east, west, weight, bias),
-        [((block_rows, outputs, LANES), F32), ((3 * outputs, LANES), BF16), ((1, LANES), F32)],
+        [((block_rows, outputs, LANES), BF16), ((3 * outputs, LANES), BF16), ((DEVICES, LANES), F32)],
         [pltpu.VMEM((block_rows + 2, 3 * channels, LANES), BF16)],
     )
 
 
-def plain_stage(scalars, raw, stats, partner, ns, east, west, weight, gain, shift, bias, width, depth):
+def plain_stage(scalars, raw, stats, partner, ns, east, west, weight, gain, shift, line, bias, first, width, depth):
     block_rows, channels, _ = raw.shape
     outputs = weight.shape[0]
     biased = bias is not None
@@ -254,7 +269,7 @@
     def body(sc, raw_in, stats_ref, partner_ref, ns_ref, east_ref, west_ref, weight_ref, gain_ref, shift_ref, *rest):
         bias_row = None
         if biased:
-            bias_row, rest = rest[0][...], rest[1:]
+            bias_row, rest = (rest[0], first), rest[1:]
         if depth:
             raw_ref, stat_ref, pack_ref, taps = rest
         else:
@@ -262,7 +277,7 @@
             pack_ref = None
         place = sc[0]
         coef = coefficients(
-            stats_ref[...], gain_ref[...], shift_ref[...], bias_row, channels, float(block_rows * width)
+            stats_ref[...], gain_ref[line : line + 1], shift_ref[line : line + 1], bias_row, channels, float(block_rows * width)
         )
         lane = lane_index((channels, LANES))
         clear = jnp.zeros((channels, LANES), BF16)
@@ -286,7 +301,7 @@
         )
         finish(taps, weight_ref, raw_ref, pack_ref, stat_ref, None, block_rows, outputs, width, depth, place)
 
-    outs = [((block_rows, outputs, LANES), F32), ((1, LANES), F32)]
+    outs = [((block_rows, outputs, LANES), BF16), ((DEVICES, LANES), F32)]
     if depth:
         outs.append(((3 * depth * outputs, LANES), BF16))
     operands = (scalars, raw, stats, partner, ns, east, west, weight, gain, shift)
@@ -305,7 +320,7 @@
         skip_ref, side_ref, raw_ref, pack_ref, stat_ref, taps, pooled,
     ):
         place = sc[0]
-        coef = coefficients(stats_ref[...], gain_ref[...], shift_ref[...], None, channels, float(block_rows * width))
+        coef = coefficients(stats_ref[...], gain_ref[1:2], shift_ref[1:2], None, channels, float(block_rows * width))
         shape = (2 * LANES, LANES)
         row, column = lax.broadcasted_iota(jnp.int32, shape, 0), lane_index(shape)
         gather = jnp.where(((row & (LANES - 1)) >> 1) == column, 0.25, 0.0).astype(BF16)
@@ -350,7 +365,7 @@
             pool(*east_lines),
             place,
         )
-        finish(taps, weight_ref, raw_ref, pack_ref, stat_ref, bias_ref[...], low_rows, outputs, low_width, 1, place)
+        finish(taps, weight_ref, raw_ref, pack_ref, stat_ref, (bias_ref, channels), low_rows, outputs, low_width, 1, place)
 
     return call(
         body,
@@ -358,9 +373,9 @@
         [
             ((block_rows, channels, LANES), BF16),
             ((4, channels, LANES), BF16),
-            ((low_rows, outputs, LANES), F32),
+            ((low_rows, outputs, LANES), BF16),
             ((3 * outputs, LANES), BF16),
-            ((1, LANES), F32),
+            ((DEVICES, LANES), F32),
         ],
         [pltpu.VMEM((low_rows + 2, 3 * channels, LANES), BF16), pltpu.VMEM((low_rows, channels, LANES), BF16)],
     )
@@ -379,7 +394,7 @@
     ):
         place = sc[0]
         coef = coefficients(
-            stats_ref[...], gain_ref[...], shift_ref[...], None, channels, float(low_rows * low_width)
+            stats_ref[...], gain_ref[1:2], shift_ref[1:2], None, channels, float(low_rows * low_width)
         )
         shape = (LANES, LANES)
         row, column = lax.broadcasted_iota(jnp.int32, shape, 0), lane_index(shape)
@@ -431,8 +446,9 @@
     return call(
         body,
         (scalars, raw, stats, partner, ns, east, west, skip, sides, weight, gain, shift),
-        [((block_rows, outputs, LANES), F32), ((3 * outputs, LANES), BF16), ((1, LANES), F32)],
+        [((block_rows, outputs, LANES), BF16), ((3 * outputs, LANES), BF16), ((DEVICES, LANES), F32)],
         [pltpu.VMEM((block_rows + 2, 3 * joined, LANES), BF16), pltpu.VMEM((low_rows, channels, LANES), BF16)],
+        20,
     )
 
 
@@ -440,7 +456,7 @@
     block_rows, channels, width = raw.shape
 
     def body(sc, raw_in, stats_ref, weight_ref, gain_ref, shift_ref, out_ref):
-        coef = coefficients(stats_ref[...], gain_ref[...], shift_ref[...], None, channels, float(block_rows * width))
+        coef = coefficients(stats_ref[...], gain_ref[3:4], shift_ref[3:4], None, channels, float(block_rows * width))
         project = weight_ref[...]
 
         def make(step, carry):
@@ -474,13 +490,20 @@
 def exchange(scalars, pack, width):
     partner = lax.ppermute(pack, "split", [(0, 1), (1, 0)])
     ns, east, west = strips(scalars, pack, partner, width)
-    return partner, vertical(ns), shift_tiles(east, -1), shift_tiles(west, 1)
+    west = shift_tiles(west, 1)
+    east = shift_tiles(east, -1)
+    ns = vertical(ns)
+    return partner, ns, east, west
 
 
 def share(stat):
-    devices = lax.axis_size(TILE) * lax.axis_size("split")
-    copies = jnp.broadcast_to(stat[None], (devices, 1, LANES))
-    return lax.all_to_all(copies, TILE_SPLIT, 0, 0).reshape(devices, LANES)
+    copies = stat.reshape(DEVICES, 1, LANES)
+    return lax.all_to_all(copies, TILE_SPLIT, 0, 0).reshape(DEVICES, LANES)
+
+
+def meet(scalars, pack, stat, width):
+    received = exchange(scalars, pack, width) if pack is not None else None
+    return (share(stat) if stat is not None else None), received
 
 
 def embedding(timestep, time_weight, bias_upper, bias_lower):
@@ -492,7 +515,7 @@
     embedded = jax.nn.silu(jnp.dot(features, time_weight, precision=lax.Precision.HIGHEST))
     both = jnp.concatenate([bias_upper, bias_lower], axis=1)
     biases = jnp.dot(embedded, both, precision=lax.Precision.HIGHEST)
-    return biases[:, : bias_upper.shape[1]], biases[:, bias_upper.shape[1] :]
+    return biases
 
 
 def flat_kernel(kernel):
@@ -536,46 +559,47 @@
     shifts_lower,
 ):
     scalars = seam_scalars(seam_codes)
-    first_bias, second_bias = embedding(timestep, time_weight, bias_upper, bias_lower)
-    channels, block_rows, width = noisy_image.shape[1:]
+    biases = embedding(timestep, time_weight, bias_upper, bias_lower)
+    channels, _, width = noisy_image.shape[1:]
     padding = kernel_upper_first.shape[2] - channels
     image = jnp.transpose(jnp.pad(noisy_image[0], ((0, padding), (0, 0), (0, 0))), (1, 0, 2))
     upper_first = flat_kernel(jnp.pad(kernel_upper_first, ((0, 0), (0, 0), (0, 0), (0, padding))))
     low_width = width // 2
+    width_one = kernel_upper_first.shape[2]
 
     pack = edges_of_image(scalars, image)
-    received = exchange(scalars, pack, width)
-    raw, pack, stat = first_stage(scalars, image, *received, upper_first, first_bias)
-
-    stats, received = share(stat), exchange(scalars, pack, width)
+    _, received = meet(scalars, pack, None, width)
+    raw, pack, stat = first_stage(scalars, image, *received, upper_first, biases)
+
+    stats, received = meet(scalars, pack, stat, width)
     raw, stat, pack = plain_stage(
-        scalars, raw, stats, *received, flat_kernel(kernel_upper_second), gains_upper[0:1], shifts_upper[0:1], first_bias,
-        width, 2,
-    )
-
-    stats, received = share(stat), exchange(scalars, pack, width)
+        scalars, raw, stats, *received, flat_kernel(kernel_upper_second), gains_upper, shifts_upper, 0, biases, 0, width, 2
+    )
+
+    stats, received = meet(scalars, pack, stat, width)
     skip, sides, raw, pack, stat = pool_stage(
-        scalars, raw, stats, *received, flat_kernel(kernel_lower_first), gains_upper[1:2], shifts_upper[1:2], second_bias
-    )
-
-    stats, received = share(stat), exchange(scalars, pack, low_width)
+        scalars, raw, stats, *received, flat_kernel(kernel_lower_first), gains_upper, shifts_upper, biases
+    )
+
+    stats, received = meet(scalars, pack, stat, low_width)
     raw, stat, pack = plain_stage(
-        scalars, raw, stats, *received, flat_kernel(kernel_lower_second), gains_lower[0:1], shifts_lower[0:1], second_bias,
+        scalars, raw, stats, *received, flat_kernel(kernel_lower_second), gains_lower, shifts_lower, 0, biases, width_one,
         low_width, 1,
     )
 
-    stats, received = share(stat), exchange(scalars, pack, low_width)
+    stats, received = meet(scalars, pack, stat, low_width)
     raw, pack, stat = decode_stage(
-        scalars, raw, stats, *received, skip, sides, flat_kernel(kernel_decode_first), gains_lower[1:2], shifts_lower[1:2]
-    )
-
-    stats, received = share(stat), exchange(scalars, pack, width)
+        scalars, raw, stats, *received, skip, sides, flat_kernel(kernel_decode_first), gains_lower, shifts_lower
+    )
+
+    stats, received = meet(scalars, pack, stat, width)
     raw, stat = plain_stage(
-        scalars, raw, stats, *received, flat_kernel(kernel_decode_second), gains_upper[2:3], shifts_upper[2:3], None, width, 0
-    )
-
+        scalars, raw, stats, *received, flat_kernel(kernel_decode_second), gains_upper, shifts_upper, 2, None, 0, width, 0
+    )
+
+    stats, _ = meet(scalars, None, stat, width)
     project = jnp.pad(output_weight, ((0, padding), (0, 0)))
-    result = project_stage(scalars, raw, share(stat), project, gains_upper[3:4], shifts_upper[3:4], channels)
+    result = project_stage(scalars, raw, stats, project, gains_upper, shifts_upper, channels)
     return jnp.transpose(result, (1, 0, 2))[None]
 
 

time: 243 us -> 214 us (0.88)
  local copies, waits for them, and re-layouts: 26.3 us -> 6.92 us
  Pallas kernels: 75.9 us -> 61.6 us
  starting transfers between devices: 98.8 us -> 102 us
    pallas_call x14, Pallas kernels: 75.9 us -> 61.6 us  [call(): pl.pallas_call(body, in_specs=[SCALARS] + [WHOLE] * (len(operands) - 1),...]
    unnamed x62 -> x32, local copies, waits for them, and re-layouts: 15.7 us -> 3.66 us
    broadcast_in_dim x6 -> x0, local copies, waits for them, and re-layouts: 3.98 us -> none  [share(): copies = jnp.broadcast_to(stat[None], (devices, 1, LANES))]
    all_to_all x6, starting transfers between devices: 56.8 us -> 60 us  [share(): return lax.all_to_all(copies, TILE_SPLIT, 0, 0).reshape(DEVICES, LANES)]
  transfers between devices with their start and end apart: 30 -> 30, of which waited for: 12 -> 12; matrix products, arithmetic and copies ran while one was open for 3% -> 1% of each run, Pallas kernels for 2% -> 2%
where the time goes in v1:
time: 214 us; the launch traced here: 213 us
  starting transfers between devices  102 us (48%)
  Pallas kernels  61.6 us (29%)
  waiting for transfers between devices  38.3 us (18%)
  local copies, waits for them, and re-layouts  6.92 us (3%)
  between operations  3.52 us (2%)
    pallas_call x14, Pallas kernels, call(): pl.pallas_call(body, in_specs=[SCALARS] + [WHOLE] * (len(operands) - 1),...  61.6 us
    all_to_all x6, starting transfers between devices, share(): return lax.all_to_all(copies, TILE_SPLIT, 0, 0).reshape(DEVICES, LANES)  60 us
    all_to_all x6, waiting for transfers between devices, share(): return lax.all_to_all(copies, TILE_SPLIT, 0, 0).reshape(DEVICES, LANES)  25.6 us
    ppermute x6, starting transfers between devices, exchange(): partner = lax.ppermute(pack, 'split', [(0, 1), (1, 0)])  18.8 us
    ppermute x12, starting transfers between devices, shift_tiles(): lax.ppermute(value, TILE, [(t, (t + steps) % count) for t in range(count)])  13.7 us
    ppermute x6, starting transfers between devices, vertical(): return lax.ppermute(value, TILE_SPLIT, pairs)  9.61 us
    ppermute x6, waiting for transfers between devices, vertical(): return lax.ppermute(value, TILE_SPLIT, pairs)  6.8 us
  transfers between devices with their start and end apart: 30, of which 12 were waited for; matrix products, arithmetic and copies ran while one was open for 1% of the time, Pallas kernels for 2%

profile of v1, /device:TPU:1, one launch (start us, length us, event | category | flops | bytes accessed | tf_op | source)
XLA Modules:
  0.0 213.0 jit_solution(6593462363557962258)
XLA Ops:
  0.0 0.7 copy-done.14
  0.7 0.7 constant_dynamic-slice_fusion.1
  3.9 1.6 copy.54
  5.7 1.3 shard_map.163.mine_ref
  7.0 3.8 %collective-permute-start = (bf16[144,128]{1,0:T(8,128)(2,1)S(1)}, bf16[144,128]{1,0:T(8,128)(2,1)S(1)}, u32[]{:S(2)}, u32[]{:S(2)}) collective-permute-start(bf16[144,128]{1,0:T(8,128)(2,1)S(1)} %shard_map.163.mine_ref), channel_id=1, source_target_pairs={{0,1},{1,0},{2,3},{3,2},{4,5},{5,4},{6,7},{7,6},{8,9},{9,8},{10,11... | collective-permute-start | bytes 110600 | tf_op jit(solution)/shard_map/ppermute | solution.py:491
  11.5 0.2 fusion.4
  11.9 0.6 copy-done.11
  12.4 0.3 fusion.bias_ref.rest_0_
  12.7 0.9 shard_map.164
  13.6 1.7 collective-permute-start.1
  15.3 1.6 collective-permute-start.2
  16.9 1.2 collective-permute-start.3
  18.3 2.4 %collective-permute-done.1.ns_ref = bf16[48,128]{1,0:T(8,128)(2,1)S(1)} collective-permute-done((bf16[48,128]{1,0:T(8,128)(2,1)S(1)}, bf16[48,128]{1,0:T(8,128)(2,1)S(1)}, u32[]{:S(2)}, u32[]{:S(2)}) %collective-permute-start.1) | collective-permute-done | bytes 12320 | tf_op jit(solution)/shard_map/ppermute | solution.py:487
  20.7 0.6 collective-permute-done.3.west_ref
  21.2 7.4 %shard_map.165 = (bf16[64,48,128]{2,1,0:T(8,128)(2,1)S(1)}, bf16[144,128]{1,0:T(8,128)(2,1)S(1)}, f32[128,128]{1,0:T(8,128)}) custom-call(s32[7]{0:T(128)S(1)} %stack.39.sc, bf16[64,48,128]{2,1,0:T(8,128)(2,1)S(1)} %pad_bitcast_fusion.image_ref, bf16[144,128]{1,0:T(8,128)(2,1)S(1)} %collective-permute-done.their_ref.partner_ref, ...), custom_call_target="tpu_custom_call" | custom-call | tf_op jit(solution)/shard_map/pallas_call | solution.py:184
  28.7 11.3 %all-to-all-start = ((f32[128,1,128]{2,1,0:T(1,128)}), f32[128,1,128]{2,1,0:T(1,128)S(1)}, u32[]{:S(2)}, u32[]{:S(2)}) async-start(f32[128,1,128]{2,1,0:T(1,128)} %bitcast.20), calls=%async_computation | async-start | bytes 131072 | tf_op jit(solution)/shard_map/all_to_all | solution.py:501
  40.0 2.9 %collective-permute-start.4 = (bf16[144,128]{1,0:T(8,128)(2,1)S(1)}, bf16[144,128]{1,0:T(8,128)(2,1)S(1)}, u32[]{:S(2)}, u32[]{:S(2)}) collective-permute-start(bf16[144,128]{1,0:T(8,128)(2,1)S(1)} %get-tuple-element.47.mine_ref), channel_id=1, source_target_pairs={{0,1},{1,0},{2,3},{3,2},{4,5},{5,4},{6,7},{7,6},{8,9},{9,8},{10,11... | collective-permute-start | bytes 110600 | tf_op jit(solution)/shard_map/ppermute | solution.py:491
  43.0 1.8 collective-permute-done.4.their_ref.partner_ref
  44.8 0.8 shard_map.166
  45.6 1.5 collective-permute-start.5
  47.2 1.5 collective-permute-start.6
  48.7 1.3 collective-permute-start.7
  50.2 2.2 %collective-permute-done.5.ns_ref = bf16[48,128]{1,0:T(8,128)(2,1)S(1)} collective-permute-done((bf16[48,128]{1,0:T(8,128)(2,1)S(1)}, bf16[48,128]{1,0:T(8,128)(2,1)S(1)}, u32[]{:S(2)}, u32[]{:S(2)}) %collective-permute-start.5) | collective-permute-done | bytes 12320 | tf_op jit(solution)/shard_map/ppermute | solution.py:487
  52.3 0.8 collective-permute-done.7.west_ref
  53.2 8.0 %shard_map.167 = (bf16[64,48,128]{2,1,0:T(8,128)(2,1)S(1)}, f32[128,128]{1,0:T(8,128)}, bf16[288,128]{1,0:T(8,128)(2,1)S(1)}) custom-call(s32[7]{0:T(128)S(1)} %stack.39.sc, bf16[64,48,128]{2,1,0:T(8,128)(2,1)S(1)} %get-tuple-element.45.raw_in, f32[128,128]{1,0:T(8,128)S(1)} %bitcast.63, bf16[144,128]{1,0:T(8,128)(2,1)S(1)} %collective-permute-done.4.their_ref.partner_ref, ...), custom_call_target="tpu_custom_call" | custom-call | tf_op jit(solution)/shard_map/pallas_call | solution.py:184
  61.2 4.4 %collective-permute-start.8 = (bf16[288,128]{1,0:T(8,128)(2,1)S(1)}, bf16[288,128]{1,0:T(8,128)(2,1)S(1)}, u32[]{:S(2)}, u32[]{:S(2)}) collective-permute-start(bf16[288,128]{1,0:T(8,128)(2,1)S(1)} %get-tuple-element.53.mine_ref), channel_id=1, source_target_pairs={{0,1},{1,0},{2,3},{3,2},{4,5},{5,4},{6,7},{7,6},{8,9},{9,8},{10,11... | collective-permute-start | bytes 221192 | tf_op jit(solution)/shard_map/ppermute | solution.py:491
  65.6 8.8 %all-to-all-start.1 = ((f32[128,1,128]{2,1,0:T(1,128)}), f32[128,1,128]{2,1,0:T(1,128)S(1)}, u32[]{:S(2)}, u32[]{:S(2)}) async-start(f32[128,1,128]{2,1,0:T(1,128)} %bitcast.24), calls=%async_computation.1 | async-start | bytes 131072 | tf_op jit(solution)/shard_map/all_to_all | solution.py:501
  74.4 0.9 shard_map.168
  75.2 1.3 collective-permute-start.10
  76.5 0.6 collective-permute-start.11
  77.1 1.6 collective-permute-start.9
  78.8 5.5 %all-to-all-done.1 = f32[128,1,128]{2,1,0:T(1,128)S(1)} async-done(((f32[128,1,128]{2,1,0:T(1,128)}), f32[128,1,128]{2,1,0:T(1,128)S(1)}, u32[]{:S(2)}, u32[]{:S(2)}) %all-to-all-start.1) | async-done | bytes 65568 | tf_op jit(solution)/shard_map/all_to_all | solution.py:501
  84.3 7.7 %shard_map.169 = (bf16[64,48,128]{2,1,0:T(8,128)(2,1)S(1)}, bf16[4,48,128]{2,1,0:T(8,128)(2,1)S(1)}, bf16[32,96,128]{2,1,0:T(8,128)(2,1)S(1)}, bf16[288,128]{1,0:T(8,128)(2,1)S(1)}, f32[128,128]{1,0:T(8,128)}) custom-call(s32[7]{0:T(128)S(1)} %stack.39.sc, bf16[64,48,128]{2,1,0:T(8,128)(2,1)S(1)} %get-tuple-element.51.raw_in, f32[128,128]{1,0:T(8,128)S(1)} %bitcast.66, ...), custom_call_target="tpu_custom_call" | custom-call | tf_op jit(solution)/shard_map/pallas_call | solution.py:184
  92.0 2.1 collective-permute-start.12
  94.1 10.6 %all-to-all-start.2 = ((f32[128,1,128]{2,1,0:T(1,128)}), f32[128,1,128]{2,1,0:T(1,128)S(1)}, u32[]{:S(2)}, u32[]{:S(2)}) async-start(f32[128,1,128]{2,1,0:T(1,128)} %bitcast.29), calls=%async_computation.2 | async-start | bytes 131072 | tf_op jit(solution)/shard_map/all_to_all | solution.py:501
  104.7 0.9 shard_map.170
  105.6 1.5 collective-permute-start.13
  107.1 0.7 collective-permute-start.14
  107.8 1.1 collective-permute-start.15
  109.3 5.2 %all-to-all-done.2 = f32[128,1,128]{2,1,0:T(1,128)S(1)} async-done(((f32[128,1,128]{2,1,0:T(1,128)}), f32[128,1,128]{2,1,0:T(1,128)S(1)}, u32[]{:S(2)}, u32[]{:S(2)}) %all-to-all-start.2) | async-done | bytes 65568 | tf_op jit(solution)/shard_map/all_to_all | solution.py:501
  114.5 0.7 copy-done.3
  115.2 6.0 %shard_map.171 = (bf16[32,96,128]{2,1,0:T(8,128)(2,1)S(1)}, f32[128,128]{1,0:T(8,128)}, bf16[288,128]{1,0:T(8,128)(2,1)S(1)}) custom-call(s32[7]{0:T(128)S(1)} %stack.39.sc, bf16[32,96,128]{2,1,0:T(8,128)(2,1)S(1)} %get-tuple-element.57.raw_in, f32[128,128]{1,0:T(8,128)S(1)} %bitcast.67, bf16[288,128]{1,0:T(8,128)(2,1)S(1)} %collective-permute-done.12.their_ref.partner_ref, ...), custom_call_target="tpu_custom_call" | custom-call | tf_op jit(solution)/shard_map/pallas_call | solution.py:184
  121.2 2.6 %collective-permute-start.16 = (bf16[288,128]{1,0:T(8,128)(2,1)S(1)}, bf16[288,128]{1,0:T(8,128)(2,1)S(1)}, u32[]{:S(2)}, u32[]{:S(2)}) collective-permute-start(bf16[288,128]{1,0:T(8,128)(2,1)S(1)} %get-tuple-element.65.mine_ref), channel_id=1, source_target_pairs={{0,1},{1,0},{2,3},{3,2},{4,5},{5,4},{6,7},{7,6},{8,9},{9,8},{10,11... | collective-permute-start | bytes 221192 | tf_op jit(solution)/shard_map/ppermute | solution.py:491
  123.8 9.2 %all-to-all-start.3 = ((f32[128,1,128]{2,1,0:T(1,128)}), f32[128,1,128]{2,1,0:T(1,128)S(1)}, u32[]{:S(2)}, u32[]{:S(2)}) async-start(f32[128,1,128]{2,1,0:T(1,128)} %bitcast.34), calls=%async_computation.3 | async-start | bytes 131072 | tf_op jit(solution)/shard_map/all_to_all | solution.py:501
  133.1 0.9 shard_map.172
  134.0 1.7 collective-permute-start.17
  135.7 0.7 collective-permute-start.18
  136.3 1.1 collective-permute-start.19
  137.8 5.2 %all-to-all-done.3 = f32[128,1,128]{2,1,0:T(1,128)S(1)} async-done(((f32[128,1,128]{2,1,0:T(1,128)}), f32[128,1,128]{2,1,0:T(1,128)S(1)}, u32[]{:S(2)}, u32[]{:S(2)}) %all-to-all-start.3) | async-done | bytes 65568 | tf_op jit(solution)/shard_map/all_to_all | solution.py:501
  143.0 15.9 %shard_map.173 = (bf16[64,48,128]{2,1,0:T(8,128)(2,1)S(1)}, bf16[144,128]{1,0:T(8,128)(2,1)S(1)}, f32[128,128]{1,0:T(8,128)}) custom-call(s32[7]{0:T(128)S(1)} %stack.39.sc, bf16[32,96,128]{2,1,0:T(8,128)(2,1)S(1)} %get-tuple-element.63.raw_in, f32[128,128]{1,0:T(8,128)S(1)} %bitcast.64, bf16[288,128]{1,0:T(8,128)(2,1)S(1)} %collective-permute-done.16.their_ref.partner_ref, ...), custom_call_target="tpu_custom_call" | custom-call | tf_op jit(solution)/shard_map/pallas_call | solution.py:184
  158.9 9.4 %all-to-all-start.4 = ((f32[128,1,128]{2,1,0:T(1,128)}), f32[128,1,128]{2,1,0:T(1,128)S(1)}, u32[]{:S(2)}, u32[]{:S(2)}) async-start(f32[128,1,128]{2,1,0:T(1,128)} %bitcast.38), calls=%async_computation.4 | async-start | bytes 131072 | tf_op jit(solution)/shard_map/all_to_all | solution.py:501
  168.3 2.9 %collective-permute-start.20 = (bf16[144,128]{1,0:T(8,128)(2,1)S(1)}, bf16[144,128]{1,0:T(8,128)(2,1)S(1)}, u32[]{:S(2)}, u32[]{:S(2)}) collective-permute-start(bf16[144,128]{1,0:T(8,128)(2,1)S(1)} %get-tuple-element.73.mine_ref), channel_id=1, source_target_pairs={{0,1},{1,0},{2,3},{3,2},{4,5},{5,4},{6,7},{7,6},{8,9},{9,8},{10,11... | collective-permute-start | bytes 110600 | tf_op jit(solution)/shard_map/ppermute | solution.py:491
  171.2 1.8 collective-permute-done.20.their_ref.partner_ref
  173.1 0.8 shard_map.174
  173.9 1.5 collective-permute-start.21
  175.4 1.5 collective-permute-start.22
  176.9 1.3 collective-permute-start.23
  178.4 2.2 %collective-permute-done.21.ns_ref = bf16[48,128]{1,0:T(8,128)(2,1)S(1)} collective-permute-done((bf16[48,128]{1,0:T(8,128)(2,1)S(1)}, bf16[48,128]{1,0:T(8,128)(2,1)S(1)}, u32[]{:S(2)}, u32[]{:S(2)}) %collective-permute-start.21) | collective-permute-done | bytes 12320 | tf_op jit(solution)/shard_map/ppermute | solution.py:487
  180.6 0.8 collective-permute-done.23.west_ref
  181.4 6.9 %shard_map.175 = (bf16[64,48,128]{2,1,0:T(8,128)(2,1)S(1)}, f32[128,128]{1,0:T(8,128)}) custom-call(s32[7]{0:T(128)S(1)} %stack.39.sc, bf16[64,48,128]{2,1,0:T(8,128)(2,1)S(1)} %get-tuple-element.71.raw_in, f32[128,128]{1,0:T(8,128)S(1)} %bitcast.65, bf16[144,128]{1,0:T(8,128)(2,1)S(1)} %collective-permute-done.20.their_ref.partner_ref, ...), custom_call_target="tpu_custom_call" | custom-call | tf_op jit(solution)/shard_map/pallas_call | solution.py:184
  188.3 10.7 %all-to-all-start.5 = ((f32[128,1,128]{2,1,0:T(1,128)}), f32[128,1,128]{2,1,0:T(1,128)S(1)}, u32[]{:S(2)}, u32[]{:S(2)}) async-start(f32[128,1,128]{2,1,0:T(1,128)} %bitcast.42), calls=%async_computation.5 | async-start | bytes 131072 | tf_op jit(solution)/shard_map/all_to_all | solution.py:501
  199.0 9.7 %all-to-all-done.5 = f32[128,1,128]{2,1,0:T(1,128)S(1)} async-done(((f32[128,1,128]{2,1,0:T(1,128)}), f32[128,1,128]{2,1,0:T(1,128)S(1)}, u32[]{:S(2)}, u32[]{:S(2)}) %all-to-all-start.5) | async-done | bytes 65568 | tf_op jit(solution)/shard_map/all_to_all | solution.py:501
  208.7 3.2 %shard_map.176 = bf16[64,45,128]{2,1,0:T(8,128)(2,1)S(1)} custom-call(s32[7]{0:T(128)S(1)} %stack.39.sc, bf16[64,48,128]{2,1,0:T(8,128)(2,1)S(1)} %get-tuple-element.77.raw_in, f32[128,128]{1,0:T(8,128)S(1)} %bitcast.68, bf16[48,48]{1,0:T(8,128)(2,1)S(1)} %pad.14.weight_ref, f32[4,48]{1,0:T(4,128)S(1)} %copy-done.1, f32[4,48]{1,0:T(4,128)S(1)} %copy-done.2), custom_call_target="tpu_custom_call" | custom-call | tf_op jit(solution)/shard_map/pallas_call | solution.py:184
  211.9 1.1 copy.52
  (63 shorter events, 1.8 us)
Async XLA Ops:
  0.0 11.5 %copy-start = (f32[48,192]{1,0:T(8,128)S(1)}, f32[48,192]{1,0:T(8,128)}, u32[]{:S(2)}) copy-start(f32[48,192]{1,0:T(8,128)} %param.20) | copy-start | bytes 110596
  0.0 0.7 copy-start.14
  7.0 4.8 %copy-start.12 = (f32[192,48]{0,1:T(8,128)S(1)}, f32[192,48]{0,1:T(8,128)}, u32[]{:S(2)}) copy-start(f32[192,48]{0,1:T(8,128)} %param.21) | copy-start | bytes 110596
  7.0 5.7 %collective-permute-start = (bf16[144,128]{1,0:T(8,128)(2,1)S(1)}, bf16[144,128]{1,0:T(8,128)(2,1)S(1)}, u32[]{:S(2)}, u32[]{:S(2)}) collective-permute-start(bf16[144,128]{1,0:T(8,128)(2,1)S(1)} %shard_map.163.mine_ref), channel_id=1, source_target_pairs={{0,1},{1,0},{2,3},{3,2},{4,5},{5,4},{6,7},{7,6},{8,9},{9,8},{10,11... | collective-permute-start | bytes 110600 | tf_op jit(solution)/shard_map/ppermute | solution.py:491
  11.5 0.9 copy-start.11
  12.4 5.6 %copy-start.7 = (bf16[3,3,48,45]{3,2,1,0:T(8,128)(2,1)S(1)}, bf16[3,3,48,45]{3,2,1,0:T(8,128)(2,1)}, u32[]{:S(2)}) copy-start(bf16[3,3,48,45]{3,2,1,0:T(8,128)(2,1)} %param.23) | copy-start | bytes 116644
  13.6 7.1 %collective-permute-start.1 = (bf16[48,128]{1,0:T(8,128)(2,1)S(1)}, bf16[48,128]{1,0:T(8,128)(2,1)S(1)}, u32[]{:S(2)}, u32[]{:S(2)}) collective-permute-start(bf16[48,128]{1,0:T(8,128)(2,1)S(1)} %get-tuple-element.42), channel_id=1, source_target_pairs={{0,8},{1,121},{2,10},{3,123},{4,12},{5,125},{6,14},{7,127},{8,16},... | collective-permute-start | bytes 36872 | tf_op jit(solution)/shard_map/ppermute | solution.py:487
  15.3 5.4 %collective-permute-start.2 = (bf16[48,128]{1,0:T(8,128)(2,1)S(1)}, bf16[48,128]{1,0:T(8,128)(2,1)S(1)}, u32[]{:S(2)}, u32[]{:S(2)}) collective-permute-start(bf16[48,128]{1,0:T(8,128)(2,1)S(1)} %get-tuple-element.43), channel_id=1, source_target_pairs={{0,126},{2,0},{4,2},{6,4},{8,6},{10,8},{12,10},{14,12},{16,14},{18... | collective-permute-start | bytes 36872 | tf_op jit(solution)/shard_map/ppermute | solution.py:478
  16.9 4.4 %collective-permute-start.3 = (bf16[48,128]{1,0:T(8,128)(2,1)S(1)}, bf16[48,128]{1,0:T(8,128)(2,1)S(1)}, u32[]{:S(2)}, u32[]{:S(2)}) collective-permute-start(bf16[48,128]{1,0:T(8,128)(2,1)S(1)} %get-tuple-element.44), channel_id=1, source_target_pairs={{0,2},{2,4},{4,6},{6,8},{8,10},{10,12},{12,14},{14,16},{16,18},{18... | collective-permute-start | bytes 36872 | tf_op jit(solution)/shard_map/ppermute | solution.py:478
  28.7 21.3 %copy-start.9 = (bf16[3,3,48,48]{3,2,1,0:T(8,128)(2,1)S(1)}, bf16[3,3,48,48]{3,2,1,0:T(8,128)(2,1)}, u32[]{:S(2)}) copy-start(bf16[3,3,48,48]{3,2,1,0:T(8,128)(2,1)} %param.24) | copy-start | bytes 124420
  28.7 24.5 %all-to-all-start = ((f32[128,1,128]{2,1,0:T(1,128)}), f32[128,1,128]{2,1,0:T(1,128)S(1)}, u32[]{:S(2)}, u32[]{:S(2)}) async-start(f32[128,1,128]{2,1,0:T(1,128)} %bitcast.20), calls=%async_computation | async-start | bytes 131072 | tf_op jit(solution)/shard_map/all_to_all | solution.py:501
  40.0 4.8 %collective-permute-start.4 = (bf16[144,128]{1,0:T(8,128)(2,1)S(1)}, bf16[144,128]{1,0:T(8,128)(2,1)S(1)}, u32[]{:S(2)}, u32[]{:S(2)}) collective-permute-start(bf16[144,128]{1,0:T(8,128)(2,1)S(1)} %get-tuple-element.47.mine_ref), channel_id=1, source_target_pairs={{0,1},{1,0},{2,3},{3,2},{4,5},{5,4},{6,7},{7,6},{8,9},{9,8},{10,11... | collective-permute-start | bytes 110600 | tf_op jit(solution)/shard_map/ppermute | solution.py:491
  45.6 6.7 %collective-permute-start.5 = (bf16[48,128]{1,0:T(8,128)(2,1)S(1)}, bf16[48,128]{1,0:T(8,128)(2,1)S(1)}, u32[]{:S(2)}, u32[]{:S(2)}) collective-permute-start(bf16[48,128]{1,0:T(8,128)(2,1)S(1)} %get-tuple-element.48), channel_id=1, source_target_pairs={{0,8},{1,121},{2,10},{3,123},{4,12},{5,125},{6,14},{7,127},{8,16},... | collective-permute-start | bytes 36872 | tf_op jit(solution)/shard_map/ppermute | solution.py:487
  47.2 5.2 %collective-permute-start.6 = (bf16[48,128]{1,0:T(8,128)(2,1)S(1)}, bf16[48,128]{1,0:T(8,128)(2,1)S(1)}, u32[]{:S(2)}, u32[]{:S(2)}) collective-permute-start(bf16[48,128]{1,0:T(8,128)(2,1)S(1)} %get-tuple-element.49), channel_id=1, source_target_pairs={{0,126},{2,0},{4,2},{6,4},{8,6},{10,8},{12,10},{14,12},{16,14},{18... | collective-permute-start | bytes 36872 | tf_op jit(solution)/shard_map/ppermute | solution.py:478
  48.7 4.5 %collective-permute-start.7 = (bf16[48,128]{1,0:T(8,128)(2,1)S(1)}, bf16[48,128]{1,0:T(8,128)(2,1)S(1)}, u32[]{:S(2)}, u32[]{:S(2)}) collective-permute-start(bf16[48,128]{1,0:T(8,128)(2,1)S(1)} %get-tuple-element.50), channel_id=1, source_target_pairs={{0,2},{2,4},{4,6},{6,8},{8,10},{10,12},{12,14},{14,16},{16,18},{18... | collective-permute-start | bytes 36872 | tf_op jit(solution)/shard_map/ppermute | solution.py:478
  50.0 3.2 %copy-start.2 = (f32[4,48]{1,0:T(4,128)S(1)}, f32[4,48]{1,0:T(4,128)}, u32[]{:S(2)}) copy-start(f32[4,48]{1,0:T(4,128)} %shift_ref.11) | copy-start | bytes 2308
  50.1 3.0 %copy-start.1 = (f32[4,48]{1,0:T(4,128)S(1)}, f32[4,48]{1,0:T(4,128)}, u32[]{:S(2)}) copy-start(f32[4,48]{1,0:T(4,128)} %gain_ref.11) | copy-start | bytes 2308
  61.2 13.2 %collective-permute-start.8 = (bf16[288,128]{1,0:T(8,128)(2,1)S(1)}, bf16[288,128]{1,0:T(8,128)(2,1)S(1)}, u32[]{:S(2)}, u32[]{:S(2)}) collective-permute-start(bf16[288,128]{1,0:T(8,128)(2,1)S(1)} %get-tuple-element.53.mine_ref), channel_id=1, source_target_pairs={{0,1},{1,0},{2,3},{3,2},{4,5},{5,4},{6,7},{7,6},{8,9},{9,8},{10,11... | collective-permute-start | bytes 221192 | tf_op jit(solution)/shard_map/ppermute | solution.py:491
  65.6 18.7 %all-to-all-start.1 = ((f32[128,1,128]{2,1,0:T(1,128)}), f32[128,1,128]{2,1,0:T(1,128)S(1)}, u32[]{:S(2)}, u32[]{:S(2)}) async-start(f32[128,1,128]{2,1,0:T(1,128)} %bitcast.24), calls=%async_computation.1 | async-start | bytes 131072 | tf_op jit(solution)/shard_map/all_to_all | solution.py:501
  74.4 4.3 %copy-start.8 = (bf16[3,3,96,48]{2,3,1,0:T(8,128)(2,1)S(1)}, bf16[3,3,96,48]{2,3,1,0:T(8,128)(2,1)}, u32[]{:S(2)}) copy-start(bf16[3,3,96,48]{2,3,1,0:T(8,128)(2,1)} %param.25) | copy-start | bytes 248836
  75.2 9.0 %collective-permute-start.10 = (bf16[96,128]{1,0:T(8,128)(2,1)S(1)}, bf16[96,128]{1,0:T(8,128)(2,1)S(1)}, u32[]{:S(2)}, u32[]{:S(2)}) collective-permute-start(bf16[96,128]{1,0:T(8,128)(2,1)S(1)} %get-tuple-element.55), channel_id=1, source_target_pairs={{0,126},{2,0},{4,2},{6,4},{8,6},{10,8},{12,10},{14,12},{16,14},{18... | collective-permute-start | bytes 73736 | tf_op jit(solution)/shard_map/ppermute | solution.py:478
  76.5 7.7 %collective-permute-start.11 = (bf16[96,128]{1,0:T(8,128)(2,1)S(1)}, bf16[96,128]{1,0:T(8,128)(2,1)S(1)}, u32[]{:S(2)}, u32[]{:S(2)}) collective-permute-start(bf16[96,128]{1,0:T(8,128)(2,1)S(1)} %get-tuple-element.56), channel_id=1, source_target_pairs={{0,2},{2,4},{4,6},{6,8},{8,10},{10,12},{12,14},{14,16},{16,18},{18... | collective-permute-start | bytes 73736 | tf_op jit(solution)/shard_map/ppermute | solution.py:478
  77.1 7.2 %collective-permute-start.9 = (bf16[96,128]{1,0:T(8,128)(2,1)S(1)}, bf16[96,128]{1,0:T(8,128)(2,1)S(1)}, u32[]{:S(2)}, u32[]{:S(2)}) collective-permute-start(bf16[96,128]{1,0:T(8,128)(2,1)S(1)} %get-tuple-element.54), channel_id=1, source_target_pairs={{0,8},{1,121},{2,10},{3,123},{4,12},{5,125},{6,14},{7,127},{8,16},... | collective-permute-start | bytes 73736 | tf_op jit(solution)/shard_map/ppermute | solution.py:487
  92.0 16.9 %copy-start.5 = (bf16[3,3,96,96]{3,2,1,0:T(8,128)(2,1)S(1)}, bf16[3,3,96,96]{3,2,1,0:T(8,128)(2,1)}, u32[]{:S(2)}) copy-start(bf16[3,3,96,96]{3,2,1,0:T(8,128)(2,1)} %param.26) | copy-start | bytes 497668
  92.0 12.7 %collective-permute-start.12 = (bf16[288,128]{1,0:T(8,128)(2,1)S(1)}, bf16[288,128]{1,0:T(8,128)(2,1)S(1)}, u32[]{:S(2)}, u32[]{:S(2)}) collective-permute-start(bf16[288,128]{1,0:T(8,128)(2,1)S(1)} %get-tuple-element.59.mine_ref), channel_id=1, source_target_pairs={{0,1},{1,0},{2,3},{3,2},{4,5},{5,4},{6,7},{7,6},{8,9},{9,8},{10,11... | collective-permute-start | bytes 221192 | tf_op jit(solution)/shard_map/ppermute | solution.py:491
  94.1 20.4 %all-to-all-start.2 = ((f32[128,1,128]{2,1,0:T(1,128)}), f32[128,1,128]{2,1,0:T(1,128)S(1)}, u32[]{:S(2)}, u32[]{:S(2)}) async-start(f32[128,1,128]{2,1,0:T(1,128)} %bitcast.29), calls=%async_computation.2 | async-start | bytes 131072 | tf_op jit(solution)/shard_map/all_to_all | solution.py:501
  105.6 8.9 %collective-permute-start.13 = (bf16[96,128]{1,0:T(8,128)(2,1)S(1)}, bf16[96,128]{1,0:T(8,128)(2,1)S(1)}, u32[]{:S(2)}, u32[]{:S(2)}) collective-permute-start(bf16[96,128]{1,0:T(8,128)(2,1)S(1)} %get-tuple-element.60), channel_id=1, source_target_pairs={{0,8},{1,121},{2,10},{3,123},{4,12},{5,125},{6,14},{7,127},{8,16},... | collective-permute-start | bytes 73736 | tf_op jit(solution)/shard_map/ppermute | solution.py:487
  107.1 7.4 %collective-permute-start.14 = (bf16[96,128]{1,0:T(8,128)(2,1)S(1)}, bf16[96,128]{1,0:T(8,128)(2,1)S(1)}, u32[]{:S(2)}, u32[]{:S(2)}) collective-permute-start(bf16[96,128]{1,0:T(8,128)(2,1)S(1)} %get-tuple-element.61), channel_id=1, source_target_pairs={{0,126},{2,0},{4,2},{6,4},{8,6},{10,8},{12,10},{14,12},{16,14},{18... | collective-permute-start | bytes 73736 | tf_op jit(solution)/shard_map/ppermute | solution.py:478
  107.8 6.7 %collective-permute-start.15 = (bf16[96,128]{1,0:T(8,128)(2,1)S(1)}, bf16[96,128]{1,0:T(8,128)(2,1)S(1)}, u32[]{:S(2)}, u32[]{:S(2)}) collective-permute-start(bf16[96,128]{1,0:T(8,128)(2,1)S(1)} %get-tuple-element.62), channel_id=1, source_target_pairs={{0,2},{2,4},{4,6},{6,8},{8,10},{10,12},{12,14},{14,16},{16,18},{18... | collective-permute-start | bytes 73736 | tf_op jit(solution)/shard_map/ppermute | solution.py:478
  109.1 5.4 %copy-start.4 = (f32[2,96]{1,0:T(2,128)S(1)}, f32[2,96]{1,0:T(2,128)}, u32[]{:S(2)}) copy-start(f32[2,96]{1,0:T(2,128)} %shift_ref.9) | copy-start | bytes 2308
  114.5 0.7 copy-start.3
  121.2 16.3 %copy-start.6 = (bf16[3,3,48,144]{3,2,1,0:T(8,128)(2,1)S(1)}, bf16[3,3,48,144]{3,2,1,0:T(8,128)(2,1)}, u32[]{:S(2)}) copy-start(bf16[3,3,48,144]{3,2,1,0:T(8,128)(2,1)} %param.27) | copy-start | bytes 373252
  121.2 11.9 %collective-permute-start.16 = (bf16[288,128]{1,0:T(8,128)(2,1)S(1)}, bf16[288,128]{1,0:T(8,128)(2,1)S(1)}, u32[]{:S(2)}, u32[]{:S(2)}) collective-permute-start(bf16[288,128]{1,0:T(8,128)(2,1)S(1)} %get-tuple-element.65.mine_ref), channel_id=1, source_target_pairs={{0,1},{1,0},{2,3},{3,2},{4,5},{5,4},{6,7},{7,6},{8,9},{9,8},{10,11... | collective-permute-start | bytes 221192 | tf_op jit(solution)/shard_map/ppermute | solution.py:491
  123.8 19.2 %all-to-all-start.3 = ((f32[128,1,128]{2,1,0:T(1,128)}), f32[128,1,128]{2,1,0:T(1,128)S(1)}, u32[]{:S(2)}, u32[]{:S(2)}) async-start(f32[128,1,128]{2,1,0:T(1,128)} %bitcast.34), calls=%async_computation.3 | async-start | bytes 131072 | tf_op jit(solution)/shard_map/all_to_all | solution.py:501
  134.0 9.0 %collective-permute-start.17 = (bf16[96,128]{1,0:T(8,128)(2,1)S(1)}, bf16[96,128]{1,0:T(8,128)(2,1)S(1)}, u32[]{:S(2)}, u32[]{:S(2)}) collective-permute-start(bf16[96,128]{1,0:T(8,128)(2,1)S(1)} %get-tuple-element.66), channel_id=1, source_target_pairs={{0,8},{1,121},{2,10},{3,123},{4,12},{5,125},{6,14},{7,127},{8,16},... | collective-permute-start | bytes 73736 | tf_op jit(solution)/shard_map/ppermute | solution.py:487
  135.7 7.4 %collective-permute-start.18 = (bf16[96,128]{1,0:T(8,128)(2,1)S(1)}, bf16[96,128]{1,0:T(8,128)(2,1)S(1)}, u32[]{:S(2)}, u32[]{:S(2)}) collective-permute-start(bf16[96,128]{1,0:T(8,128)(2,1)S(1)} %get-tuple-element.67), channel_id=1, source_target_pairs={{0,126},{2,0},{4,2},{6,4},{8,6},{10,8},{12,10},{14,12},{16,14},{18... | collective-permute-start | bytes 73736 | tf_op jit(solution)/shard_map/ppermute | solution.py:478
  136.3 6.7 %collective-permute-start.19 = (bf16[96,128]{1,0:T(8,128)(2,1)S(1)}, bf16[96,128]{1,0:T(8,128)(2,1)S(1)}, u32[]{:S(2)}, u32[]{:S(2)}) collective-permute-start(bf16[96,128]{1,0:T(8,128)(2,1)S(1)} %get-tuple-element.68), channel_id=1, source_target_pairs={{0,2},{2,4},{4,6},{6,8},{8,10},{10,12},{12,14},{14,16},{16,18},{18... | collective-permute-start | bytes 73736 | tf_op jit(solution)/shard_map/ppermute | solution.py:478
  158.9 19.3 %copy-start.10 = (bf16[3,3,48,48]{3,2,1,0:T(8,128)(2,1)S(1)}, bf16[3,3,48,48]{3,2,1,0:T(8,128)(2,1)}, u32[]{:S(2)}) copy-start(bf16[3,3,48,48]{3,2,1,0:T(8,128)(2,1)} %param.28) | copy-start | bytes 124420
  158.9 22.5 %all-to-all-start.4 = ((f32[128,1,128]{2,1,0:T(1,128)}), f32[128,1,128]{2,1,0:T(1,128)S(1)}, u32[]{:S(2)}, u32[]{:S(2)}) async-start(f32[128,1,128]{2,1,0:T(1,128)} %bitcast.38), calls=%async_computation.4 | async-start | bytes 131072 | tf_op jit(solution)/shard_map/all_to_all | solution.py:501
  168.3 4.8 %collective-permute-start.20 = (bf16[144,128]{1,0:T(8,128)(2,1)S(1)}, bf16[144,128]{1,0:T(8,128)(2,1)S(1)}, u32[]{:S(2)}, u32[]{:S(2)}) collective-permute-start(bf16[144,128]{1,0:T(8,128)(2,1)S(1)} %get-tuple-element.73.mine_ref), channel_id=1, source_target_pairs={{0,1},{1,0},{2,3},{3,2},{4,5},{5,4},{6,7},{7,6},{8,9},{9,8},{10,11... | collective-permute-start | bytes 110600 | tf_op jit(solution)/shard_map/ppermute | solution.py:491
  173.9 6.7 %collective-permute-start.21 = (bf16[48,128]{1,0:T(8,128)(2,1)S(1)}, bf16[48,128]{1,0:T(8,128)(2,1)S(1)}, u32[]{:S(2)}, u32[]{:S(2)}) collective-permute-start(bf16[48,128]{1,0:T(8,128)(2,1)S(1)} %get-tuple-element.74), channel_id=1, source_target_pairs={{0,8},{1,121},{2,10},{3,123},{4,12},{5,125},{6,14},{7,127},{8,16},... | collective-permute-start | bytes 36872 | tf_op jit(solution)/shard_map/ppermute | solution.py:487
  175.4 5.2 %collective-permute-start.22 = (bf16[48,128]{1,0:T(8,128)(2,1)S(1)}, bf16[48,128]{1,0:T(8,128)(2,1)S(1)}, u32[]{:S(2)}, u32[]{:S(2)}) collective-permute-start(bf16[48,128]{1,0:T(8,128)(2,1)S(1)} %get-tuple-element.75), channel_id=1, source_target_pairs={{0,126},{2,0},{4,2},{6,4},{8,6},{10,8},{12,10},{14,12},{16,14},{18... | collective-permute-start | bytes 36872 | tf_op jit(solution)/shard_map/ppermute | solution.py:478
  176.9 4.5 %collective-permute-start.23 = (bf16[48,128]{1,0:T(8,128)(2,1)S(1)}, bf16[48,128]{1,0:T(8,128)(2,1)S(1)}, u32[]{:S(2)}, u32[]{:S(2)}) collective-permute-start(bf16[48,128]{1,0:T(8,128)(2,1)S(1)} %get-tuple-element.76), channel_id=1, source_target_pairs={{0,2},{2,4},{4,6},{6,8},{8,10},{10,12},{12,14},{14,16},{16,18},{18... | collective-permute-start | bytes 36872 | tf_op jit(solution)/shard_map/ppermute | solution.py:478
  188.3 10.7 %copy-start.13 = (bf16[45,48]{1,0:T(8,128)(2,1)S(1)}, bf16[45,48]{1,0:T(8,128)(2,1)}, u32[]{:S(2)}) copy-start(bf16[45,48]{1,0:T(8,128)(2,1)} %param.29) | copy-start | bytes 12964
  188.3 20.4 %all-to-all-start.5 = ((f32[128,1,128]{2,1,0:T(1,128)}), f32[128,1,128]{2,1,0:T(1,128)S(1)}, u32[]{:S(2)}, u32[]{:S(2)}) async-start(f32[128,1,128]{2,1,0:T(1,128)} %bitcast.42), calls=%async_computation.5 | async-start | bytes 131072 | tf_op jit(solution)/shard_map/all_to_all | solution.py:501

commit v2 on v1

--- a/solution.py
+++ b/solution.py
@@ -82,7 +82,7 @@
     return mean_row + jnp.sum(jnp.where(lane == group + GROUPS, total, 0.0), axis=0, keepdims=True)
 
 
-def frame_rows(taps, first, channels, width, block_rows, rows_of, upper, lower, west, east, place, together=4):
+def frame_rows(taps, first, channels, width, block_rows, rows_of, upper, lower, west, east, place, together=16):
     stride = taps.shape[1] // 3
     lane = lane_index((channels, LANES))
     base = place * block_rows
@@ -110,7 +110,7 @@
     put(block_rows + 1, lower, jnp.where(place == 1, zero, hw), jnp.where(place == 1, zero, he))
 
 
-def convolve_rows(taps, weight_ref, raw_ref, block_rows, together=4):
+def convolve_rows(taps, weight_ref, raw_ref, block_rows, together=16):
     outputs = weight_ref.shape[0]
     depth = taps.shape[1] * 3
     weight = weight_ref[...]
@@ -134,7 +134,7 @@
     return lax.fori_loop(0, block_rows // together, body, (zero, zero))
 
 
-def pack_edges(raw_ref, pack_ref, block_rows, channels, width, depth, place, together=8):
+def pack_edges(raw_ref, pack_ref, block_rows, channels, width, depth, place, together=16):
     size = depth * channels
     lane = lane_index((channels, LANES))
     last = block_rows - 1
@@ -191,20 +191,45 @@
     )(*operands)
 
 
-def edges_of_image(scalars, image):
+def edges_of_image(here, image, seam_codes):
     block_rows, channels, width = image.shape
-
-    def body(sc, image_ref, pack_ref):
-        pack_edges(image_ref, pack_ref, block_rows, channels, width, 1, sc[0])
-
-    return call(body, (scalars, image), [((3 * channels, LANES), BF16)])[0]
+    count = seam_codes.shape[0]
+
+    def body(here_ref, codes, image_ref, pack_ref, scalar_ref):
+        tile, place = here_ref[0], here_ref[1]
+        pack_edges(image_ref, pack_ref, block_rows, channels, width, 1, place)
+
+        def facing(steps, side):
+            k = (side + 2 + codes[(tile + count + steps) % count, side]) % 4
+            return k, jnp.where((k < 2) == (side < 2), 1, 0)
+
+        odd = tile % 2 == 1
+        north, south = facing(ROW_TILES, 0), facing(-ROW_TILES, 2)
+        east, west = facing(-1, 1), facing(1, 3)
+        scalar_ref[0] = place
+        for k in range(2):
+            scalar_ref[1 + k] = jnp.where(place == 0, north[k], south[k])
+            scalar_ref[3 + k] = jnp.where(odd, east[k], west[k])
+            scalar_ref[5 + k] = jnp.where(odd, west[k], east[k])
+        scalar_ref[7] = jnp.where(odd, 1, 0)
+
+    return pl.pallas_call(
+        body,
+        in_specs=[SCALARS, SCALARS, WHOLE],
+        out_specs=[WHOLE, SCALARS],
+        out_shape=[
+            jax.ShapeDtypeStruct((3 * channels, LANES), BF16),
+            jax.ShapeDtypeStruct((8,), jnp.int32),
+        ],
+        compiler_params=pltpu.CompilerParams(vmem_limit_bytes=12 * 1024 * 1024),
+    )(here, seam_codes, image)
 
 
 def strips(scalars, pack, partner, width):
     size = pack.shape[0] // 3
     half = width // 2
 
-    def body(sc, mine_ref, their_ref, ns_ref, east_ref, west_ref, side_ref):
+    def body(sc, mine_ref, their_ref, ns_ref, near_ref, far_ref, side_ref):
         place = sc[0]
         lane = lane_index((size, LANES))
 
@@ -226,7 +251,7 @@
             spread = jnp.concatenate([upper, under], axis=0)
             spread = jnp.where(spread, 1.0, 0.0).astype(BF16)
             side_ref[side] = jnp.dot(both, spread, preferred_element_type=F32).astype(BF16)
-        for k, out in enumerate((ns_ref, east_ref, west_ref)):
+        for k, out in enumerate((ns_ref, near_ref, far_ref)):
             reverse = sc[2 + 2 * k]
             hit = jnp.where(reverse == 1, width - 1 - row, row) == column
             order = jnp.where(hit & (column < width), 1.0, 0.0).astype(BF16)
@@ -237,36 +262,41 @@
     return call(body, (scalars, pack, partner), outs, [pltpu.VMEM((4, size, LANES), BF16)])
 
 
+def west_east(scalars, near_ref, far_ref):
+    near, far = near_ref[...], far_ref[...]
+    odd = scalars[7] == 1
+    return jnp.where(odd, near, far), jnp.where(odd, far, near)
+
+
 def above_below(place, facing, inner):
     return jnp.where(place == 0, facing, inner), jnp.where(place == 0, inner, facing)
 
 
-def first_stage(scalars, image, partner, ns, east, west, weight, bias):
+def first_stage(scalars, image, partner, ns, near, far, weight, bias):
     block_rows, channels, width = image.shape
     outputs = weight.shape[0]
 
-    def body(sc, image_ref, partner_ref, ns_ref, east_ref, west_ref, weight_ref, bias_ref, raw_ref, pack_ref, stat_ref, taps):
+    def body(sc, image_ref, partner_ref, ns_ref, near_ref, far_ref, weight_ref, bias_ref, raw_ref, pack_ref, stat_ref, taps):
         place = sc[0]
         upper, lower = above_below(place, ns_ref[...], partner_ref[pl.ds(channels, channels)])
-        frame_rows(
-            taps, 0, channels, width, block_rows, lambda r: image_ref[r], upper, lower, west_ref[...], east_ref[...], place
-        )
+        west, east = west_east(sc, near_ref, far_ref)
+        frame_rows(taps, 0, channels, width, block_rows, lambda r: image_ref[r], upper, lower, west, east, place)
         finish(taps, weight_ref, raw_ref, pack_ref, stat_ref, (bias_ref, 0), block_rows, outputs, width, 1, place)
 
     return call(
         body,
-        (scalars, image, partner, ns, east, west, weight, bias),
+        (scalars, image, partner, ns, near, far, weight, bias),
         [((block_rows, outputs, LANES), BF16), ((3 * outputs, LANES), BF16), ((DEVICES, LANES), F32)],
         [pltpu.VMEM((block_rows + 2, 3 * channels, LANES), BF16)],
     )
 
 
-def plain_stage(scalars, raw, stats, partner, ns, east, west, weight, gain, shift, line, bias, first, width, depth):
+def plain_stage(scalars, raw, stats, partner, ns, near, far, weight, gain, shift, line, bias, first, width, depth):
     block_rows, channels, _ = raw.shape
     outputs = weight.shape[0]
     biased = bias is not None
 
-    def body(sc, raw_in, stats_ref, partner_ref, ns_ref, east_ref, west_ref, weight_ref, gain_ref, shift_ref, *rest):
+    def body(sc, raw_in, stats_ref, partner_ref, ns_ref, near_ref, far_ref, weight_ref, gain_ref, shift_ref, *rest):
         bias_row = None
         if biased:
             bias_row, rest = (rest[0], first), rest[1:]
@@ -282,10 +312,11 @@
         lane = lane_index((channels, LANES))
         clear = jnp.zeros((channels, LANES), BF16)
 
-        def strip(ref):
-            return jnp.where(lane < width, activate(ref[...], coef), clear)
-
-        upper, lower = above_below(place, strip(ns_ref), activate(partner_ref[pl.ds(channels, channels)], coef))
+        def strip(value):
+            return jnp.where(lane < width, activate(value, coef), clear)
+
+        west, east = west_east(sc, near_ref, far_ref)
+        upper, lower = above_below(place, strip(ns_ref[...]), activate(partner_ref[pl.ds(channels, channels)], coef))
         frame_rows(
             taps,
             0,
@@ -295,8 +326,8 @@
             lambda r: activate(raw_in[r], coef),
             upper,
             lower,
-            strip(west_ref),
-            strip(east_ref),
+            strip(west),
+            strip(east),
             place,
         )
         finish(taps, weight_ref, raw_ref, pack_ref, stat_ref, None, block_rows, outputs, width, depth, place)
@@ -304,19 +335,19 @@
     outs = [((block_rows, outputs, LANES), BF16), ((DEVICES, LANES), F32)]
     if depth:
         outs.append(((3 * depth * outputs, LANES), BF16))
-    operands = (scalars, raw, stats, partner, ns, east, west, weight, gain, shift)
+    operands = (scalars, raw, stats, partner, ns, near, far, weight, gain, shift)
     if biased:
         operands += (bias,)
     return call(body, operands, outs, [pltpu.VMEM((block_rows + 2, 3 * channels, LANES), BF16)])
 
 
-def pool_stage(scalars, raw, stats, partner, ns, east, west, weight, gain, shift, bias):
+def pool_stage(scalars, raw, stats, partner, ns, near, far, weight, gain, shift, bias):
     block_rows, channels, width = raw.shape
     low_rows, low_width = block_rows // 2, width // 2
     outputs = weight.shape[0]
 
     def body(
-        sc, raw_in, stats_ref, partner_ref, ns_ref, east_ref, west_ref, weight_ref, gain_ref, shift_ref, bias_ref,
+        sc, raw_in, stats_ref, partner_ref, ns_ref, near_ref, far_ref, weight_ref, gain_ref, shift_ref, bias_ref,
         skip_ref, side_ref, raw_ref, pack_ref, stat_ref, taps, pooled,
     ):
         place = sc[0]
@@ -329,11 +360,12 @@
             both = jnp.concatenate([outer, second], axis=1)
             return jnp.dot(both, gather, preferred_element_type=F32).astype(BF16)
 
-        def lines(ref, first):
-            return activate(ref[pl.ds(first, channels)], coef), activate(ref[pl.ds(first + channels, channels)], coef)
-
-        ns_lines, east_lines, west_lines = lines(ns_ref, 0), lines(east_ref, 0), lines(west_ref, 0)
-        inner_lines = lines(partner_ref, 2 * channels)
+        def lines(value):
+            return activate(value[:channels], coef), activate(value[channels:], coef)
+
+        west, east = west_east(sc, near_ref, far_ref)
+        ns_lines, east_lines, west_lines = lines(ns_ref[...]), lines(east), lines(west)
+        inner_lines = lines(partner_ref[pl.ds(2 * channels, 2 * channels)])
         upper, lower = above_below(place, ns_lines[0], inner_lines[0])
         side_ref[0] = upper
         side_ref[1] = lower
@@ -341,8 +373,8 @@
         side_ref[3] = east_lines[0]
 
         def make(step, carry):
-            for k in range(2):
-                row = step * 2 + k
+            for k in range(8):
+                row = step * 8 + k
                 first = activate(raw_in[2 * row], coef)
                 second = activate(raw_in[2 * row + 1], coef)
                 skip_ref[2 * row] = first
@@ -350,7 +382,7 @@
                 pooled[row] = pool(first, second)
             return carry
 
-        lax.fori_loop(0, low_rows // 2, make, 0)
+        lax.fori_loop(0, low_rows // 8, make, 0)
         upper, lower = above_below(place, pool(*ns_lines), pool(*inner_lines))
         frame_rows(
             taps,
@@ -369,7 +401,7 @@
 
     return call(
         body,
-        (scalars, raw, stats, partner, ns, east, west, weight, gain, shift, bias),
+        (scalars, raw, stats, partner, ns, near, far, weight, gain, shift, bias),
         [
             ((block_rows, channels, LANES), BF16),
             ((4, channels, LANES), BF16),
@@ -381,16 +413,15 @@
     )
 
 
-def decode_stage(scalars, raw, stats, partner, ns, east, west, skip, sides, weight, gain, shift):
+def decode_stage(scalars, raw, stats, partner, ns, near, far, skip, sides, deep_weight, skip_weight, gain, shift):
     low_rows, channels, _ = raw.shape
     block_rows, skip_channels, width = skip.shape
     low_width = width // 2
-    joined = channels + skip_channels
-    outputs = weight.shape[0]
+    outputs = skip_weight.shape[0]
 
     def body(
-        sc, raw_in, stats_ref, partner_ref, ns_ref, east_ref, west_ref, skip_ref, side_ref, weight_ref, gain_ref, shift_ref,
-        raw_ref, pack_ref, stat_ref, taps, wide,
+        sc, raw_in, stats_ref, partner_ref, ns_ref, near_ref, far_ref, skip_ref, side_ref, deep_ref, weight_ref, gain_ref,
+        shift_ref, raw_ref, pack_ref, stat_ref, deep_taps, skip_taps, wide,
     ):
         place = sc[0]
         coef = coefficients(
@@ -402,35 +433,26 @@
 
         lane = lane_index((channels, LANES))
 
+        def kept(value):
+            return jnp.where(lane < low_width, activate(value, coef), jnp.zeros((channels, LANES), BF16))
+
         def widen(value):
-            kept = jnp.where(lane < low_width, activate(value, coef), jnp.zeros((channels, LANES), BF16))
-            return jnp.dot(kept, spread, preferred_element_type=F32).astype(BF16)
+            return jnp.dot(kept(value), spread, preferred_element_type=F32).astype(BF16)
 
         def make(step, carry):
-            for k in range(4):
-                row = step * 4 + k
-                wide[row] = widen(raw_in[row])
+            for k in range(8):
+                wide[step * 8 + k] = widen(raw_in[step * 8 + k])
             return carry
 
-        lax.fori_loop(0, low_rows // 4, make, 0)
+        lax.fori_loop(0, low_rows // 8, make, 0)
+        west, east = west_east(sc, near_ref, far_ref)
         upper, lower = above_below(place, widen(ns_ref[...]), widen(partner_ref[pl.ds(channels, channels)]))
         frame_rows(
-            taps,
-            0,
-            channels,
-            width,
-            block_rows,
-            lambda r: wide[r >> 1],
-            upper,
-            lower,
-            widen(west_ref[...]),
-            widen(east_ref[...]),
-            place,
-            2,
+            deep_taps, 0, channels, width, low_rows, lambda r: wide[r], upper, lower, kept(west), kept(east), place
         )
         frame_rows(
-            taps,
-            channels,
+            skip_taps,
+            0,
             skip_channels,
             width,
             block_rows,
@@ -441,14 +463,47 @@
             side_ref[3],
             place,
         )
-        finish(taps, weight_ref, raw_ref, pack_ref, stat_ref, None, block_rows, outputs, width, 1, place)
+        deep_weights, skip_weights = deep_ref[...], weight_ref[...]
+        zero = jnp.zeros((outputs, LANES), F32)
+        together = 4
+
+        def convolve(step, carry):
+            sums, squares = carry
+            for k in range(0, together, 2):
+                low = step * together + k
+                window = jnp.concatenate(
+                    [deep_taps[pl.ds(low + j, 3)].reshape(9 * channels, LANES) for j in range(2)], axis=1
+                )
+                deep = jnp.dot(deep_weights, window, preferred_element_type=F32)
+                for j in range(2):
+                    high = 2 * (low + j)
+                    window = jnp.concatenate(
+                        [skip_taps[pl.ds(high + i, 3)].reshape(9 * skip_channels, LANES) for i in range(2)], axis=1
+                    )
+                    both = jnp.dot(skip_weights, window, preferred_element_type=F32)
+                    for i in range(2):
+                        value = both[:, i * LANES : (i + 1) * LANES]
+                        value = value + deep[i * outputs : (i + 1) * outputs, j * LANES : (j + 1) * LANES]
+                        raw_ref[high + i] = value.astype(BF16)
+                        sums = sums + value
+                        squares = squares + value * value
+            return sums, squares
+
+        sums, squares = lax.fori_loop(0, low_rows // together, convolve, (zero, zero))
+        stat = group_stats(sums, squares, None, outputs, float(block_rows * width), width)
+        stat_ref[...] = jnp.broadcast_to(stat, stat_ref.shape)
+        pack_edges(raw_ref, pack_ref, block_rows, outputs, width, 1, place)
 
     return call(
         body,
-        (scalars, raw, stats, partner, ns, east, west, skip, sides, weight, gain, shift),
+        (scalars, raw, stats, partner, ns, near, far, skip, sides, deep_weight, skip_weight, gain, shift),
         [((block_rows, outputs, LANES), BF16), ((3 * outputs, LANES), BF16), ((DEVICES, LANES), F32)],
-        [pltpu.VMEM((block_rows + 2, 3 * joined, LANES), BF16), pltpu.VMEM((low_rows, channels, LANES), BF16)],
-        20,
+        [
+            pltpu.VMEM((low_rows + 2, 3 * channels, LANES), BF16),
+            pltpu.VMEM((block_rows + 2, 3 * skip_channels, LANES), BF16),
+            pltpu.VMEM((low_rows, channels, LANES), BF16),
+        ],
+        16,
     )
 
 
@@ -460,22 +515,17 @@
         project = weight_ref[...]
 
         def make(step, carry):
-            for k in range(0, 4, 2):
-                row = step * 4 + k
+            for k in range(0, 16, 2):
+                row = step * 16 + k
                 both = jnp.concatenate([activate(raw_in[row], coef), activate(raw_in[row + 1], coef)], axis=1)
                 result = jnp.dot(project, both, preferred_element_type=F32).astype(BF16)
                 out_ref[row] = result[:kept, :LANES]
                 out_ref[row + 1] = result[:kept, LANES:]
             return carry
 
-        lax.fori_loop(0, block_rows // 4, make, 0)
+        lax.fori_loop(0, block_rows // 16, make, 0)
 
     return call(body, (scalars, raw, stats, weight, gain, shift), [((block_rows, kept, LANES), BF16)])[0]
-
-
-def shift_tiles(value, steps):
-    count = lax.axis_size(TILE)
-    return lax.ppermute(value, TILE, [(t, (t + steps) % count) for t in range(count)])
 
 
 def vertical(value):
@@ -489,11 +539,12 @@
 
 def exchange(scalars, pack, width):
     partner = lax.ppermute(pack, "split", [(0, 1), (1, 0)])
-    ns, east, west = strips(scalars, pack, partner, width)
-    west = shift_tiles(west, 1)
-    east = shift_tiles(east, -1)
+    ns, near, far = strips(scalars, pack, partner, width)
+    count = lax.axis_size(TILE)
+    far = lax.ppermute(far, TILE, [(t, (t - 1 + 2 * (t % 2)) % count) for t in range(count)])
+    near = lax.ppermute(near, TILE, [(t, t + 1 - 2 * (t % 2)) for t in range(count)])
     ns = vertical(ns)
-    return partner, ns, east, west
+    return partner, ns, near, far
 
 
 def share(stat):
@@ -522,21 +573,13 @@
     return jnp.transpose(kernel, (2, 0, 1, 3)).reshape(kernel.shape[2], -1)
 
 
-def seam_scalars(seam_codes):
-    count = lax.axis_size(TILE)
-    tile, place = lax.axis_index(TILE), lax.axis_index("split")
-
-    def facing(target, side):
-        k = (side + 2 + seam_codes[target % count, side]) % 4
-        reverse = (k < 2) == (side < 2)
-        return k, reverse.astype(jnp.int32)
-
-    north = facing(tile + ROW_TILES, 0)
-    south = facing(tile - ROW_TILES, 2)
-    up = place == 0
-    vertical_pick = (jnp.where(up, north[0], south[0]), jnp.where(up, north[1], south[1]))
-    picks = vertical_pick + facing(tile - 1, 1) + facing(tile + 1, 3)
-    return jnp.stack([place] + [p.astype(jnp.int32) for p in picks])
+def deep_kernel(kernel):
+    wide = kernel.astype(F32)
+    none = jnp.zeros_like(wide[0])
+    even = jnp.stack([wide[0], wide[1] + wide[2], none])
+    odd = jnp.stack([none, wide[0] + wide[1], wide[2]])
+    both = jnp.stack([even, odd]).astype(BF16)
+    return jnp.transpose(both, (0, 3, 1, 2, 4)).reshape(2 * kernel.shape[2], -1)
 
 
 def per_device(
@@ -558,7 +601,7 @@
     gains_lower,
     shifts_lower,
 ):
-    scalars = seam_scalars(seam_codes)
+    here = jnp.stack([lax.axis_index(TILE), lax.axis_index("split")]).astype(jnp.int32)
     biases = embedding(timestep, time_weight, bias_upper, bias_lower)
     channels, _, width = noisy_image.shape[1:]
     padding = kernel_upper_first.shape[2] - channels
@@ -567,7 +610,7 @@
     low_width = width // 2
     width_one = kernel_upper_first.shape[2]
 
-    pack = edges_of_image(scalars, image)
+    pack, scalars = edges_of_image(here, image, seam_codes)
     _, received = meet(scalars, pack, None, width)
     raw, pack, stat = first_stage(scalars, image, *received, upper_first, biases)
 
@@ -589,7 +632,8 @@
 
     stats, received = meet(scalars, pack, stat, low_width)
     raw, pack, stat = decode_stage(
-        scalars, raw, stats, *received, skip, sides, flat_kernel(kernel_decode_first), gains_lower, shifts_lower
+        scalars, raw, stats, *received, skip, sides, deep_kernel(kernel_decode_first[..., :-width_one]),
+        flat_kernel(kernel_decode_first[..., -width_one:]), gains_lower, shifts_lower,
     )
 
     stats, received = meet(scalars, pack, stat, width)

time: 214 us -> 186 us (0.87)
  Pallas kernels: 61.6 us -> 41.7 us
  waiting for transfers between devices: 38.3 us -> 35.8 us
  between operations: 3.52 us -> 1.05 us
    pallas_call x14 -> x13, Pallas kernels: 61.6 us -> 39.6 us  [call(): pl.pallas_call(body, in_specs=[SCALARS] + [WHOLE] * (len(operands) - 1),...]
    all_to_all x6, starting transfers between devices: 60 us -> 56 us  [share(): return lax.all_to_all(copies, TILE_SPLIT, 0, 0).reshape(DEVICES, LANES)]
    pallas_call x0 -> x1, Pallas kernels: none -> 2.17 us  [edges_of_image(): pl.pallas_call(body, in_specs=[SCALARS, SCALARS, WHOLE], out_specs=[WHOLE...]
    ppermute x12, waiting for transfers between devices: 2.18 us -> 0.03 us  [the longest x6 0.02 us: exchange(): lax.ppermute(near, TILE, [(t, t + 1 - 2 * (t % 2)) for t in range(count)])]
  transfers between devices with their start and end apart: 30 -> 30, of which waited for: 12 -> 9; matrix products, arithmetic and copies ran while one was open for 1% -> 1% of each run, Pallas kernels for 2% -> 2%
where the time goes in v2:
time: 186 us
  starting transfers between devices  100 us (54%)
  Pallas kernels  41.7 us (22%)
  waiting for transfers between devices  35.8 us (19%)
  local copies, waits for them, and re-layouts  6.47 us (3%)
    all_to_all x6, starting transfers between devices, share(): return lax.all_to_all(copies, TILE_SPLIT, 0, 0).reshape(DEVICES, LANES)  56 us
    pallas_call x13, Pallas kernels, call(): pl.pallas_call(body, in_specs=[SCALARS] + [WHOLE] * (len(operands) - 1),...  39.6 us
    all_to_all x6, waiting for transfers between devices, share(): return lax.all_to_all(copies, TILE_SPLIT, 0, 0).reshape(DEVICES, LANES)  25.3 us
    ppermute x6, starting transfers between devices, exchange(): partner = lax.ppermute(pack, 'split', [(0, 1), (1, 0)])  20.8 us
    ppermute x6, starting transfers between devices, vertical(): return lax.ppermute(value, TILE_SPLIT, pairs)  9.47 us
    ppermute x6, starting transfers between devices, exchange(): lax.ppermute(near, TILE, [(t, t + 1 - 2 * (t % 2)) for t in range(count)])  7.19 us
    ppermute x6, waiting for transfers between devices, vertical(): return lax.ppermute(value, TILE_SPLIT, pairs)  6.81 us
    ppermute x6, starting transfers between devices, exchange(): lax.ppermute(far, TILE, [(t, (t - 1 + 2 * (t % 2)) % count) for t in rang...  6.6 us
  transfers between devices with their start and end apart: 30, of which 9 were waited for; matrix products, arithmetic and copies ran while one was open for 1% of the time, Pallas kernels for 2%

profile of v2, /device:TPU:1, one launch (start us, length us, event | category | flops | bytes accessed | tf_op | source)
XLA Modules:
  0.0 185.9 jit_solution(2173485674533486302)
XLA Ops:
  0.0 1.6 copy.60
  1.7 0.6 copy-done.14
  2.5 2.2 %shard_map.163 = (bf16[144,128]{1,0:T(8,128)(2,1)S(1)}, s32[8]{0:T(128)S(1)}) custom-call(s32[2]{0:T(128)S(1)} %pad_add_fusion.here_ref, s32[64,4]{1,0:T(8,128)S(1)} %copy.42.codes, bf16[64,48,128]{2,1,0:T(8,128)(2,1)S(1)} %pad_bitcast_fusion.image_ref), custom_call_target="tpu_custom_call" | custom-call | tf_op jit(solution)/shard_map/pallas_call | solution.py:216
  4.7 3.8 %collective-permute-start = (bf16[144,128]{1,0:T(8,128)(2,1)S(1)}, bf16[144,128]{1,0:T(8,128)(2,1)S(1)}, u32[]{:S(2)}, u32[]{:S(2)}) collective-permute-start(bf16[144,128]{1,0:T(8,128)(2,1)S(1)} %get-tuple-element.45.mine_ref), channel_id=1, source_target_pairs={{0,1},{1,0},{2,3},{3,2},{4,5},{5,4},{6,7},{7,6},{8,9},{9,8},{10,11... | collective-permute-start | bytes 110600 | tf_op jit(solution)/shard_map/ppermute | solution.py:541
  9.2 0.2 fusion.4
  9.5 0.6 copy-done.11
  10.1 0.3 fusion.bias_ref.rest_0_
  10.4 0.9 shard_map.164
  11.2 1.7 collective-permute-start.1
  12.9 1.6 collective-permute-start.2
  14.5 1.2 collective-permute-start.3
  15.9 2.4 %collective-permute-done.1.ns_ref = bf16[48,128]{1,0:T(8,128)(2,1)S(1)} collective-permute-done((bf16[48,128]{1,0:T(8,128)(2,1)S(1)}, bf16[48,128]{1,0:T(8,128)(2,1)S(1)}, u32[]{:S(2)}, u32[]{:S(2)}) %collective-permute-start.1) | collective-permute-done | bytes 12320 | tf_op jit(solution)/shard_map/ppermute | solution.py:537
  18.3 4.8 %shard_map.165 = (bf16[64,48,128]{2,1,0:T(8,128)(2,1)S(1)}, bf16[144,128]{1,0:T(8,128)(2,1)S(1)}, f32[128,128]{1,0:T(8,128)}) custom-call(s32[8]{0:T(128)S(1)} %get-tuple-element.44.sc, bf16[64,48,128]{2,1,0:T(8,128)(2,1)S(1)} %pad_bitcast_fusion.image_ref, bf16[144,128]{1,0:T(8,128)(2,1)S(1)} %collective-permute-done.their_ref.partner_ref, ...), custom_call_target="tpu_custom_call" | custom-call | tf_op jit(solution)/shard_map/pallas_call | solution.py:184
  23.1 11.9 %all-to-all-start = ((f32[128,1,128]{2,1,0:T(1,128)}), f32[128,1,128]{2,1,0:T(1,128)S(1)}, u32[]{:S(2)}, u32[]{:S(2)}) async-start(f32[128,1,128]{2,1,0:T(1,128)} %bitcast.11), calls=%async_computation | async-start | bytes 131072 | tf_op jit(solution)/shard_map/all_to_all | solution.py:552
  35.1 2.9 %collective-permute-start.4 = (bf16[144,128]{1,0:T(8,128)(2,1)S(1)}, bf16[144,128]{1,0:T(8,128)(2,1)S(1)}, u32[]{:S(2)}, u32[]{:S(2)}) collective-permute-start(bf16[144,128]{1,0:T(8,128)(2,1)S(1)} %get-tuple-element.51.mine_ref), channel_id=1, source_target_pairs={{0,1},{1,0},{2,3},{3,2},{4,5},{5,4},{6,7},{7,6},{8,9},{9,8},{10,11... | collective-permute-start | bytes 110600 | tf_op jit(solution)/shard_map/ppermute | solution.py:541
  38.0 1.8 collective-permute-done.4.their_ref.partner_ref
  39.8 0.8 shard_map.166
  40.7 1.5 collective-permute-start.5
  42.2 1.5 collective-permute-start.6
  43.7 1.3 collective-permute-start.7
  45.2 2.2 %collective-permute-done.5.ns_ref = bf16[48,128]{1,0:T(8,128)(2,1)S(1)} collective-permute-done((bf16[48,128]{1,0:T(8,128)(2,1)S(1)}, bf16[48,128]{1,0:T(8,128)(2,1)S(1)}, u32[]{:S(2)}, u32[]{:S(2)}) %collective-permute-start.5) | collective-permute-done | bytes 12320 | tf_op jit(solution)/shard_map/ppermute | solution.py:537
  47.4 5.4 %shard_map.167 = (bf16[64,48,128]{2,1,0:T(8,128)(2,1)S(1)}, f32[128,128]{1,0:T(8,128)}, bf16[288,128]{1,0:T(8,128)(2,1)S(1)}) custom-call(s32[8]{0:T(128)S(1)} %get-tuple-element.44.sc, bf16[64,48,128]{2,1,0:T(8,128)(2,1)S(1)} %get-tuple-element.49.raw_in, f32[128,128]{1,0:T(8,128)S(1)} %bitcast.63, ...), custom_call_target="tpu_custom_call" | custom-call | tf_op jit(solution)/shard_map/pallas_call | solution.py:184
  52.8 6.1 %collective-permute-start.8 = (bf16[288,128]{1,0:T(8,128)(2,1)S(1)}, bf16[288,128]{1,0:T(8,128)(2,1)S(1)}, u32[]{:S(2)}, u32[]{:S(2)}) collective-permute-start(bf16[288,128]{1,0:T(8,128)(2,1)S(1)} %get-tuple-element.57.mine_ref), channel_id=1, source_target_pairs={{0,1},{1,0},{2,3},{3,2},{4,5},{5,4},{6,7},{7,6},{8,9},{9,8},{10,11... | collective-permute-start | bytes 221192 | tf_op jit(solution)/shard_map/ppermute | solution.py:541
  59.0 7.9 %all-to-all-start.1 = ((f32[128,1,128]{2,1,0:T(1,128)}), f32[128,1,128]{2,1,0:T(1,128)S(1)}, u32[]{:S(2)}, u32[]{:S(2)}) async-start(f32[128,1,128]{2,1,0:T(1,128)} %bitcast.15), calls=%async_computation.1 | async-start | bytes 131072 | tf_op jit(solution)/shard_map/all_to_all | solution.py:552
  66.9 0.9 shard_map.168
  67.8 1.3 collective-permute-start.10
  69.0 0.6 collective-permute-start.11
  69.6 1.5 collective-permute-start.9
  71.3 5.5 %all-to-all-done.1 = f32[128,1,128]{2,1,0:T(1,128)S(1)} async-done(((f32[128,1,128]{2,1,0:T(1,128)}), f32[128,1,128]{2,1,0:T(1,128)S(1)}, u32[]{:S(2)}, u32[]{:S(2)}) %all-to-all-start.1) | async-done | bytes 65568 | tf_op jit(solution)/shard_map/all_to_all | solution.py:552
  76.8 4.6 %shard_map.169 = (bf16[64,48,128]{2,1,0:T(8,128)(2,1)S(1)}, bf16[4,48,128]{2,1,0:T(8,128)(2,1)S(1)}, bf16[32,96,128]{2,1,0:T(8,128)(2,1)S(1)}, bf16[288,128]{1,0:T(8,128)(2,1)S(1)}, f32[128,128]{1,0:T(8,128)}) custom-call(s32[8]{0:T(128)S(1)} %get-tuple-element.44.sc, bf16[64,48,128]{2,1,0:T(8,128)(2,1)S(1)} %get-tuple-element.55.raw_in, ...), custom_call_target="tpu_custom_call" | custom-call | tf_op jit(solution)/shard_map/pallas_call | solution.py:184
  81.4 1.7 collective-permute-start.12
  83.1 8.2 %all-to-all-start.2 = ((f32[128,1,128]{2,1,0:T(1,128)}), f32[128,1,128]{2,1,0:T(1,128)S(1)}, u32[]{:S(2)}, u32[]{:S(2)}) async-start(f32[128,1,128]{2,1,0:T(1,128)} %bitcast.20), calls=%async_computation.2 | async-start | bytes 131072 | tf_op jit(solution)/shard_map/all_to_all | solution.py:552
  91.3 0.9 shard_map.170
  92.2 1.5 collective-permute-start.13
  93.7 0.7 collective-permute-start.14
  94.4 1.1 collective-permute-start.15
  95.6 0.2 copy.50
  95.8 0.2 copy.51.weight_ref
  95.9 5.1 %all-to-all-done.2 = f32[128,1,128]{2,1,0:T(1,128)S(1)} async-done(((f32[128,1,128]{2,1,0:T(1,128)}), f32[128,1,128]{2,1,0:T(1,128)S(1)}, u32[]{:S(2)}, u32[]{:S(2)}) %all-to-all-start.2) | async-done | bytes 65568 | tf_op jit(solution)/shard_map/all_to_all | solution.py:552
  101.1 0.7 copy-done.3
  101.8 4.6 %shard_map.171 = (bf16[32,96,128]{2,1,0:T(8,128)(2,1)S(1)}, f32[128,128]{1,0:T(8,128)}, bf16[288,128]{1,0:T(8,128)(2,1)S(1)}) custom-call(s32[8]{0:T(128)S(1)} %get-tuple-element.44.sc, bf16[32,96,128]{2,1,0:T(8,128)(2,1)S(1)} %get-tuple-element.61.raw_in, f32[128,128]{1,0:T(8,128)S(1)} %bitcast.62, ...), custom_call_target="tpu_custom_call" | custom-call | tf_op jit(solution)/shard_map/pallas_call | solution.py:184
  106.3 3.3 %collective-permute-start.16 = (bf16[288,128]{1,0:T(8,128)(2,1)S(1)}, bf16[288,128]{1,0:T(8,128)(2,1)S(1)}, u32[]{:S(2)}, u32[]{:S(2)}) collective-permute-start(bf16[288,128]{1,0:T(8,128)(2,1)S(1)} %get-tuple-element.69.mine_ref), channel_id=1, source_target_pairs={{0,1},{1,0},{2,3},{3,2},{4,5},{5,4},{6,7},{7,6},{8,9},{9,8},{10,11... | collective-permute-start | bytes 221192 | tf_op jit(solution)/shard_map/ppermute | solution.py:541
  109.7 7.9 %all-to-all-start.3 = ((f32[128,1,128]{2,1,0:T(1,128)}), f32[128,1,128]{2,1,0:T(1,128)S(1)}, u32[]{:S(2)}, u32[]{:S(2)}) async-start(f32[128,1,128]{2,1,0:T(1,128)} %bitcast.25), calls=%async_computation.3 | async-start | bytes 131072 | tf_op jit(solution)/shard_map/all_to_all | solution.py:552
  117.6 0.9 shard_map.172
  118.5 1.7 collective-permute-start.17
  120.2 0.7 collective-permute-start.18
  120.8 1.1 collective-permute-start.19
  122.2 0.2 reshape.81.deep_ref
  122.6 5.0 %all-to-all-done.3 = f32[128,1,128]{2,1,0:T(1,128)S(1)} async-done(((f32[128,1,128]{2,1,0:T(1,128)}), f32[128,1,128]{2,1,0:T(1,128)S(1)}, u32[]{:S(2)}, u32[]{:S(2)}) %all-to-all-start.3) | async-done | bytes 65568 | tf_op jit(solution)/shard_map/all_to_all | solution.py:552
  127.5 8.8 %shard_map.173 = (bf16[64,48,128]{2,1,0:T(8,128)(2,1)S(1)}, bf16[144,128]{1,0:T(8,128)(2,1)S(1)}, f32[128,128]{1,0:T(8,128)}) custom-call(s32[8]{0:T(128)S(1)} %get-tuple-element.44.sc, bf16[32,96,128]{2,1,0:T(8,128)(2,1)S(1)} %get-tuple-element.67.raw_in, f32[128,128]{1,0:T(8,128)S(1)} %bitcast.61, ...), custom_call_target="tpu_custom_call" | custom-call | tf_op jit(solution)/shard_map/pallas_call | solution.py:184
  136.3 8.6 %all-to-all-start.4 = ((f32[128,1,128]{2,1,0:T(1,128)}), f32[128,1,128]{2,1,0:T(1,128)S(1)}, u32[]{:S(2)}, u32[]{:S(2)}) async-start(f32[128,1,128]{2,1,0:T(1,128)} %bitcast.32), calls=%async_computation.4 | async-start | bytes 131072 | tf_op jit(solution)/shard_map/all_to_all | solution.py:552
  145.0 2.9 %collective-permute-start.20 = (bf16[144,128]{1,0:T(8,128)(2,1)S(1)}, bf16[144,128]{1,0:T(8,128)(2,1)S(1)}, u32[]{:S(2)}, u32[]{:S(2)}) collective-permute-start(bf16[144,128]{1,0:T(8,128)(2,1)S(1)} %get-tuple-element.77.mine_ref), channel_id=1, source_target_pairs={{0,1},{1,0},{2,3},{3,2},{4,5},{5,4},{6,7},{7,6},{8,9},{9,8},{10,11... | collective-permute-start | bytes 110600 | tf_op jit(solution)/shard_map/ppermute | solution.py:541
  147.9 1.8 collective-permute-done.20.their_ref.partner_ref
  149.8 0.8 shard_map.174
  150.6 1.5 collective-permute-start.21
  152.2 1.5 collective-permute-start.22
  153.7 1.3 collective-permute-start.23
  155.0 0.1 reshape.85.weight_ref
  155.1 2.2 %collective-permute-done.21.ns_ref = bf16[48,128]{1,0:T(8,128)(2,1)S(1)} collective-permute-done((bf16[48,128]{1,0:T(8,128)(2,1)S(1)}, bf16[48,128]{1,0:T(8,128)(2,1)S(1)}, u32[]{:S(2)}, u32[]{:S(2)}) %collective-permute-start.21) | collective-permute-done | bytes 12320 | tf_op jit(solution)/shard_map/ppermute | solution.py:537
  157.3 4.5 %shard_map.175 = (bf16[64,48,128]{2,1,0:T(8,128)(2,1)S(1)}, f32[128,128]{1,0:T(8,128)}) custom-call(s32[8]{0:T(128)S(1)} %get-tuple-element.44.sc, bf16[64,48,128]{2,1,0:T(8,128)(2,1)S(1)} %get-tuple-element.75.raw_in, f32[128,128]{1,0:T(8,128)S(1)} %bitcast.64, bf16[144,128]{1,0:T(8,128)(2,1)S(1)} %collective-permute-done.20.their_ref.partner_ref, ...), custom_call_target="tpu_custom_call" | custom-call | tf_op jit(solution)/shard_map/pallas_call | solution.py:184
  161.9 11.5 %all-to-all-start.5 = ((f32[128,1,128]{2,1,0:T(1,128)}), f32[128,1,128]{2,1,0:T(1,128)S(1)}, u32[]{:S(2)}, u32[]{:S(2)}) async-start(f32[128,1,128]{2,1,0:T(1,128)} %bitcast.36), calls=%async_computation.5 | async-start | bytes 131072 | tf_op jit(solution)/shard_map/all_to_all | solution.py:552
  173.4 9.7 %all-to-all-done.5 = f32[128,1,128]{2,1,0:T(1,128)S(1)} async-done(((f32[128,1,128]{2,1,0:T(1,128)}), f32[128,1,128]{2,1,0:T(1,128)S(1)}, u32[]{:S(2)}, u32[]{:S(2)}) %all-to-all-start.5) | async-done | bytes 65568 | tf_op jit(solution)/shard_map/all_to_all | solution.py:552
  183.1 1.7 shard_map.176
  184.8 1.1 copy.58
  (72 shorter events, 1.7 us)
Async XLA Ops:
  0.0 9.2 %copy-start = (f32[48,192]{1,0:T(8,128)S(1)}, f32[48,192]{1,0:T(8,128)}, u32[]{:S(2)}) copy-start(f32[48,192]{1,0:T(8,128)} %param.20) | copy-start | bytes 110596
  1.6 0.7 copy-start.14
  4.6 4.8 %copy-start.12 = (f32[192,48]{0,1:T(8,128)S(1)}, f32[192,48]{0,1:T(8,128)}, u32[]{:S(2)}) copy-start(f32[192,48]{0,1:T(8,128)} %param.21) | copy-start | bytes 110596
  4.7 5.7 %collective-permute-start = (bf16[144,128]{1,0:T(8,128)(2,1)S(1)}, bf16[144,128]{1,0:T(8,128)(2,1)S(1)}, u32[]{:S(2)}, u32[]{:S(2)}) collective-permute-start(bf16[144,128]{1,0:T(8,128)(2,1)S(1)} %get-tuple-element.45.mine_ref), channel_id=1, source_target_pairs={{0,1},{1,0},{2,3},{3,2},{4,5},{5,4},{6,7},{7,6},{8,9},{9,8},{10,11... | collective-permute-start | bytes 110600 | tf_op jit(solution)/shard_map/ppermute | solution.py:541
  9.2 0.9 copy-start.11
  10.1 5.6 %copy-start.7 = (bf16[3,3,48,45]{3,2,1,0:T(8,128)(2,1)S(1)}, bf16[3,3,48,45]{3,2,1,0:T(8,128)(2,1)}, u32[]{:S(2)}) copy-start(bf16[3,3,48,45]{3,2,1,0:T(8,128)(2,1)} %param.23) | copy-start | bytes 116644
  11.2 7.1 %collective-permute-start.1 = (bf16[48,128]{1,0:T(8,128)(2,1)S(1)}, bf16[48,128]{1,0:T(8,128)(2,1)S(1)}, u32[]{:S(2)}, u32[]{:S(2)}) collective-permute-start(bf16[48,128]{1,0:T(8,128)(2,1)S(1)} %get-tuple-element.46), channel_id=1, source_target_pairs={{0,8},{1,121},{2,10},{3,123},{4,12},{5,125},{6,14},{7,127},{8,16},... | collective-permute-start | bytes 36872 | tf_op jit(solution)/shard_map/ppermute | solution.py:537
  12.9 5.4 %collective-permute-start.2 = (bf16[48,128]{1,0:T(8,128)(2,1)S(1)}, bf16[48,128]{1,0:T(8,128)(2,1)S(1)}, u32[]{:S(2)}, u32[]{:S(2)}) collective-permute-start(bf16[48,128]{1,0:T(8,128)(2,1)S(1)} %get-tuple-element.47), channel_id=1, source_target_pairs={{0,2},{2,0},{4,6},{6,4},{8,10},{10,8},{12,14},{14,12},{16,18},{18,... | collective-permute-start | bytes 36872 | tf_op jit(solution)/shard_map/ppermute | solution.py:545
  14.5 3.8 %collective-permute-start.3 = (bf16[48,128]{1,0:T(8,128)(2,1)S(1)}, bf16[48,128]{1,0:T(8,128)(2,1)S(1)}, u32[]{:S(2)}, u32[]{:S(2)}) collective-permute-start(bf16[48,128]{1,0:T(8,128)(2,1)S(1)} %get-tuple-element.48), channel_id=1, source_target_pairs={{0,126},{2,4},{4,2},{6,8},{8,6},{10,12},{12,10},{14,16},{16,14},{1... | collective-permute-start | bytes 36872 | tf_op jit(solution)/shard_map/ppermute | solution.py:544
  23.1 21.8 %copy-start.9 = (bf16[3,3,48,48]{3,2,1,0:T(8,128)(2,1)S(1)}, bf16[3,3,48,48]{3,2,1,0:T(8,128)(2,1)}, u32[]{:S(2)}) copy-start(bf16[3,3,48,48]{3,2,1,0:T(8,128)(2,1)} %param.24) | copy-start | bytes 124420
  23.1 24.2 %all-to-all-start = ((f32[128,1,128]{2,1,0:T(1,128)}), f32[128,1,128]{2,1,0:T(1,128)S(1)}, u32[]{:S(2)}, u32[]{:S(2)}) async-start(f32[128,1,128]{2,1,0:T(1,128)} %bitcast.11), calls=%async_computation | async-start | bytes 131072 | tf_op jit(solution)/shard_map/all_to_all | solution.py:552
  35.1 4.8 %collective-permute-start.4 = (bf16[144,128]{1,0:T(8,128)(2,1)S(1)}, bf16[144,128]{1,0:T(8,128)(2,1)S(1)}, u32[]{:S(2)}, u32[]{:S(2)}) collective-permute-start(bf16[144,128]{1,0:T(8,128)(2,1)S(1)} %get-tuple-element.51.mine_ref), channel_id=1, source_target_pairs={{0,1},{1,0},{2,3},{3,2},{4,5},{5,4},{6,7},{7,6},{8,9},{9,8},{10,11... | collective-permute-start | bytes 110600 | tf_op jit(solution)/shard_map/ppermute | solution.py:541
  40.7 6.7 %collective-permute-start.5 = (bf16[48,128]{1,0:T(8,128)(2,1)S(1)}, bf16[48,128]{1,0:T(8,128)(2,1)S(1)}, u32[]{:S(2)}, u32[]{:S(2)}) collective-permute-start(bf16[48,128]{1,0:T(8,128)(2,1)S(1)} %get-tuple-element.52), channel_id=1, source_target_pairs={{0,8},{1,121},{2,10},{3,123},{4,12},{5,125},{6,14},{7,127},{8,16},... | collective-permute-start | bytes 36872 | tf_op jit(solution)/shard_map/ppermute | solution.py:537
  42.2 5.2 %collective-permute-start.6 = (bf16[48,128]{1,0:T(8,128)(2,1)S(1)}, bf16[48,128]{1,0:T(8,128)(2,1)S(1)}, u32[]{:S(2)}, u32[]{:S(2)}) collective-permute-start(bf16[48,128]{1,0:T(8,128)(2,1)S(1)} %get-tuple-element.53), channel_id=1, source_target_pairs={{0,2},{2,0},{4,6},{6,4},{8,10},{10,8},{12,14},{14,12},{16,18},{18,... | collective-permute-start | bytes 36872 | tf_op jit(solution)/shard_map/ppermute | solution.py:545
  43.7 3.7 %collective-permute-start.7 = (bf16[48,128]{1,0:T(8,128)(2,1)S(1)}, bf16[48,128]{1,0:T(8,128)(2,1)S(1)}, u32[]{:S(2)}, u32[]{:S(2)}) collective-permute-start(bf16[48,128]{1,0:T(8,128)(2,1)S(1)} %get-tuple-element.54), channel_id=1, source_target_pairs={{0,126},{2,4},{4,2},{6,8},{8,6},{10,12},{12,10},{14,16},{16,14},{1... | collective-permute-start | bytes 36872 | tf_op jit(solution)/shard_map/ppermute | solution.py:544
  45.0 2.4 %copy-start.2 = (f32[4,48]{1,0:T(4,128)S(1)}, f32[4,48]{1,0:T(4,128)}, u32[]{:S(2)}) copy-start(f32[4,48]{1,0:T(4,128)} %shift_ref.11) | copy-start | bytes 2308
  45.2 2.2 %copy-start.1 = (f32[4,48]{1,0:T(4,128)S(1)}, f32[4,48]{1,0:T(4,128)}, u32[]{:S(2)}) copy-start(f32[4,48]{1,0:T(4,128)} %gain_ref.11) | copy-start | bytes 2308
  47.4 11.5 %copy-start.6 = (bf16[3,3,48,144]{3,2,1,0:T(8,128)(2,1)S(1)}, bf16[3,3,48,144]{3,2,1,0:T(8,128)(2,1)}, u32[]{:S(2)}) copy-start(bf16[3,3,48,144]{3,2,1,0:T(8,128)(2,1)} %param.27) | copy-start | bytes 373252
  52.8 14.0 %collective-permute-start.8 = (bf16[288,128]{1,0:T(8,128)(2,1)S(1)}, bf16[288,128]{1,0:T(8,128)(2,1)S(1)}, u32[]{:S(2)}, u32[]{:S(2)}) collective-permute-start(bf16[288,128]{1,0:T(8,128)(2,1)S(1)} %get-tuple-element.57.mine_ref), channel_id=1, source_target_pairs={{0,1},{1,0},{2,3},{3,2},{4,5},{5,4},{6,7},{7,6},{8,9},{9,8},{10,11... | collective-permute-start | bytes 221192 | tf_op jit(solution)/shard_map/ppermute | solution.py:541
  59.0 17.8 %all-to-all-start.1 = ((f32[128,1,128]{2,1,0:T(1,128)}), f32[128,1,128]{2,1,0:T(1,128)S(1)}, u32[]{:S(2)}, u32[]{:S(2)}) async-start(f32[128,1,128]{2,1,0:T(1,128)} %bitcast.15), calls=%async_computation.1 | async-start | bytes 131072 | tf_op jit(solution)/shard_map/all_to_all | solution.py:552
  67.8 9.0 %collective-permute-start.10 = (bf16[96,128]{1,0:T(8,128)(2,1)S(1)}, bf16[96,128]{1,0:T(8,128)(2,1)S(1)}, u32[]{:S(2)}, u32[]{:S(2)}) collective-permute-start(bf16[96,128]{1,0:T(8,128)(2,1)S(1)} %get-tuple-element.59), channel_id=1, source_target_pairs={{0,2},{2,0},{4,6},{6,4},{8,10},{10,8},{12,14},{14,12},{16,18},{18,... | collective-permute-start | bytes 73736 | tf_op jit(solution)/shard_map/ppermute | solution.py:545
  69.0 7.8 %collective-permute-start.11 = (bf16[96,128]{1,0:T(8,128)(2,1)S(1)}, bf16[96,128]{1,0:T(8,128)(2,1)S(1)}, u32[]{:S(2)}, u32[]{:S(2)}) collective-permute-start(bf16[96,128]{1,0:T(8,128)(2,1)S(1)} %get-tuple-element.60), channel_id=1, source_target_pairs={{0,126},{2,4},{4,2},{6,8},{8,6},{10,12},{12,10},{14,16},{16,14},{1... | collective-permute-start | bytes 73736 | tf_op jit(solution)/shard_map/ppermute | solution.py:544
  69.6 1.6 copy-start.8
  69.6 7.1 %collective-permute-start.9 = (bf16[96,128]{1,0:T(8,128)(2,1)S(1)}, bf16[96,128]{1,0:T(8,128)(2,1)S(1)}, u32[]{:S(2)}, u32[]{:S(2)}) collective-permute-start(bf16[96,128]{1,0:T(8,128)(2,1)S(1)} %get-tuple-element.58), channel_id=1, source_target_pairs={{0,8},{1,121},{2,10},{3,123},{4,12},{5,125},{6,14},{7,127},{8,16},... | collective-permute-start | bytes 73736 | tf_op jit(solution)/shard_map/ppermute | solution.py:537
  81.4 9.9 %collective-permute-start.12 = (bf16[288,128]{1,0:T(8,128)(2,1)S(1)}, bf16[288,128]{1,0:T(8,128)(2,1)S(1)}, u32[]{:S(2)}, u32[]{:S(2)}) collective-permute-start(bf16[288,128]{1,0:T(8,128)(2,1)S(1)} %get-tuple-element.63.mine_ref), channel_id=1, source_target_pairs={{0,1},{1,0},{2,3},{3,2},{4,5},{5,4},{6,7},{7,6},{8,9},{9,8},{10,11... | collective-permute-start | bytes 221192 | tf_op jit(solution)/shard_map/ppermute | solution.py:541
  83.1 18.0 %all-to-all-start.2 = ((f32[128,1,128]{2,1,0:T(1,128)}), f32[128,1,128]{2,1,0:T(1,128)S(1)}, u32[]{:S(2)}, u32[]{:S(2)}) async-start(f32[128,1,128]{2,1,0:T(1,128)} %bitcast.20), calls=%async_computation.2 | async-start | bytes 131072 | tf_op jit(solution)/shard_map/all_to_all | solution.py:552
  91.3 4.3 %copy-start.5 = (bf16[3,3,96,96]{3,2,1,0:T(8,128)(2,1)S(1)}, bf16[3,3,96,96]{3,2,1,0:T(8,128)(2,1)}, u32[]{:S(2)}) copy-start(bf16[3,3,96,96]{3,2,1,0:T(8,128)(2,1)} %param.26) | copy-start | bytes 497668
  92.2 8.9 %collective-permute-start.13 = (bf16[96,128]{1,0:T(8,128)(2,1)S(1)}, bf16[96,128]{1,0:T(8,128)(2,1)S(1)}, u32[]{:S(2)}, u32[]{:S(2)}) collective-permute-start(bf16[96,128]{1,0:T(8,128)(2,1)S(1)} %get-tuple-element.64), channel_id=1, source_target_pairs={{0,8},{1,121},{2,10},{3,123},{4,12},{5,125},{6,14},{7,127},{8,16},... | collective-permute-start | bytes 73736 | tf_op jit(solution)/shard_map/ppermute | solution.py:537
  93.7 7.3 %collective-permute-start.14 = (bf16[96,128]{1,0:T(8,128)(2,1)S(1)}, bf16[96,128]{1,0:T(8,128)(2,1)S(1)}, u32[]{:S(2)}, u32[]{:S(2)}) collective-permute-start(bf16[96,128]{1,0:T(8,128)(2,1)S(1)} %get-tuple-element.65), channel_id=1, source_target_pairs={{0,2},{2,0},{4,6},{6,4},{8,10},{10,8},{12,14},{14,12},{16,18},{18,... | collective-permute-start | bytes 73736 | tf_op jit(solution)/shard_map/ppermute | solution.py:545
  94.4 6.7 %collective-permute-start.15 = (bf16[96,128]{1,0:T(8,128)(2,1)S(1)}, bf16[96,128]{1,0:T(8,128)(2,1)S(1)}, u32[]{:S(2)}, u32[]{:S(2)}) collective-permute-start(bf16[96,128]{1,0:T(8,128)(2,1)S(1)} %get-tuple-element.66), channel_id=1, source_target_pairs={{0,126},{2,4},{4,2},{6,8},{8,6},{10,12},{12,10},{14,16},{16,14},{1... | collective-permute-start | bytes 73736 | tf_op jit(solution)/shard_map/ppermute | solution.py:544
  95.7 5.3 %copy-start.4 = (f32[2,96]{1,0:T(2,128)S(1)}, f32[2,96]{1,0:T(2,128)}, u32[]{:S(2)}) copy-start(f32[2,96]{1,0:T(2,128)} %shift_ref.9) | copy-start | bytes 2308
  101.1 0.7 copy-start.3
  106.3 11.3 %collective-permute-start.16 = (bf16[288,128]{1,0:T(8,128)(2,1)S(1)}, bf16[288,128]{1,0:T(8,128)(2,1)S(1)}, u32[]{:S(2)}, u32[]{:S(2)}) collective-permute-start(bf16[288,128]{1,0:T(8,128)(2,1)S(1)} %get-tuple-element.69.mine_ref), channel_id=1, source_target_pairs={{0,1},{1,0},{2,3},{3,2},{4,5},{5,4},{6,7},{7,6},{8,9},{9,8},{10,11... | collective-permute-start | bytes 221192 | tf_op jit(solution)/shard_map/ppermute | solution.py:541
  109.7 17.8 %all-to-all-start.3 = ((f32[128,1,128]{2,1,0:T(1,128)}), f32[128,1,128]{2,1,0:T(1,128)S(1)}, u32[]{:S(2)}, u32[]{:S(2)}) async-start(f32[128,1,128]{2,1,0:T(1,128)} %bitcast.25), calls=%async_computation.3 | async-start | bytes 131072 | tf_op jit(solution)/shard_map/all_to_all | solution.py:552
  118.5 9.0 %collective-permute-start.17 = (bf16[96,128]{1,0:T(8,128)(2,1)S(1)}, bf16[96,128]{1,0:T(8,128)(2,1)S(1)}, u32[]{:S(2)}, u32[]{:S(2)}) collective-permute-start(bf16[96,128]{1,0:T(8,128)(2,1)S(1)} %get-tuple-element.70), channel_id=1, source_target_pairs={{0,8},{1,121},{2,10},{3,123},{4,12},{5,125},{6,14},{7,127},{8,16},... | collective-permute-start | bytes 73736 | tf_op jit(solution)/shard_map/ppermute | solution.py:537
  120.2 7.4 %collective-permute-start.18 = (bf16[96,128]{1,0:T(8,128)(2,1)S(1)}, bf16[96,128]{1,0:T(8,128)(2,1)S(1)}, u32[]{:S(2)}, u32[]{:S(2)}) collective-permute-start(bf16[96,128]{1,0:T(8,128)(2,1)S(1)} %get-tuple-element.71), channel_id=1, source_target_pairs={{0,2},{2,0},{4,6},{6,4},{8,10},{10,8},{12,14},{14,12},{16,18},{18,... | collective-permute-start | bytes 73736 | tf_op jit(solution)/shard_map/ppermute | solution.py:545
  120.8 6.7 %collective-permute-start.19 = (bf16[96,128]{1,0:T(8,128)(2,1)S(1)}, bf16[96,128]{1,0:T(8,128)(2,1)S(1)}, u32[]{:S(2)}, u32[]{:S(2)}) collective-permute-start(bf16[96,128]{1,0:T(8,128)(2,1)S(1)} %get-tuple-element.72), channel_id=1, source_target_pairs={{0,126},{2,4},{4,2},{6,8},{8,6},{10,12},{12,10},{14,16},{16,14},{1... | collective-permute-start | bytes 73736 | tf_op jit(solution)/shard_map/ppermute | solution.py:544
  136.3 18.6 %copy-start.10 = (bf16[3,3,48,48]{3,2,1,0:T(8,128)(2,1)S(1)}, bf16[3,3,48,48]{3,2,1,0:T(8,128)(2,1)}, u32[]{:S(2)}) copy-start(bf16[3,3,48,48]{3,2,1,0:T(8,128)(2,1)} %param.28) | copy-start | bytes 124420
  136.3 21.0 %all-to-all-start.4 = ((f32[128,1,128]{2,1,0:T(1,128)}), f32[128,1,128]{2,1,0:T(1,128)S(1)}, u32[]{:S(2)}, u32[]{:S(2)}) async-start(f32[128,1,128]{2,1,0:T(1,128)} %bitcast.32), calls=%async_computation.4 | async-start | bytes 131072 | tf_op jit(solution)/shard_map/all_to_all | solution.py:552
  145.0 4.8 %collective-permute-start.20 = (bf16[144,128]{1,0:T(8,128)(2,1)S(1)}, bf16[144,128]{1,0:T(8,128)(2,1)S(1)}, u32[]{:S(2)}, u32[]{:S(2)}) collective-permute-start(bf16[144,128]{1,0:T(8,128)(2,1)S(1)} %get-tuple-element.77.mine_ref), channel_id=1, source_target_pairs={{0,1},{1,0},{2,3},{3,2},{4,5},{5,4},{6,7},{7,6},{8,9},{9,8},{10,11... | collective-permute-start | bytes 110600 | tf_op jit(solution)/shard_map/ppermute | solution.py:541
  150.6 6.7 %collective-permute-start.21 = (bf16[48,128]{1,0:T(8,128)(2,1)S(1)}, bf16[48,128]{1,0:T(8,128)(2,1)S(1)}, u32[]{:S(2)}, u32[]{:S(2)}) collective-permute-start(bf16[48,128]{1,0:T(8,128)(2,1)S(1)} %get-tuple-element.78), channel_id=1, source_target_pairs={{0,8},{1,121},{2,10},{3,123},{4,12},{5,125},{6,14},{7,127},{8,16},... | collective-permute-start | bytes 36872 | tf_op jit(solution)/shard_map/ppermute | solution.py:537
  152.2 5.2 %collective-permute-start.22 = (bf16[48,128]{1,0:T(8,128)(2,1)S(1)}, bf16[48,128]{1,0:T(8,128)(2,1)S(1)}, u32[]{:S(2)}, u32[]{:S(2)}) collective-permute-start(bf16[48,128]{1,0:T(8,128)(2,1)S(1)} %get-tuple-element.79), channel_id=1, source_target_pairs={{0,2},{2,0},{4,6},{6,4},{8,10},{10,8},{12,14},{14,12},{16,18},{18,... | collective-permute-start | bytes 36872 | tf_op jit(solution)/shard_map/ppermute | solution.py:545
  153.7 3.7 %collective-permute-start.23 = (bf16[48,128]{1,0:T(8,128)(2,1)S(1)}, bf16[48,128]{1,0:T(8,128)(2,1)S(1)}, u32[]{:S(2)}, u32[]{:S(2)}) collective-permute-start(bf16[48,128]{1,0:T(8,128)(2,1)S(1)} %get-tuple-element.80), channel_id=1, source_target_pairs={{0,126},{2,4},{4,2},{6,8},{8,6},{10,12},{12,10},{14,16},{16,14},{1... | collective-permute-start | bytes 36872 | tf_op jit(solution)/shard_map/ppermute | solution.py:544
  161.9 11.5 %copy-start.13 = (bf16[45,48]{1,0:T(8,128)(2,1)S(1)}, bf16[45,48]{1,0:T(8,128)(2,1)}, u32[]{:S(2)}) copy-start(bf16[45,48]{1,0:T(8,128)(2,1)} %param.29) | copy-start | bytes 12964
  161.9 21.2 %all-to-all-start.5 = ((f32[128,1,128]{2,1,0:T(1,128)}), f32[128,1,128]{2,1,0:T(1,128)S(1)}, u32[]{:S(2)}, u32[]{:S(2)}) async-start(f32[128,1,128]{2,1,0:T(1,128)} %bitcast.36), calls=%async_computation.5 | async-start | bytes 131072 | tf_op jit(solution)/shard_map/all_to_all | solution.py:552

commit v3 on v2

--- a/solution.py
+++ b/solution.py
@@ -16,6 +16,7 @@
 EPSILON = 1e-05
 LANES = 128
 DEVICES = 128
+TOGETHER = 64
 F32 = jnp.float32
 BF16 = jnp.bfloat16
 
@@ -82,8 +83,9 @@
     return mean_row + jnp.sum(jnp.where(lane == group + GROUPS, total, 0.0), axis=0, keepdims=True)
 
 
-def frame_rows(taps, first, channels, width, block_rows, rows_of, upper, lower, west, east, place, together=16):
+def frame_rows(taps, first, channels, width, block_rows, rows_of, upper, lower, west, east, place):
     stride = taps.shape[1] // 3
+    together = min(block_rows, TOGETHER)
     lane = lane_index((channels, LANES))
     base = place * block_rows
 
@@ -110,8 +112,9 @@
     put(block_rows + 1, lower, jnp.where(place == 1, zero, hw), jnp.where(place == 1, zero, he))
 
 
-def convolve_rows(taps, weight_ref, raw_ref, block_rows, together=16):
+def convolve_rows(taps, weight_ref, raw_ref, block_rows):
     outputs = weight_ref.shape[0]
+    together = min(block_rows, TOGETHER)
     depth = taps.shape[1] * 3
     weight = weight_ref[...]
     zero = jnp.zeros((outputs, LANES), F32)
@@ -126,7 +129,7 @@
             both = jnp.dot(weight, window, preferred_element_type=F32)
             for j in range(2):
                 value = both[:, j * LANES : (j + 1) * LANES]
-                raw_ref[row + k + j] = value.astype(BF16)
+                raw_ref[row + k + j] = value.astype(raw_ref.dtype)
                 sums = sums + value
                 squares = squares + value * value
         return sums, squares
@@ -134,8 +137,9 @@
     return lax.fori_loop(0, block_rows // together, body, (zero, zero))
 
 
-def pack_edges(raw_ref, pack_ref, block_rows, channels, width, depth, place, together=16):
+def pack_edges(raw_ref, pack_ref, block_rows, channels, width, depth, place):
     size = depth * channels
+    together = min(block_rows, TOGETHER)
     lane = lane_index((channels, LANES))
     last = block_rows - 1
     for d in range(depth):
@@ -168,36 +172,57 @@
         pack_ref[pl.ds(2 * size + d * channels, channels)] = columns[d]
 
 
-def finish(taps, weight_ref, raw_ref, pack_ref, stat_ref, bias, block_rows, channels, width, depth, place):
+def send_stats(stat, held, stat_ref, sent):
+    held[...] = jnp.broadcast_to(stat, held.shape)
+    leave = pltpu.make_async_copy(held, stat_ref, sent)
+    leave.start()
+    return leave
+
+
+def finish(taps, weight_ref, raw_ref, pack_ref, stat_ref, held, sent, bias, block_rows, channels, width, depth, place):
     sums, squares = convolve_rows(taps, weight_ref, raw_ref, block_rows)
     stat = group_stats(sums, squares, bias, channels, float(block_rows * width), width)
-    stat_ref[...] = jnp.broadcast_to(stat, stat_ref.shape)
+    leave = send_stats(stat, held, stat_ref, sent)
     if pack_ref is not None:
         pack_edges(raw_ref, pack_ref, block_rows, channels, width, depth, place)
+    leave.wait()
 
 
 WHOLE = pl.BlockSpec(memory_space=pltpu.VMEM)
 SCALARS = pl.BlockSpec(memory_space=pltpu.SMEM)
+ANYWHERE = pl.BlockSpec(memory_space=pl.ANY)
+STATS = (pltpu.VMEM((DEVICES, LANES), F32), pltpu.SemaphoreType.DMA)
 
 
 def call(body, operands, outs, scratch=(), limit=12):
     return pl.pallas_call(
         body,
         in_specs=[SCALARS] + [WHOLE] * (len(operands) - 1),
-        out_specs=[WHOLE] * len(outs),
+        out_specs=[ANYWHERE if s == (DEVICES, LANES) else WHOLE for s, _ in outs],
         out_shape=[jax.ShapeDtypeStruct(s, d) for s, d in outs],
         scratch_shapes=list(scratch),
         compiler_params=pltpu.CompilerParams(vmem_limit_bytes=limit * 1024 * 1024),
     )(*operands)
 
 
-def edges_of_image(here, image, seam_codes):
+def edges_of_image(here, image):
     block_rows, channels, width = image.shape
+
+    def body(here_ref, image_ref, pack_ref):
+        pack_edges(image_ref, pack_ref, block_rows, channels, width, 1, here_ref[1])
+
+    return call(body, (here, image), [((3 * channels, LANES), BF16)])[0]
+
+
+def setup(here, seam_codes, tables):
     count = seam_codes.shape[0]
 
-    def body(here_ref, codes, image_ref, pack_ref, scalar_ref):
+    def body(here_ref, codes, *rest):
+        table_refs, (scalar_ref, param_ref) = rest[: len(tables)], rest[len(tables) :]
         tile, place = here_ref[0], here_ref[1]
-        pack_edges(image_ref, pack_ref, block_rows, channels, width, 1, place)
+        for k, table_ref in enumerate(table_refs):
+            lines, columns = table_ref.shape
+            param_ref[4 * k : 4 * k + lines, 0:columns] = table_ref[...]
 
         def facing(steps, side):
             k = (side + 2 + codes[(tile + count + steps) % count, side]) % 4
@@ -215,14 +240,14 @@
 
     return pl.pallas_call(
         body,
-        in_specs=[SCALARS, SCALARS, WHOLE],
-        out_specs=[WHOLE, SCALARS],
+        in_specs=[SCALARS, SCALARS] + [WHOLE] * len(tables),
+        out_specs=[SCALARS, WHOLE],
         out_shape=[
-            jax.ShapeDtypeStruct((3 * channels, LANES), BF16),
             jax.ShapeDtypeStruct((8,), jnp.int32),
+            jax.ShapeDtypeStruct((4 * len(tables), LANES), F32),
         ],
-        compiler_params=pltpu.CompilerParams(vmem_limit_bytes=12 * 1024 * 1024),
-    )(here, seam_codes, image)
+        compiler_params=pltpu.CompilerParams(vmem_limit_bytes=2 * 1024 * 1024),
+    )(here, seam_codes, *tables)
 
 
 def strips(scalars, pack, partner, width):
@@ -262,6 +287,10 @@
     return call(body, (scalars, pack, partner), outs, [pltpu.VMEM((4, size, LANES), BF16)])
 
 
+def norm_lines(param_ref, line):
+    return param_ref[line : line + 1], param_ref[line + 4 : line + 5]
+
+
 def west_east(scalars, near_ref, far_ref):
     near, far = near_ref[...], far_ref[...]
     odd = scalars[7] == 1
@@ -276,38 +305,43 @@
     block_rows, channels, width = image.shape
     outputs = weight.shape[0]
 
-    def body(sc, image_ref, partner_ref, ns_ref, near_ref, far_ref, weight_ref, bias_ref, raw_ref, pack_ref, stat_ref, taps):
+    def body(sc, image_ref, partner_ref, ns_ref, near_ref, far_ref, weight_ref, bias_ref, *rest):
+        raw_ref, pack_ref, stat_ref, taps, held, sent = rest
         place = sc[0]
         upper, lower = above_below(place, ns_ref[...], partner_ref[pl.ds(channels, channels)])
         west, east = west_east(sc, near_ref, far_ref)
         frame_rows(taps, 0, channels, width, block_rows, lambda r: image_ref[r], upper, lower, west, east, place)
-        finish(taps, weight_ref, raw_ref, pack_ref, stat_ref, (bias_ref, 0), block_rows, outputs, width, 1, place)
+        finish(taps, weight_ref, raw_ref, pack_ref, stat_ref, held, sent, (bias_ref, 0), block_rows, outputs, width, 1, place)
 
     return call(
         body,
         (scalars, image, partner, ns, near, far, weight, bias),
-        [((block_rows, outputs, LANES), BF16), ((3 * outputs, LANES), BF16), ((DEVICES, LANES), F32)],
-        [pltpu.VMEM((block_rows + 2, 3 * channels, LANES), BF16)],
-    )
-
-
-def plain_stage(scalars, raw, stats, partner, ns, near, far, weight, gain, shift, line, bias, first, width, depth):
+        [
+            ((block_rows, outputs, LANES), BF16),
+            ((3 * outputs, LANES), BF16),
+            ((DEVICES, LANES), F32),
+        ],
+        [pltpu.VMEM((block_rows + 2, 3 * channels, LANES), BF16), *STATS],
+    )
+
+
+def plain_stage(scalars, raw, stats, partner, ns, near, far, weight, params, line, bias, first, width, depth):
     block_rows, channels, _ = raw.shape
     outputs = weight.shape[0]
     biased = bias is not None
 
-    def body(sc, raw_in, stats_ref, partner_ref, ns_ref, near_ref, far_ref, weight_ref, gain_ref, shift_ref, *rest):
+    def body(sc, raw_in, stats_ref, partner_ref, ns_ref, near_ref, far_ref, weight_ref, param_ref, *rest):
         bias_row = None
         if biased:
             bias_row, rest = (rest[0], first), rest[1:]
         if depth:
-            raw_ref, stat_ref, pack_ref, taps = rest
+            raw_ref, stat_ref, pack_ref, taps, held, sent = rest
         else:
-            raw_ref, stat_ref, taps = rest
+            raw_ref, stat_ref, taps, held, sent = rest
             pack_ref = None
         place = sc[0]
         coef = coefficients(
-            stats_ref[...], gain_ref[line : line + 1], shift_ref[line : line + 1], bias_row, channels, float(block_rows * width)
+            stats_ref[...], *norm_lines(param_ref, line), bias_row, channels, float(block_rows * width)
         )
         lane = lane_index((channels, LANES))
         clear = jnp.zeros((channels, LANES), BF16)
@@ -330,28 +364,30 @@
             strip(east),
             place,
         )
-        finish(taps, weight_ref, raw_ref, pack_ref, stat_ref, None, block_rows, outputs, width, depth, place)
+        finish(
+            taps, weight_ref, raw_ref, pack_ref, stat_ref, held, sent, None, block_rows, outputs, width, depth, place
+        )
 
     outs = [((block_rows, outputs, LANES), BF16), ((DEVICES, LANES), F32)]
     if depth:
         outs.append(((3 * depth * outputs, LANES), BF16))
-    operands = (scalars, raw, stats, partner, ns, near, far, weight, gain, shift)
+    operands = (scalars, raw, stats, partner, ns, near, far, weight, params)
     if biased:
         operands += (bias,)
-    return call(body, operands, outs, [pltpu.VMEM((block_rows + 2, 3 * channels, LANES), BF16)])
-
-
-def pool_stage(scalars, raw, stats, partner, ns, near, far, weight, gain, shift, bias):
+    return call(body, operands, outs, [pltpu.VMEM((block_rows + 2, 3 * channels, LANES), BF16), *STATS])
+
+
+def pool_stage(scalars, raw, stats, partner, ns, near, far, weight, params, bias):
     block_rows, channels, width = raw.shape
     low_rows, low_width = block_rows // 2, width // 2
     outputs = weight.shape[0]
 
     def body(
-        sc, raw_in, stats_ref, partner_ref, ns_ref, near_ref, far_ref, weight_ref, gain_ref, shift_ref, bias_ref,
-        skip_ref, side_ref, raw_ref, pack_ref, stat_ref, taps, pooled,
+        sc, raw_in, stats_ref, partner_ref, ns_ref, near_ref, far_ref, weight_ref, param_ref, bias_ref,
+        skip_ref, side_ref, raw_ref, pack_ref, stat_ref, taps, pooled, held, sent,
     ):
         place = sc[0]
-        coef = coefficients(stats_ref[...], gain_ref[1:2], shift_ref[1:2], None, channels, float(block_rows * width))
+        coef = coefficients(stats_ref[...], *norm_lines(param_ref, 1), None, channels, float(block_rows * width))
         shape = (2 * LANES, LANES)
         row, column = lax.broadcasted_iota(jnp.int32, shape, 0), lane_index(shape)
         gather = jnp.where(((row & (LANES - 1)) >> 1) == column, 0.25, 0.0).astype(BF16)
@@ -373,8 +409,8 @@
         side_ref[3] = east_lines[0]
 
         def make(step, carry):
-            for k in range(8):
-                row = step * 8 + k
+            for k in range(low_rows):
+                row = step * low_rows + k
                 first = activate(raw_in[2 * row], coef)
                 second = activate(raw_in[2 * row + 1], coef)
                 skip_ref[2 * row] = first
@@ -382,7 +418,7 @@
                 pooled[row] = pool(first, second)
             return carry
 
-        lax.fori_loop(0, low_rows // 8, make, 0)
+        lax.fori_loop(0, 1, make, 0)
         upper, lower = above_below(place, pool(*ns_lines), pool(*inner_lines))
         frame_rows(
             taps,
@@ -397,11 +433,11 @@
             pool(*east_lines),
             place,
         )
-        finish(taps, weight_ref, raw_ref, pack_ref, stat_ref, (bias_ref, channels), low_rows, outputs, low_width, 1, place)
+        finish(taps, weight_ref, raw_ref, pack_ref, stat_ref, held, sent, (bias_ref, channels), low_rows, outputs, low_width, 1, place)
 
     return call(
         body,
-        (scalars, raw, stats, partner, ns, near, far, weight, gain, shift, bias),
+        (scalars, raw, stats, partner, ns, near, far, weight, params, bias),
         [
             ((block_rows, channels, LANES), BF16),
             ((4, channels, LANES), BF16),
@@ -409,51 +445,23 @@
             ((3 * outputs, LANES), BF16),
             ((DEVICES, LANES), F32),
         ],
-        [pltpu.VMEM((low_rows + 2, 3 * channels, LANES), BF16), pltpu.VMEM((low_rows, channels, LANES), BF16)],
-    )
-
-
-def decode_stage(scalars, raw, stats, partner, ns, near, far, skip, sides, deep_weight, skip_weight, gain, shift):
-    low_rows, channels, _ = raw.shape
-    block_rows, skip_channels, width = skip.shape
-    low_width = width // 2
-    outputs = skip_weight.shape[0]
-
-    def body(
-        sc, raw_in, stats_ref, partner_ref, ns_ref, near_ref, far_ref, skip_ref, side_ref, deep_ref, weight_ref, gain_ref,
-        shift_ref, raw_ref, pack_ref, stat_ref, deep_taps, skip_taps, wide,
-    ):
-        place = sc[0]
-        coef = coefficients(
-            stats_ref[...], gain_ref[1:2], shift_ref[1:2], None, channels, float(low_rows * low_width)
-        )
-        shape = (LANES, LANES)
-        row, column = lax.broadcasted_iota(jnp.int32, shape, 0), lane_index(shape)
-        spread = jnp.where(row == column >> 1, 1.0, 0.0).astype(BF16)
-
-        lane = lane_index((channels, LANES))
-
-        def kept(value):
-            return jnp.where(lane < low_width, activate(value, coef), jnp.zeros((channels, LANES), BF16))
-
-        def widen(value):
-            return jnp.dot(kept(value), spread, preferred_element_type=F32).astype(BF16)
-
-        def make(step, carry):
-            for k in range(8):
-                wide[step * 8 + k] = widen(raw_in[step * 8 + k])
-            return carry
-
-        lax.fori_loop(0, low_rows // 8, make, 0)
-        west, east = west_east(sc, near_ref, far_ref)
-        upper, lower = above_below(place, widen(ns_ref[...]), widen(partner_ref[pl.ds(channels, channels)]))
+        [
+            pltpu.VMEM((low_rows + 2, 3 * channels, LANES), BF16),
+            pltpu.VMEM((low_rows, channels, LANES), BF16),
+            *STATS,
+        ],
+    )
+
+
+def skip_stage(scalars, skip, sides, weight):
+    block_rows, channels, width = skip.shape
+    outputs = weight.shape[0]
+
+    def body(sc, skip_ref, side_ref, weight_ref, part_ref, taps):
         frame_rows(
-            deep_taps, 0, channels, width, low_rows, lambda r: wide[r], upper, lower, kept(west), kept(east), place
-        )
-        frame_rows(
-            skip_taps,
+            taps,
             0,
-            skip_channels,
+            channels,
             width,
             block_rows,
             lambda r: skip_ref[r],
@@ -461,11 +469,57 @@
             side_ref[1],
             side_ref[2],
             side_ref[3],
-            place,
+            sc[0],
         )
-        deep_weights, skip_weights = deep_ref[...], weight_ref[...]
+        convolve_rows(taps, weight_ref, part_ref, block_rows)
+
+    return call(
+        body,
+        (scalars, skip, sides, weight),
+        [((block_rows, outputs, LANES), BF16)],
+        [pltpu.VMEM((block_rows + 2, 3 * channels, LANES), BF16)],
+    )[0]
+
+
+def decode_stage(scalars, raw, stats, partner, ns, near, far, part, deep_weight, params):
+    low_rows, channels, _ = raw.shape
+    block_rows, outputs, width = part.shape
+    low_width = width // 2
+
+    def body(
+        sc, raw_in, stats_ref, partner_ref, ns_ref, near_ref, far_ref, part_ref, deep_ref, param_ref,
+        raw_ref, pack_ref, stat_ref, deep_taps, wide, held, sent,
+    ):
+        place = sc[0]
+        coef = coefficients(
+            stats_ref[...], *norm_lines(param_ref, 9), None, channels, float(low_rows * low_width)
+        )
+        shape = (LANES, LANES)
+        row, column = lax.broadcasted_iota(jnp.int32, shape, 0), lane_index(shape)
+        spread = jnp.where(row == column >> 1, 1.0, 0.0).astype(BF16)
+
+        lane = lane_index((channels, LANES))
+
+        def kept(value):
+            return jnp.where(lane < low_width, activate(value, coef), jnp.zeros((channels, LANES), BF16))
+
+        def widen(value):
+            return jnp.dot(kept(value), spread, preferred_element_type=F32).astype(BF16)
+
+        def make(step, carry):
+            for k in range(low_rows):
+                wide[step * low_rows + k] = widen(raw_in[step * low_rows + k])
+            return carry
+
+        lax.fori_loop(0, 1, make, 0)
+        west, east = west_east(sc, near_ref, far_ref)
+        upper, lower = above_below(place, widen(ns_ref[...]), widen(partner_ref[pl.ds(channels, channels)]))
+        frame_rows(
+            deep_taps, 0, channels, width, low_rows, lambda r: wide[r], upper, lower, kept(west), kept(east), place
+        )
+        deep_weights = deep_ref[...]
         zero = jnp.zeros((outputs, LANES), F32)
-        together = 4
+        together = 32
 
         def convolve(step, carry):
             sums, squares = carry
@@ -477,12 +531,8 @@
                 deep = jnp.dot(deep_weights, window, preferred_element_type=F32)
                 for j in range(2):
                     high = 2 * (low + j)
-                    window = jnp.concatenate(
-                        [skip_taps[pl.ds(high + i, 3)].reshape(9 * skip_channels, LANES) for i in range(2)], axis=1
-                    )
-                    both = jnp.dot(skip_weights, window, preferred_element_type=F32)
                     for i in range(2):
-                        value = both[:, i * LANES : (i + 1) * LANES]
+                        value = part_ref[high + i].astype(F32)
                         value = value + deep[i * outputs : (i + 1) * outputs, j * LANES : (j + 1) * LANES]
                         raw_ref[high + i] = value.astype(BF16)
                         sums = sums + value
@@ -491,41 +541,41 @@
 
         sums, squares = lax.fori_loop(0, low_rows // together, convolve, (zero, zero))
         stat = group_stats(sums, squares, None, outputs, float(block_rows * width), width)
-        stat_ref[...] = jnp.broadcast_to(stat, stat_ref.shape)
+        leave = send_stats(stat, held, stat_ref, sent)
         pack_edges(raw_ref, pack_ref, block_rows, outputs, width, 1, place)
+        leave.wait()
 
     return call(
         body,
-        (scalars, raw, stats, partner, ns, near, far, skip, sides, deep_weight, skip_weight, gain, shift),
+        (scalars, raw, stats, partner, ns, near, far, part, deep_weight, params),
         [((block_rows, outputs, LANES), BF16), ((3 * outputs, LANES), BF16), ((DEVICES, LANES), F32)],
         [
             pltpu.VMEM((low_rows + 2, 3 * channels, LANES), BF16),
-            pltpu.VMEM((block_rows + 2, 3 * skip_channels, LANES), BF16),
             pltpu.VMEM((low_rows, channels, LANES), BF16),
+            *STATS,
         ],
-        16,
-    )
-
-
-def project_stage(scalars, raw, stats, weight, gain, shift, kept):
+    )
+
+
+def project_stage(scalars, raw, stats, weight, params, kept):
     block_rows, channels, width = raw.shape
 
-    def body(sc, raw_in, stats_ref, weight_ref, gain_ref, shift_ref, out_ref):
-        coef = coefficients(stats_ref[...], gain_ref[3:4], shift_ref[3:4], None, channels, float(block_rows * width))
+    def body(sc, raw_in, stats_ref, weight_ref, param_ref, out_ref):
+        coef = coefficients(stats_ref[...], *norm_lines(param_ref, 3), None, channels, float(block_rows * width))
         project = weight_ref[...]
 
         def make(step, carry):
-            for k in range(0, 16, 2):
-                row = step * 16 + k
+            for k in range(0, 64, 2):
+                row = step * 64 + k
                 both = jnp.concatenate([activate(raw_in[row], coef), activate(raw_in[row + 1], coef)], axis=1)
                 result = jnp.dot(project, both, preferred_element_type=F32).astype(BF16)
                 out_ref[row] = result[:kept, :LANES]
                 out_ref[row + 1] = result[:kept, LANES:]
             return carry
 
-        lax.fori_loop(0, block_rows // 16, make, 0)
-
-    return call(body, (scalars, raw, stats, weight, gain, shift), [((block_rows, kept, LANES), BF16)])[0]
+        lax.fori_loop(0, block_rows // 64, make, 0)
+
+    return call(body, (scalars, raw, stats, weight, params), [((block_rows, kept, LANES), BF16)])[0]
 
 
 def vertical(value):
@@ -537,14 +587,15 @@
     return lax.ppermute(value, TILE_SPLIT, pairs)
 
 
-def exchange(scalars, pack, width):
+def exchange(scalars, pack, width, later=()):
     partner = lax.ppermute(pack, "split", [(0, 1), (1, 0)])
     ns, near, far = strips(scalars, pack, partner, width)
+    (ns, near, far), later = lax.optimization_barrier(((ns, near, far), later)) if later else ((ns, near, far), later)
     count = lax.axis_size(TILE)
     far = lax.ppermute(far, TILE, [(t, (t - 1 + 2 * (t % 2)) % count) for t in range(count)])
     near = lax.ppermute(near, TILE, [(t, t + 1 - 2 * (t % 2)) for t in range(count)])
     ns = vertical(ns)
-    return partner, ns, near, far
+    return (partner, ns, near, far), later
 
 
 def share(stat):
@@ -553,7 +604,7 @@
 
 
 def meet(scalars, pack, stat, width):
-    received = exchange(scalars, pack, width) if pack is not None else None
+    received = exchange(scalars, pack, width)[0] if pack is not None else None
     return (share(stat) if stat is not None else None), received
 
 
@@ -602,48 +653,79 @@
     shifts_lower,
 ):
     here = jnp.stack([lax.axis_index(TILE), lax.axis_index("split")]).astype(jnp.int32)
-    biases = embedding(timestep, time_weight, bias_upper, bias_lower)
     channels, _, width = noisy_image.shape[1:]
     padding = kernel_upper_first.shape[2] - channels
     image = jnp.transpose(jnp.pad(noisy_image[0], ((0, padding), (0, 0), (0, 0))), (1, 0, 2))
-    upper_first = flat_kernel(jnp.pad(kernel_upper_first, ((0, 0), (0, 0), (0, 0), (0, padding))))
     low_width = width // 2
     width_one = kernel_upper_first.shape[2]
 
-    pack, scalars = edges_of_image(here, image, seam_codes)
-    _, received = meet(scalars, pack, None, width)
+    pack = edges_of_image(here, image)
+    scalars, params = setup(here, seam_codes, (gains_upper, shifts_upper, gains_lower, shifts_lower))
+    received, prepared = exchange(
+        scalars,
+        pack,
+        width,
+        (
+            timestep,
+            time_weight,
+            bias_upper,
+            bias_lower,
+            kernel_upper_first,
+            kernel_upper_second,
+            kernel_lower_first,
+            kernel_lower_second,
+            kernel_decode_first,
+            kernel_decode_second,
+            output_weight,
+        ),
+    )
+    timestep, time_weight, bias_upper, bias_lower, kernel_upper_first, kernel_upper_second = prepared[:6]
+    kernel_lower_first, kernel_lower_second, kernel_decode_first, kernel_decode_second, output_weight = prepared[6:]
+    biases = embedding(timestep, time_weight, bias_upper, bias_lower)
+    weights = (
+        flat_kernel(jnp.pad(kernel_upper_first, ((0, 0), (0, 0), (0, 0), (0, padding)))),
+        flat_kernel(kernel_upper_second),
+        flat_kernel(kernel_lower_first),
+        flat_kernel(kernel_lower_second),
+        flat_kernel(kernel_decode_first[..., -width_one:]),
+        deep_kernel(kernel_decode_first[..., :-width_one]),
+        flat_kernel(kernel_decode_second),
+        jnp.pad(output_weight, ((0, padding), (0, 0))),
+        biases,
+    )
+    received, weights = lax.optimization_barrier((received, weights))
+    upper_first, upper_second, lower_first, lower_second, decode_skip, decode_deep, decode_second, project, biases = weights
     raw, pack, stat = first_stage(scalars, image, *received, upper_first, biases)
 
     stats, received = meet(scalars, pack, stat, width)
     raw, stat, pack = plain_stage(
-        scalars, raw, stats, *received, flat_kernel(kernel_upper_second), gains_upper, shifts_upper, 0, biases, 0, width, 2
+        scalars, raw, stats, *received, upper_second, params, 0, biases, 0, width, 2
     )
 
     stats, received = meet(scalars, pack, stat, width)
     skip, sides, raw, pack, stat = pool_stage(
-        scalars, raw, stats, *received, flat_kernel(kernel_lower_first), gains_upper, shifts_upper, biases
+        scalars, raw, stats, *received, lower_first, params, biases
     )
 
     stats, received = meet(scalars, pack, stat, low_width)
+    part = skip_stage(scalars, skip, sides, decode_skip)
     raw, stat, pack = plain_stage(
-        scalars, raw, stats, *received, flat_kernel(kernel_lower_second), gains_lower, shifts_lower, 0, biases, width_one,
+        scalars, raw, stats, *received, lower_second, params, 8, biases, width_one,
         low_width, 1,
     )
 
     stats, received = meet(scalars, pack, stat, low_width)
     raw, pack, stat = decode_stage(
-        scalars, raw, stats, *received, skip, sides, deep_kernel(kernel_decode_first[..., :-width_one]),
-        flat_kernel(kernel_decode_first[..., -width_one:]), gains_lower, shifts_lower,
+        scalars, raw, stats, *received, part, decode_deep, params
     )
 
     stats, received = meet(scalars, pack, stat, width)
     raw, stat = plain_stage(
-        scalars, raw, stats, *received, flat_kernel(kernel_decode_second), gains_upper, shifts_upper, 2, None, 0, width, 0
+        scalars, raw, stats, *received, decode_second, params, 2, None, 0, width, 0
     )
 
     stats, _ = meet(scalars, None, stat, width)
-    project = jnp.pad(output_weight, ((0, padding), (0, 0)))
-    result = project_stage(scalars, raw, stats, project, gains_upper, shifts_upper, channels)
+    result = project_stage(scalars, raw, stats, project, params, channels)
     return jnp.transpose(result, (1, 0, 2))[None]
 
 

time: 186 us -> 174 us (0.935)
  blocking collectives: 0 us -> 21.1 us
  waiting for transfers between devices: 35.8 us -> 22.8 us
  Pallas kernels: 41.7 us -> 29.8 us
  starting transfers between devices: 100 us -> 88.7 us
  local copies, waits for them, and re-layouts: 6.47 us -> 8.97 us
    all_to_all x0 -> x1, blocking collectives: none -> 21.1 us  [share(): return lax.all_to_all(copies, TILE_SPLIT, 0, 0).reshape(DEVICES, LANES)]
    all_to_all x6 -> x5, starting transfers between devices: 56 us -> 43.5 us  [share(): return lax.all_to_all(copies, TILE_SPLIT, 0, 0).reshape(DEVICES, LANES)]
    pallas_call x13 -> x15, Pallas kernels: 39.6 us -> 28.1 us  [call(): pl.pallas_call(body, in_specs=[SCALARS] + [WHOLE] * (len(operands) - 1),...]
    all_to_all x6 -> x5, waiting for transfers between devices: 25.3 us -> 14.3 us  [share(): return lax.all_to_all(copies, TILE_SPLIT, 0, 0).reshape(DEVICES, LANES)]
    unnamed x33 -> x32, local copies, waits for them, and re-layouts: 3.66 us -> 6.06 us
    ppermute x6, waiting for transfers between devices: 6.81 us -> 4.82 us  [vertical(): return lax.ppermute(value, TILE_SPLIT, pairs)]
  transfers between devices with their start and end apart: 30 -> 29, of which waited for: 9 -> 7; matrix products, arithmetic and copies ran while one was open for 1% -> 1% of each run, Pallas kernels for 2% -> 5%
where the time goes in v3:
time: 174 us; the launch traced here: 173 us
  starting transfers between devices  88.7 us (51%)
  Pallas kernels  29.8 us (17%)
  waiting for transfers between devices  22.8 us (13%)
  blocking collectives  21.1 us (12%)
  local copies, waits for them, and re-layouts  8.97 us (5%)
    all_to_all x5, starting transfers between devices, share(): return lax.all_to_all(copies, TILE_SPLIT, 0, 0).reshape(DEVICES, LANES)  43.5 us
    pallas_call x15, Pallas kernels, call(): pl.pallas_call(body, in_specs=[SCALARS] + [WHOLE] * (len(operands) - 1),...  28.1 us
    ppermute x6, starting transfers between devices, exchange(): partner = lax.ppermute(pack, 'split', [(0, 1), (1, 0)])  22.6 us
    all_to_all x1, blocking collectives, share(): return lax.all_to_all(copies, TILE_SPLIT, 0, 0).reshape(DEVICES, LANES)  21.1 us
    all_to_all x5, waiting for transfers between devices, share(): return lax.all_to_all(copies, TILE_SPLIT, 0, 0).reshape(DEVICES, LANES)  14.3 us
    ppermute x6, starting transfers between devices, vertical(): return lax.ppermute(value, TILE_SPLIT, pairs)  10.1 us
    ppermute x6, starting transfers between devices, exchange(): lax.ppermute(far, TILE, [(t, (t - 1 + 2 * (t % 2)) % count) for t in rang...  6.24 us
    ppermute x6, starting transfers between devices, exchange(): lax.ppermute(near, TILE, [(t, t + 1 - 2 * (t % 2)) for t in range(count)])  6.22 us
  transfers between devices with their start and end apart: 29, of which 7 were waited for; matrix products, arithmetic and copies ran while one was open for 1% of the time, Pallas kernels for 5%

profile of v3, /device:TPU:1, one launch (start us, length us, event | category | flops | bytes accessed | tf_op | source)
XLA Modules:
  0.0 173.2 jit_solution(1346650771183849617)
XLA Ops:
  0.0 1.6 copy.60
  1.8 0.8 shard_map.164.mine_ref
  2.6 3.8 %collective-permute-start = (bf16[144,128]{1,0:T(8,128)(2,1)S(1)}, bf16[144,128]{1,0:T(8,128)(2,1)S(1)}, u32[]{:S(2)}, u32[]{:S(2)}) collective-permute-start(bf16[144,128]{1,0:T(8,128)(2,1)S(1)} %shard_map.164.mine_ref), channel_id=1, source_target_pairs={{0,1},{1,0},{2,3},{3,2},{4,5},{5,4},{6,7},{7,6},{8,9},{9,8},{10,11... | collective-permute-start | bytes 110600 | tf_op jit(solution)/shard_map/ppermute | solution.py:591
  7.2 0.6 copy-done.14
  7.9 0.6 copy-done.1
  8.5 1.7 shard_map.163
  10.2 0.8 shard_map.165
  11.2 0.2 fusion.4
  11.4 1.7 collective-permute-start.1
  13.1 1.2 collective-permute-start.2
  14.3 0.3 collective-permute-start.3
  14.8 0.8 copy-done.11
  15.6 0.3 fusion.bias_ref.rest_0_
  16.1 0.6 copy-done.13
  17.1 0.8 copy-done.10
  18.2 0.2 reshape.74.deep_ref
  18.4 0.7 copy-done.6
  19.7 2.9 %shard_map.166 = (bf16[64,48,128]{2,1,0:T(8,128)(2,1)S(1)}, bf16[144,128]{1,0:T(8,128)(2,1)S(1)}, f32[128,128]{1,0:T(8,128)}) custom-call(s32[8]{0:T(128)S(1)} %get-tuple-element.71.sc, bf16[64,48,128]{2,1,0:T(8,128)(2,1)S(1)} %pad_bitcast_fusion.image_ref, bf16[144,128]{1,0:T(8,128)(2,1)S(1)} %collective-permute-done.their_ref.partner_ref, ...), custom_call_target="tpu_custom_call" | custom-call | tf_op jit(solution)/shard_map/pallas_call | solution.py:198
  22.6 11.1 %all-to-all-start = ((f32[128,1,128]{2,1,0:T(1,128)}), f32[128,1,128]{2,1,0:T(1,128)S(1)}, u32[]{:S(2)}, u32[]{:S(2)}) async-start(f32[128,1,128]{2,1,0:T(1,128)} %bitcast.21), calls=%async_computation | async-start | bytes 131072 | tf_op jit(solution)/shard_map/all_to_all | solution.py:603
  33.7 2.9 %collective-permute-start.4 = (bf16[144,128]{1,0:T(8,128)(2,1)S(1)}, bf16[144,128]{1,0:T(8,128)(2,1)S(1)}, u32[]{:S(2)}, u32[]{:S(2)}) collective-permute-start(bf16[144,128]{1,0:T(8,128)(2,1)S(1)} %get-tuple-element.97.mine_ref), channel_id=1, source_target_pairs={{0,1},{1,0},{2,3},{3,2},{4,5},{5,4},{6,7},{7,6},{8,9},{9,8},{10,11... | collective-permute-start | bytes 110600 | tf_op jit(solution)/shard_map/ppermute | solution.py:591
  36.7 1.8 %collective-permute-done.4.their_ref.partner_ref = bf16[144,128]{1,0:T(8,128)(2,1)S(1)} collective-permute-done((bf16[144,128]{1,0:T(8,128)(2,1)S(1)}, bf16[144,128]{1,0:T(8,128)(2,1)S(1)}, u32[]{:S(2)}, u32[]{:S(2)}) %collective-permute-start.4) | collective-permute-done | bytes 36896 | tf_op jit(solution)/shard_map/ppermute | solution.py:591
  38.5 0.8 shard_map.167
  39.3 1.5 collective-permute-start.5
  40.9 1.5 collective-permute-start.6
  42.4 1.3 collective-permute-start.7
  43.6 2.4 %collective-permute-done.5.ns_ref = bf16[48,128]{1,0:T(8,128)(2,1)S(1)} collective-permute-done((bf16[48,128]{1,0:T(8,128)(2,1)S(1)}, bf16[48,128]{1,0:T(8,128)(2,1)S(1)}, u32[]{:S(2)}, u32[]{:S(2)}) %collective-permute-start.5) | collective-permute-done | bytes 12320 | tf_op jit(solution)/shard_map/ppermute | solution.py:587
  46.1 3.2 %shard_map.168 = (bf16[64,48,128]{2,1,0:T(8,128)(2,1)S(1)}, f32[128,128]{1,0:T(8,128)}, bf16[288,128]{1,0:T(8,128)(2,1)S(1)}) custom-call(s32[8]{0:T(128)S(1)} %get-tuple-element.71.sc, bf16[64,48,128]{2,1,0:T(8,128)(2,1)S(1)} %get-tuple-element.95.raw_in, f32[128,128]{1,0:T(8,128)S(1)} %bitcast.62, ...), custom_call_target="tpu_custom_call" | custom-call | tf_op jit(solution)/shard_map/pallas_call | solution.py:198
  49.2 6.2 %collective-permute-start.8 = (bf16[288,128]{1,0:T(8,128)(2,1)S(1)}, bf16[288,128]{1,0:T(8,128)(2,1)S(1)}, u32[]{:S(2)}, u32[]{:S(2)}) collective-permute-start(bf16[288,128]{1,0:T(8,128)(2,1)S(1)} %get-tuple-element.105.mine_ref), channel_id=1, source_target_pairs={{0,1},{1,0},{2,3},{3,2},{4,5},{5,4},{6,7},{7,6},{8,9},{9,8},{10,11... | collective-permute-start | bytes 221192 | tf_op jit(solution)/shard_map/ppermute | solution.py:591
  55.4 8.0 %all-to-all-start.1 = ((f32[128,1,128]{2,1,0:T(1,128)}), f32[128,1,128]{2,1,0:T(1,128)S(1)}, u32[]{:S(2)}, u32[]{:S(2)}) async-start(f32[128,1,128]{2,1,0:T(1,128)} %bitcast.24), calls=%async_computation.1 | async-start | bytes 131072 | tf_op jit(solution)/shard_map/all_to_all | solution.py:603
  63.5 0.9 shard_map.169
  64.3 1.7 collective-permute-start.9
  66.0 0.7 collective-permute-start.10
  66.7 1.1 collective-permute-start.11
  67.9 5.4 %all-to-all-done.1 = f32[128,1,128]{2,1,0:T(1,128)S(1)} async-done(((f32[128,1,128]{2,1,0:T(1,128)}), f32[128,1,128]{2,1,0:T(1,128)S(1)}, u32[]{:S(2)}, u32[]{:S(2)}) %all-to-all-start.1) | async-done | bytes 65568 | tf_op jit(solution)/shard_map/all_to_all | solution.py:603
  73.4 3.1 %shard_map.170 = (bf16[64,48,128]{2,1,0:T(8,128)(2,1)S(1)}, bf16[4,48,128]{2,1,0:T(8,128)(2,1)S(1)}, bf16[32,96,128]{2,1,0:T(8,128)(2,1)S(1)}, bf16[288,128]{1,0:T(8,128)(2,1)S(1)}, f32[128,128]{1,0:T(8,128)}) custom-call(s32[8]{0:T(128)S(1)} %get-tuple-element.71.sc, bf16[64,48,128]{2,1,0:T(8,128)(2,1)S(1)} %get-tuple-element.103.raw_in, ...), custom_call_target="tpu_custom_call" | custom-call | tf_op jit(solution)/shard_map/pallas_call | solution.py:198
  76.5 3.4 %collective-permute-start.12 = (bf16[288,128]{1,0:T(8,128)(2,1)S(1)}, bf16[288,128]{1,0:T(8,128)(2,1)S(1)}, u32[]{:S(2)}, u32[]{:S(2)}) collective-permute-start(bf16[288,128]{1,0:T(8,128)(2,1)S(1)} %get-tuple-element.112.mine_ref), channel_id=1, source_target_pairs={{0,1},{1,0},{2,3},{3,2},{4,5},{5,4},{6,7},{7,6},{8,9},{9,8},{10,11... | collective-permute-start | bytes 221192 | tf_op jit(solution)/shard_map/ppermute | solution.py:591
  79.8 7.9 %all-to-all-start.2 = ((f32[128,1,128]{2,1,0:T(1,128)}), f32[128,1,128]{2,1,0:T(1,128)S(1)}, u32[]{:S(2)}, u32[]{:S(2)}) async-start(f32[128,1,128]{2,1,0:T(1,128)} %bitcast.27), calls=%async_computation.2 | async-start | bytes 131072 | tf_op jit(solution)/shard_map/all_to_all | solution.py:603
  87.7 0.9 shard_map.171
  88.6 1.7 collective-permute-start.13
  90.3 0.7 collective-permute-start.14
  91.0 1.1 collective-permute-start.15
  92.2 5.4 %all-to-all-done.2 = f32[128,1,128]{2,1,0:T(1,128)S(1)} async-done(((f32[128,1,128]{2,1,0:T(1,128)}), f32[128,1,128]{2,1,0:T(1,128)S(1)}, u32[]{:S(2)}, u32[]{:S(2)}) %all-to-all-start.2) | async-done | bytes 65568 | tf_op jit(solution)/shard_map/all_to_all | solution.py:603
  97.6 3.3 %shard_map.172 = (bf16[32,96,128]{2,1,0:T(8,128)(2,1)S(1)}, f32[128,128]{1,0:T(8,128)}, bf16[288,128]{1,0:T(8,128)(2,1)S(1)}) custom-call(s32[8]{0:T(128)S(1)} %get-tuple-element.71.sc, bf16[32,96,128]{2,1,0:T(8,128)(2,1)S(1)} %get-tuple-element.110.raw_in, f32[128,128]{1,0:T(8,128)S(1)} %bitcast.65, ...), custom_call_target="tpu_custom_call" | custom-call | tf_op jit(solution)/shard_map/pallas_call | solution.py:198
  100.9 3.4 %collective-permute-start.16 = (bf16[288,128]{1,0:T(8,128)(2,1)S(1)}, bf16[288,128]{1,0:T(8,128)(2,1)S(1)}, u32[]{:S(2)}, u32[]{:S(2)}) collective-permute-start(bf16[288,128]{1,0:T(8,128)(2,1)S(1)} %get-tuple-element.119.mine_ref), channel_id=1, source_target_pairs={{0,1},{1,0},{2,3},{3,2},{4,5},{5,4},{6,7},{7,6},{8,9},{9,8},{10,11... | collective-permute-start | bytes 221192 | tf_op jit(solution)/shard_map/ppermute | solution.py:591
  104.3 7.9 %all-to-all-start.3 = ((f32[128,1,128]{2,1,0:T(1,128)}), f32[128,1,128]{2,1,0:T(1,128)S(1)}, u32[]{:S(2)}, u32[]{:S(2)}) async-start(f32[128,1,128]{2,1,0:T(1,128)} %bitcast.30), calls=%async_computation.3 | async-start | bytes 131072 | tf_op jit(solution)/shard_map/all_to_all | solution.py:603
  112.2 0.9 shard_map.173
  113.1 1.7 collective-permute-start.17
  114.7 0.7 collective-permute-start.18
  115.4 1.1 collective-permute-start.19
  116.5 2.1 %shard_map.174.part_ref = bf16[64,48,128]{2,1,0:T(8,128)(2,1)S(1)} custom-call(s32[8]{0:T(128)S(1)} %get-tuple-element.71.sc, bf16[64,48,128]{2,1,0:T(8,128)(2,1)S(1)} %get-tuple-element.123.skip_ref, bf16[4,48,128]{2,1,0:T(8,128)(2,1)S(1)} %get-tuple-element.124.side_ref, bf16[48,432]{1,0:T(8,128)(2,1)S(1)} %reshape.73.weight_ref), custom_call_target="tpu_custom_call" | custom-call | tf_op jit(solution)/shard_map/pallas_call | solution.py:198
  118.6 3.4 %all-to-all-done.3 = f32[128,1,128]{2,1,0:T(1,128)S(1)} async-done(((f32[128,1,128]{2,1,0:T(1,128)}), f32[128,1,128]{2,1,0:T(1,128)S(1)}, u32[]{:S(2)}, u32[]{:S(2)}) %all-to-all-start.3) | async-done | bytes 65568 | tf_op jit(solution)/shard_map/all_to_all | solution.py:603
  122.1 3.7 %shard_map.175 = (bf16[64,48,128]{2,1,0:T(8,128)(2,1)S(1)}, bf16[144,128]{1,0:T(8,128)(2,1)S(1)}, f32[128,128]{1,0:T(8,128)}) custom-call(s32[8]{0:T(128)S(1)} %get-tuple-element.71.sc, bf16[32,96,128]{2,1,0:T(8,128)(2,1)S(1)} %get-tuple-element.117.raw_in, f32[128,128]{1,0:T(8,128)S(1)} %bitcast.61, ...), custom_call_target="tpu_custom_call" | custom-call | tf_op jit(solution)/shard_map/pallas_call | solution.py:198
  125.8 8.7 %all-to-all-start.4 = ((f32[128,1,128]{2,1,0:T(1,128)}), f32[128,1,128]{2,1,0:T(1,128)S(1)}, u32[]{:S(2)}, u32[]{:S(2)}) async-start(f32[128,1,128]{2,1,0:T(1,128)} %bitcast.33), calls=%async_computation.4 | async-start | bytes 131072 | tf_op jit(solution)/shard_map/all_to_all | solution.py:603
  134.5 2.9 %collective-permute-start.20 = (bf16[144,128]{1,0:T(8,128)(2,1)S(1)}, bf16[144,128]{1,0:T(8,128)(2,1)S(1)}, u32[]{:S(2)}, u32[]{:S(2)}) collective-permute-start(bf16[144,128]{1,0:T(8,128)(2,1)S(1)} %get-tuple-element.129.mine_ref), channel_id=1, source_target_pairs={{0,1},{1,0},{2,3},{3,2},{4,5},{5,4},{6,7},{7,6},{8,9},{9,8},{10,11... | collective-permute-start | bytes 110600 | tf_op jit(solution)/shard_map/ppermute | solution.py:591
  137.4 1.8 %collective-permute-done.20.their_ref.partner_ref = bf16[144,128]{1,0:T(8,128)(2,1)S(1)} collective-permute-done((bf16[144,128]{1,0:T(8,128)(2,1)S(1)}, bf16[144,128]{1,0:T(8,128)(2,1)S(1)}, u32[]{:S(2)}, u32[]{:S(2)}) %collective-permute-start.20) | collective-permute-done | bytes 36896 | tf_op jit(solution)/shard_map/ppermute | solution.py:591
  139.3 0.8 shard_map.176
  140.1 1.8 %collective-permute-start.21 = (bf16[48,128]{1,0:T(8,128)(2,1)S(1)}, bf16[48,128]{1,0:T(8,128)(2,1)S(1)}, u32[]{:S(2)}, u32[]{:S(2)}) collective-permute-start(bf16[48,128]{1,0:T(8,128)(2,1)S(1)} %get-tuple-element.130), channel_id=1, source_target_pairs={{0,8},{1,121},{2,10},{3,123},{4,12},{5,125},{6,14},{7,127},{8,16},... | collective-permute-start | bytes 36872 | tf_op jit(solution)/shard_map/ppermute | solution.py:587
  141.9 1.5 collective-permute-start.22
  143.4 1.3 collective-permute-start.23
  144.6 2.4 %collective-permute-done.21.ns_ref = bf16[48,128]{1,0:T(8,128)(2,1)S(1)} collective-permute-done((bf16[48,128]{1,0:T(8,128)(2,1)S(1)}, bf16[48,128]{1,0:T(8,128)(2,1)S(1)}, u32[]{:S(2)}, u32[]{:S(2)}) %collective-permute-start.21) | collective-permute-done | bytes 12320 | tf_op jit(solution)/shard_map/ppermute | solution.py:587
  147.0 2.6 %shard_map.177 = (bf16[64,48,128]{2,1,0:T(8,128)(2,1)S(1)}, f32[128,128]{1,0:T(8,128)S(1)}) custom-call(s32[8]{0:T(128)S(1)} %get-tuple-element.71.sc, bf16[64,48,128]{2,1,0:T(8,128)(2,1)S(1)} %get-tuple-element.127.raw_in, f32[128,128]{1,0:T(8,128)S(1)} %bitcast.64, bf16[144,128]{1,0:T(8,128)(2,1)S(1)} %collective-permute-done.20.their_ref.partner_ref, ...), custom_call_target="tpu_custom_call" | custom-call | tf_op jit(solution)/shard_map/pallas_call | solution.py:198
  149.6 21.1 %all_to_all.30 = f32[128,1,128]{2,1,0:T(1,128)S(1)} all-to-all(f32[128,1,128]{2,1,0:T(1,128)S(1)} %bitcast.67), channel_id=1, replica_groups=mesh['tile_0'=4,'tile_1'=4,'tile_2'=2,'tile_3'=2,'split'=2] {'tile_0','t..., dimensions={0} | all-to-all | bytes 131072 | tf_op jit(solution)/shard_map/all_to_all | solution.py:603
  170.7 1.3 shard_map.178
  172.1 1.1 copy.58
  (72 shorter events, 2.4 us)
Async XLA Ops:
  0.0 11.2 %copy-start = (f32[48,192]{1,0:T(8,128)S(1)}, f32[48,192]{1,0:T(8,128)}, u32[]{:S(2)}) copy-start(f32[48,192]{1,0:T(8,128)} %param.20) | copy-start | bytes 110596
  1.8 9.3 %copy-start.5 = (bf16[3,3,48,144]{3,2,1,0:T(8,128)(2,1)S(1)}, bf16[3,3,48,144]{3,2,1,0:T(8,128)(2,1)}, u32[]{:S(2)}) copy-start(bf16[3,3,48,144]{3,2,1,0:T(8,128)(2,1)} %param.27) | copy-start | bytes 373252
  2.6 7.6 %collective-permute-start = (bf16[144,128]{1,0:T(8,128)(2,1)S(1)}, bf16[144,128]{1,0:T(8,128)(2,1)S(1)}, u32[]{:S(2)}, u32[]{:S(2)}) collective-permute-start(bf16[144,128]{1,0:T(8,128)(2,1)S(1)} %shard_map.164.mine_ref), channel_id=1, source_target_pairs={{0,1},{1,0},{2,3},{3,2},{4,5},{5,4},{6,7},{7,6},{8,9},{9,8},{10,11... | collective-permute-start | bytes 110600 | tf_op jit(solution)/shard_map/ppermute | solution.py:591
  7.1 0.7 copy-start.14
  7.8 0.7 copy-start.1
  7.8 0.7 copy-start.2
  7.8 0.7 copy-start.3
  7.8 0.7 copy-start.4
  11.1 3.5 %copy-start.12 = (f32[192,48]{0,1:T(8,128)S(1)}, f32[192,48]{0,1:T(8,128)}, u32[]{:S(2)}) copy-start(f32[192,48]{0,1:T(8,128)} %param.21) | copy-start | bytes 110596
  11.2 3.6 %copy-start.7 = (bf16[3,3,48,45]{3,2,1,0:T(8,128)(2,1)S(1)}, bf16[3,3,48,45]{3,2,1,0:T(8,128)(2,1)}, u32[]{:S(2)}) copy-start(bf16[3,3,48,45]{3,2,1,0:T(8,128)(2,1)} %param.23) | copy-start | bytes 116644
  11.4 8.3 %collective-permute-start.1 = (bf16[48,128]{1,0:T(8,128)(2,1)S(1)}, bf16[48,128]{1,0:T(8,128)(2,1)S(1)}, u32[]{:S(2)}, u32[]{:S(2)}) collective-permute-start(bf16[48,128]{1,0:T(8,128)(2,1)S(1)} %get-tuple-element.75), channel_id=1, source_target_pairs={{0,8},{1,121},{2,10},{3,123},{4,12},{5,125},{6,14},{7,127},{8,16},... | collective-permute-start | bytes 36872 | tf_op jit(solution)/shard_map/ppermute | solution.py:587
  13.1 6.6 %collective-permute-start.2 = (bf16[48,128]{1,0:T(8,128)(2,1)S(1)}, bf16[48,128]{1,0:T(8,128)(2,1)S(1)}, u32[]{:S(2)}, u32[]{:S(2)}) collective-permute-start(bf16[48,128]{1,0:T(8,128)(2,1)S(1)} %get-tuple-element.76), channel_id=1, source_target_pairs={{0,2},{2,0},{4,6},{6,4},{8,10},{10,8},{12,14},{14,12},{16,18},{18,... | collective-permute-start | bytes 36872 | tf_op jit(solution)/shard_map/ppermute | solution.py:596
  14.3 5.4 %collective-permute-start.3 = (bf16[48,128]{1,0:T(8,128)(2,1)S(1)}, bf16[48,128]{1,0:T(8,128)(2,1)S(1)}, u32[]{:S(2)}, u32[]{:S(2)}) collective-permute-start(bf16[48,128]{1,0:T(8,128)(2,1)S(1)} %get-tuple-element.77), channel_id=1, source_target_pairs={{0,126},{2,4},{4,2},{6,8},{8,6},{10,12},{12,10},{14,16},{16,14},{1... | collective-permute-start | bytes 36872 | tf_op jit(solution)/shard_map/ppermute | solution.py:595
  14.7 0.9 copy-start.11
  16.0 0.7 copy-start.13
  16.0 0.9 copy-start.9
  17.0 0.9 copy-start.10
  18.2 0.9 copy-start.6
  22.6 23.4 %all-to-all-start = ((f32[128,1,128]{2,1,0:T(1,128)}), f32[128,1,128]{2,1,0:T(1,128)S(1)}, u32[]{:S(2)}, u32[]{:S(2)}) async-start(f32[128,1,128]{2,1,0:T(1,128)} %bitcast.21), calls=%async_computation | async-start | bytes 131072 | tf_op jit(solution)/shard_map/all_to_all | solution.py:603
  33.7 4.8 %collective-permute-start.4 = (bf16[144,128]{1,0:T(8,128)(2,1)S(1)}, bf16[144,128]{1,0:T(8,128)(2,1)S(1)}, u32[]{:S(2)}, u32[]{:S(2)}) collective-permute-start(bf16[144,128]{1,0:T(8,128)(2,1)S(1)} %get-tuple-element.97.mine_ref), channel_id=1, source_target_pairs={{0,1},{1,0},{2,3},{3,2},{4,5},{5,4},{6,7},{7,6},{8,9},{9,8},{10,11... | collective-permute-start | bytes 110600 | tf_op jit(solution)/shard_map/ppermute | solution.py:591
  39.3 6.7 %collective-permute-start.5 = (bf16[48,128]{1,0:T(8,128)(2,1)S(1)}, bf16[48,128]{1,0:T(8,128)(2,1)S(1)}, u32[]{:S(2)}, u32[]{:S(2)}) collective-permute-start(bf16[48,128]{1,0:T(8,128)(2,1)S(1)} %get-tuple-element.98), channel_id=1, source_target_pairs={{0,8},{1,121},{2,10},{3,123},{4,12},{5,125},{6,14},{7,127},{8,16},... | collective-permute-start | bytes 36872 | tf_op jit(solution)/shard_map/ppermute | solution.py:587
  40.9 5.2 %collective-permute-start.6 = (bf16[48,128]{1,0:T(8,128)(2,1)S(1)}, bf16[48,128]{1,0:T(8,128)(2,1)S(1)}, u32[]{:S(2)}, u32[]{:S(2)}) collective-permute-start(bf16[48,128]{1,0:T(8,128)(2,1)S(1)} %get-tuple-element.99), channel_id=1, source_target_pairs={{0,2},{2,0},{4,6},{6,4},{8,10},{10,8},{12,14},{14,12},{16,18},{18,... | collective-permute-start | bytes 36872 | tf_op jit(solution)/shard_map/ppermute | solution.py:596
  42.4 3.7 %collective-permute-start.7 = (bf16[48,128]{1,0:T(8,128)(2,1)S(1)}, bf16[48,128]{1,0:T(8,128)(2,1)S(1)}, u32[]{:S(2)}, u32[]{:S(2)}) collective-permute-start(bf16[48,128]{1,0:T(8,128)(2,1)S(1)} %get-tuple-element.100), channel_id=1, source_target_pairs={{0,126},{2,4},{4,2},{6,8},{8,6},{10,12},{12,10},{14,16},{16,14},{1... | collective-permute-start | bytes 36872 | tf_op jit(solution)/shard_map/ppermute | solution.py:595
  49.2 14.2 %collective-permute-start.8 = (bf16[288,128]{1,0:T(8,128)(2,1)S(1)}, bf16[288,128]{1,0:T(8,128)(2,1)S(1)}, u32[]{:S(2)}, u32[]{:S(2)}) collective-permute-start(bf16[288,128]{1,0:T(8,128)(2,1)S(1)} %get-tuple-element.105.mine_ref), channel_id=1, source_target_pairs={{0,1},{1,0},{2,3},{3,2},{4,5},{5,4},{6,7},{7,6},{8,9},{9,8},{10,11... | collective-permute-start | bytes 221192 | tf_op jit(solution)/shard_map/ppermute | solution.py:591
  55.4 12.4 %copy-start.8 = (bf16[3,3,96,48]{2,3,1,0:T(8,128)(2,1)S(1)}, bf16[3,3,96,48]{2,3,1,0:T(8,128)(2,1)}, u32[]{:S(2)}) copy-start(bf16[3,3,96,48]{2,3,1,0:T(8,128)(2,1)} %param.25) | copy-start | bytes 248836
  55.4 17.9 %all-to-all-start.1 = ((f32[128,1,128]{2,1,0:T(1,128)}), f32[128,1,128]{2,1,0:T(1,128)S(1)}, u32[]{:S(2)}, u32[]{:S(2)}) async-start(f32[128,1,128]{2,1,0:T(1,128)} %bitcast.24), calls=%async_computation.1 | async-start | bytes 131072 | tf_op jit(solution)/shard_map/all_to_all | solution.py:603
  64.3 9.0 %collective-permute-start.9 = (bf16[96,128]{1,0:T(8,128)(2,1)S(1)}, bf16[96,128]{1,0:T(8,128)(2,1)S(1)}, u32[]{:S(2)}, u32[]{:S(2)}) collective-permute-start(bf16[96,128]{1,0:T(8,128)(2,1)S(1)} %get-tuple-element.106), channel_id=1, source_target_pairs={{0,8},{1,121},{2,10},{3,123},{4,12},{5,125},{6,14},{7,127},{8,16},... | collective-permute-start | bytes 73736 | tf_op jit(solution)/shard_map/ppermute | solution.py:587
  66.0 7.3 %collective-permute-start.10 = (bf16[96,128]{1,0:T(8,128)(2,1)S(1)}, bf16[96,128]{1,0:T(8,128)(2,1)S(1)}, u32[]{:S(2)}, u32[]{:S(2)}) collective-permute-start(bf16[96,128]{1,0:T(8,128)(2,1)S(1)} %get-tuple-element.107), channel_id=1, source_target_pairs={{0,2},{2,0},{4,6},{6,4},{8,10},{10,8},{12,14},{14,12},{16,18},{18,... | collective-permute-start | bytes 73736 | tf_op jit(solution)/shard_map/ppermute | solution.py:596
  66.7 6.7 %collective-permute-start.11 = (bf16[96,128]{1,0:T(8,128)(2,1)S(1)}, bf16[96,128]{1,0:T(8,128)(2,1)S(1)}, u32[]{:S(2)}, u32[]{:S(2)}) collective-permute-start(bf16[96,128]{1,0:T(8,128)(2,1)S(1)} %get-tuple-element.108), channel_id=1, source_target_pairs={{0,126},{2,4},{4,2},{6,8},{8,6},{10,12},{12,10},{14,16},{16,14},{1... | collective-permute-start | bytes 73736 | tf_op jit(solution)/shard_map/ppermute | solution.py:595
  76.5 11.3 %collective-permute-start.12 = (bf16[288,128]{1,0:T(8,128)(2,1)S(1)}, bf16[288,128]{1,0:T(8,128)(2,1)S(1)}, u32[]{:S(2)}, u32[]{:S(2)}) collective-permute-start(bf16[288,128]{1,0:T(8,128)(2,1)S(1)} %get-tuple-element.112.mine_ref), channel_id=1, source_target_pairs={{0,1},{1,0},{2,3},{3,2},{4,5},{5,4},{6,7},{7,6},{8,9},{9,8},{10,11... | collective-permute-start | bytes 221192 | tf_op jit(solution)/shard_map/ppermute | solution.py:591
  79.8 17.8 %all-to-all-start.2 = ((f32[128,1,128]{2,1,0:T(1,128)}), f32[128,1,128]{2,1,0:T(1,128)S(1)}, u32[]{:S(2)}, u32[]{:S(2)}) async-start(f32[128,1,128]{2,1,0:T(1,128)} %bitcast.27), calls=%async_computation.2 | async-start | bytes 131072 | tf_op jit(solution)/shard_map/all_to_all | solution.py:603
  88.6 9.0 %collective-permute-start.13 = (bf16[96,128]{1,0:T(8,128)(2,1)S(1)}, bf16[96,128]{1,0:T(8,128)(2,1)S(1)}, u32[]{:S(2)}, u32[]{:S(2)}) collective-permute-start(bf16[96,128]{1,0:T(8,128)(2,1)S(1)} %get-tuple-element.113), channel_id=1, source_target_pairs={{0,8},{1,121},{2,10},{3,123},{4,12},{5,125},{6,14},{7,127},{8,16},... | collective-permute-start | bytes 73736 | tf_op jit(solution)/shard_map/ppermute | solution.py:587
  90.3 7.4 %collective-permute-start.14 = (bf16[96,128]{1,0:T(8,128)(2,1)S(1)}, bf16[96,128]{1,0:T(8,128)(2,1)S(1)}, u32[]{:S(2)}, u32[]{:S(2)}) collective-permute-start(bf16[96,128]{1,0:T(8,128)(2,1)S(1)} %get-tuple-element.114), channel_id=1, source_target_pairs={{0,2},{2,0},{4,6},{6,4},{8,10},{10,8},{12,14},{14,12},{16,18},{18,... | collective-permute-start | bytes 73736 | tf_op jit(solution)/shard_map/ppermute | solution.py:596
  91.0 6.7 %collective-permute-start.15 = (bf16[96,128]{1,0:T(8,128)(2,1)S(1)}, bf16[96,128]{1,0:T(8,128)(2,1)S(1)}, u32[]{:S(2)}, u32[]{:S(2)}) collective-permute-start(bf16[96,128]{1,0:T(8,128)(2,1)S(1)} %get-tuple-element.115), channel_id=1, source_target_pairs={{0,126},{2,4},{4,2},{6,8},{8,6},{10,12},{12,10},{14,16},{16,14},{1... | collective-permute-start | bytes 73736 | tf_op jit(solution)/shard_map/ppermute | solution.py:595
  100.9 11.3 %collective-permute-start.16 = (bf16[288,128]{1,0:T(8,128)(2,1)S(1)}, bf16[288,128]{1,0:T(8,128)(2,1)S(1)}, u32[]{:S(2)}, u32[]{:S(2)}) collective-permute-start(bf16[288,128]{1,0:T(8,128)(2,1)S(1)} %get-tuple-element.119.mine_ref), channel_id=1, source_target_pairs={{0,1},{1,0},{2,3},{3,2},{4,5},{5,4},{6,7},{7,6},{8,9},{9,8},{10,11... | collective-permute-start | bytes 221192 | tf_op jit(solution)/shard_map/ppermute | solution.py:591
  104.3 17.8 %all-to-all-start.3 = ((f32[128,1,128]{2,1,0:T(1,128)}), f32[128,1,128]{2,1,0:T(1,128)S(1)}, u32[]{:S(2)}, u32[]{:S(2)}) async-start(f32[128,1,128]{2,1,0:T(1,128)} %bitcast.30), calls=%async_computation.3 | async-start | bytes 131072 | tf_op jit(solution)/shard_map/all_to_all | solution.py:603
  113.1 9.0 %collective-permute-start.17 = (bf16[96,128]{1,0:T(8,128)(2,1)S(1)}, bf16[96,128]{1,0:T(8,128)(2,1)S(1)}, u32[]{:S(2)}, u32[]{:S(2)}) collective-permute-start(bf16[96,128]{1,0:T(8,128)(2,1)S(1)} %get-tuple-element.120), channel_id=1, source_target_pairs={{0,8},{1,121},{2,10},{3,123},{4,12},{5,125},{6,14},{7,127},{8,16},... | collective-permute-start | bytes 73736 | tf_op jit(solution)/shard_map/ppermute | solution.py:587
  114.7 7.4 %collective-permute-start.18 = (bf16[96,128]{1,0:T(8,128)(2,1)S(1)}, bf16[96,128]{1,0:T(8,128)(2,1)S(1)}, u32[]{:S(2)}, u32[]{:S(2)}) collective-permute-start(bf16[96,128]{1,0:T(8,128)(2,1)S(1)} %get-tuple-element.121), channel_id=1, source_target_pairs={{0,2},{2,0},{4,6},{6,4},{8,10},{10,8},{12,14},{14,12},{16,18},{18,... | collective-permute-start | bytes 73736 | tf_op jit(solution)/shard_map/ppermute | solution.py:596
  115.4 6.7 %collective-permute-start.19 = (bf16[96,128]{1,0:T(8,128)(2,1)S(1)}, bf16[96,128]{1,0:T(8,128)(2,1)S(1)}, u32[]{:S(2)}, u32[]{:S(2)}) collective-permute-start(bf16[96,128]{1,0:T(8,128)(2,1)S(1)} %get-tuple-element.122), channel_id=1, source_target_pairs={{0,126},{2,4},{4,2},{6,8},{8,6},{10,12},{12,10},{14,16},{16,14},{1... | collective-permute-start | bytes 73736 | tf_op jit(solution)/shard_map/ppermute | solution.py:595
  125.8 21.2 %all-to-all-start.4 = ((f32[128,1,128]{2,1,0:T(1,128)}), f32[128,1,128]{2,1,0:T(1,128)S(1)}, u32[]{:S(2)}, u32[]{:S(2)}) async-start(f32[128,1,128]{2,1,0:T(1,128)} %bitcast.33), calls=%async_computation.4 | async-start | bytes 131072 | tf_op jit(solution)/shard_map/all_to_all | solution.py:603
  134.5 4.8 %collective-permute-start.20 = (bf16[144,128]{1,0:T(8,128)(2,1)S(1)}, bf16[144,128]{1,0:T(8,128)(2,1)S(1)}, u32[]{:S(2)}, u32[]{:S(2)}) collective-permute-start(bf16[144,128]{1,0:T(8,128)(2,1)S(1)} %get-tuple-element.129.mine_ref), channel_id=1, source_target_pairs={{0,1},{1,0},{2,3},{3,2},{4,5},{5,4},{6,7},{7,6},{8,9},{9,8},{10,11... | collective-permute-start | bytes 110600 | tf_op jit(solution)/shard_map/ppermute | solution.py:591
  140.1 6.9 %collective-permute-start.21 = (bf16[48,128]{1,0:T(8,128)(2,1)S(1)}, bf16[48,128]{1,0:T(8,128)(2,1)S(1)}, u32[]{:S(2)}, u32[]{:S(2)}) collective-permute-start(bf16[48,128]{1,0:T(8,128)(2,1)S(1)} %get-tuple-element.130), channel_id=1, source_target_pairs={{0,8},{1,121},{2,10},{3,123},{4,12},{5,125},{6,14},{7,127},{8,16},... | collective-permute-start | bytes 36872 | tf_op jit(solution)/shard_map/ppermute | solution.py:587
  141.9 5.2 %collective-permute-start.22 = (bf16[48,128]{1,0:T(8,128)(2,1)S(1)}, bf16[48,128]{1,0:T(8,128)(2,1)S(1)}, u32[]{:S(2)}, u32[]{:S(2)}) collective-permute-start(bf16[48,128]{1,0:T(8,128)(2,1)S(1)} %get-tuple-element.131), channel_id=1, source_target_pairs={{0,2},{2,0},{4,6},{6,4},{8,10},{10,8},{12,14},{14,12},{16,18},{18,... | collective-permute-start | bytes 36872 | tf_op jit(solution)/shard_map/ppermute | solution.py:596
  143.4 3.7 %collective-permute-start.23 = (bf16[48,128]{1,0:T(8,128)(2,1)S(1)}, bf16[48,128]{1,0:T(8,128)(2,1)S(1)}, u32[]{:S(2)}, u32[]{:S(2)}) collective-permute-start(bf16[48,128]{1,0:T(8,128)(2,1)S(1)} %get-tuple-element.132), channel_id=1, source_target_pairs={{0,126},{2,4},{4,2},{6,8},{8,6},{10,12},{12,10},{14,16},{16,14},{1... | collective-permute-start | bytes 36872 | tf_op jit(solution)/shard_map/ppermute | solution.py:595

commit v4 on v3

--- a/solution.py
+++ b/solution.py
@@ -214,18 +214,14 @@
     return call(body, (here, image), [((3 * channels, LANES), BF16)])[0]
 
 
-def setup(here, seam_codes, tables):
-    count = seam_codes.shape[0]
-
-    def body(here_ref, codes, *rest):
-        table_refs, (scalar_ref, param_ref) = rest[: len(tables)], rest[len(tables) :]
+def setup(here, seam_codes):
+    count = seam_codes.shape[1]
+
+    def body(here_ref, codes, scalar_ref):
         tile, place = here_ref[0], here_ref[1]
-        for k, table_ref in enumerate(table_refs):
-            lines, columns = table_ref.shape
-            param_ref[4 * k : 4 * k + lines, 0:columns] = table_ref[...]
 
         def facing(steps, side):
-            k = (side + 2 + codes[(tile + count + steps) % count, side]) % 4
+            k = (side + 2 + codes[side, (tile + count + steps) % count]) % 4
             return k, jnp.where((k < 2) == (side < 2), 1, 0)
 
         odd = tile % 2 == 1
@@ -240,51 +236,53 @@
 
     return pl.pallas_call(
         body,
-        in_specs=[SCALARS, SCALARS] + [WHOLE] * len(tables),
-        out_specs=[SCALARS, WHOLE],
-        out_shape=[
-            jax.ShapeDtypeStruct((8,), jnp.int32),
-            jax.ShapeDtypeStruct((4 * len(tables), LANES), F32),
-        ],
+        in_specs=[SCALARS, SCALARS],
+        out_specs=SCALARS,
+        out_shape=jax.ShapeDtypeStruct((8,), jnp.int32),
         compiler_params=pltpu.CompilerParams(vmem_limit_bytes=2 * 1024 * 1024),
-    )(here, seam_codes, *tables)
+    )(here, seam_codes)
+
+
+def one_table(scalars, tables):
+    def body(sc, *rest):
+        table_refs, param_ref = rest[: len(tables)], rest[len(tables)]
+        for k, table_ref in enumerate(table_refs):
+            lines, columns = table_ref.shape
+            param_ref[4 * k : 4 * k + lines, 0:columns] = table_ref[...]
+
+    return call(body, (scalars, *tables), [((4 * len(tables), LANES), F32)])[0]
 
 
 def strips(scalars, pack, partner, width):
     size = pack.shape[0] // 3
     half = width // 2
 
-    def body(sc, mine_ref, their_ref, ns_ref, near_ref, far_ref, side_ref):
+    def body(sc, mine_ref, their_ref, ns_ref, near_ref, far_ref):
         place = sc[0]
-        lane = lane_index((size, LANES))
 
         def ordered(first):
             mine, theirs = mine_ref[pl.ds(first, size)], their_ref[pl.ds(first, size)]
-            return jnp.where(place == 0, mine, theirs), jnp.where(place == 0, theirs, mine)
-
-        low, high = ordered(0)
-        side_ref[0] = low
-        side_ref[2] = high
-        shape = (LANES, LANES)
-        row, column = lax.broadcasted_iota(jnp.int32, shape, 0), lane_index(shape)
-        low, high = ordered(2 * size)
-        both = jnp.concatenate([low, high], axis=1)
+            return [jnp.where(place == 0, mine, theirs), jnp.where(place == 0, theirs, mine)]
+
+        sources = jnp.concatenate(ordered(0) + ordered(2 * size), axis=1)
+        shape = (4 * LANES, LANES)
+        row, column = lax.broadcasted_iota(jnp.int32, shape, 0), lane_index((1, LANES))
         spacing = 2 if width == LANES else 1
-        for side, start in ((3, 0), (1, width - 1)):
-            upper = (row == (start + spacing * column) % LANES) & (column < half)
-            under = (row == (start + spacing * (column - half)) % LANES) & (column >= half) & (column < width)
-            spread = jnp.concatenate([upper, under], axis=0)
-            spread = jnp.where(spread, 1.0, 0.0).astype(BF16)
-            side_ref[side] = jnp.dot(both, spread, preferred_element_type=F32).astype(BF16)
         for k, out in enumerate((ns_ref, near_ref, far_ref)):
-            reverse = sc[2 + 2 * k]
-            hit = jnp.where(reverse == 1, width - 1 - row, row) == column
-            order = jnp.where(hit & (column < width), 1.0, 0.0).astype(BF16)
-            strip = jnp.where(lane < width, side_ref[sc[1 + 2 * k]], jnp.zeros((size, LANES), BF16))
-            out[...] = jnp.dot(strip, order, preferred_element_type=F32).astype(BF16)
+            side = sc[1 + 2 * k]
+            pixel = jnp.where(sc[2 + 2 * k] == 1, width - 1 - column, column)
+            along_row = pixel + jnp.where(side == 0, 0, LANES)
+            under = pixel >= half
+            start = jnp.where(side == 1, width - 1, 0)
+            lane = (start + spacing * jnp.where(under, pixel - half, pixel)) & (LANES - 1)
+            along_column = lane + jnp.where(under, 3 * LANES, 2 * LANES)
+            source = jnp.where((side == 0) | (side == 2), along_row, along_column)
+            source = jnp.where(column < width, source, -1)
+            pick = jnp.where(row == jnp.broadcast_to(source, shape), 1.0, 0.0).astype(BF16)
+            out[...] = jnp.dot(sources, pick, preferred_element_type=F32).astype(BF16)
 
     outs = [((size, LANES), BF16)] * 3
-    return call(body, (scalars, pack, partner), outs, [pltpu.VMEM((4, size, LANES), BF16)])
+    return call(body, (scalars, pack, partner), outs)
 
 
 def norm_lines(param_ref, line):
@@ -660,44 +658,34 @@
     width_one = kernel_upper_first.shape[2]
 
     pack = edges_of_image(here, image)
-    scalars, params = setup(here, seam_codes, (gains_upper, shifts_upper, gains_lower, shifts_lower))
-    received, prepared = exchange(
-        scalars,
-        pack,
-        width,
-        (
-            timestep,
-            time_weight,
-            bias_upper,
-            bias_lower,
-            kernel_upper_first,
-            kernel_upper_second,
-            kernel_lower_first,
-            kernel_lower_second,
-            kernel_decode_first,
-            kernel_decode_second,
-            output_weight,
-        ),
-    )
-    timestep, time_weight, bias_upper, bias_lower, kernel_upper_first, kernel_upper_second = prepared[:6]
-    kernel_lower_first, kernel_lower_second, kernel_decode_first, kernel_decode_second, output_weight = prepared[6:]
+    scalars = setup(here, seam_codes.T)
+    early = (timestep, time_weight, bias_upper, bias_lower, kernel_upper_first, kernel_upper_second)
+    late = (kernel_lower_first, kernel_lower_second, kernel_decode_first, kernel_decode_second, output_weight)
+    received, early = exchange(scalars, pack, width, early)
+    params = one_table(scalars, (gains_upper, shifts_upper, gains_lower, shifts_lower))
+    timestep, time_weight, bias_upper, bias_lower, kernel_upper_first, kernel_upper_second = early
     biases = embedding(timestep, time_weight, bias_upper, bias_lower)
     weights = (
         flat_kernel(jnp.pad(kernel_upper_first, ((0, 0), (0, 0), (0, 0), (0, padding)))),
         flat_kernel(kernel_upper_second),
+        biases,
+    )
+    received, (upper_first, upper_second, biases) = lax.optimization_barrier((received, weights))
+    raw, pack, stat = first_stage(scalars, image, *received, upper_first, biases)
+
+    received, late = exchange(scalars, pack, width, late)
+    stats = share(stat)
+    kernel_lower_first, kernel_lower_second, kernel_decode_first, kernel_decode_second, output_weight = late
+    weights = (
         flat_kernel(kernel_lower_first),
         flat_kernel(kernel_lower_second),
         flat_kernel(kernel_decode_first[..., -width_one:]),
         deep_kernel(kernel_decode_first[..., :-width_one]),
         flat_kernel(kernel_decode_second),
         jnp.pad(output_weight, ((0, padding), (0, 0))),
-        biases,
     )
     received, weights = lax.optimization_barrier((received, weights))
-    upper_first, upper_second, lower_first, lower_second, decode_skip, decode_deep, decode_second, project, biases = weights
-    raw, pack, stat = first_stage(scalars, image, *received, upper_first, biases)
-
-    stats, received = meet(scalars, pack, stat, width)
+    lower_first, lower_second, decode_skip, decode_deep, decode_second, project = weights
     raw, stat, pack = plain_stage(
         scalars, raw, stats, *received, upper_second, params, 0, biases, 0, width, 2
     )

time: 174 us -> 169 us (0.971)
  starting transfers between devices: 88.7 us -> 85.2 us
    all_to_all x5, starting transfers between devices: 43.5 us -> 39.3 us  [share(): return lax.all_to_all(copies, TILE_SPLIT, 0, 0).reshape(DEVICES, LANES)]
    all_to_all x5, waiting for transfers between devices: 14.3 us -> 16.4 us  [share(): return lax.all_to_all(copies, TILE_SPLIT, 0, 0).reshape(DEVICES, LANES)]
    ppermute x6, waiting for transfers between devices: 3.67 us -> 1.83 us  [exchange(): partner = lax.ppermute(pack, 'split', [(0, 1), (1, 0)])]
    unnamed x32 -> x31, local copies, waits for them, and re-layouts: 6.06 us -> 5.78 us
    pallas_call x15 -> x16, Pallas kernels: 28.1 us -> 28.1 us  [call(): pl.pallas_call(body, in_specs=[SCALARS] + [WHOLE] * (len(operands) - 1),...]
  transfers between devices with their start and end apart: 29 -> 29, of which waited for: 7 -> 8; matrix products, arithmetic and copies ran while one was open for 1% -> 1% of each run, Pallas kernels for 5% -> 5%
where the time goes in v4:
time: 169 us; the launch traced here: 168 us
  starting transfers between devices  85.2 us (50%)
  Pallas kernels  29.3 us (17%)
  waiting for transfers between devices  22.1 us (13%)
  blocking collectives  21.2 us (13%)
  local copies, waits for them, and re-layouts  8.68 us (5%)
    all_to_all x5, starting transfers between devices, share(): return lax.all_to_all(copies, TILE_SPLIT, 0, 0).reshape(DEVICES, LANES)  39.3 us
    pallas_call x16, Pallas kernels, call(): pl.pallas_call(body, in_specs=[SCALARS] + [WHOLE] * (len(operands) - 1),...  28.1 us
    ppermute x6, starting transfers between devices, exchange(): partner = lax.ppermute(pack, 'split', [(0, 1), (1, 0)])  23.8 us
    all_to_all x1, blocking collectives, share(): return lax.all_to_all(copies, TILE_SPLIT, 0, 0).reshape(DEVICES, LANES)  21.2 us
    all_to_all x5, waiting for transfers between devices, share(): return lax.all_to_all(copies, TILE_SPLIT, 0, 0).reshape(DEVICES, LANES)  16.4 us
    ppermute x6, starting transfers between devices, vertical(): return lax.ppermute(value, TILE_SPLIT, pairs)  10 us
    ppermute x6, starting transfers between devices, exchange(): lax.ppermute(far, TILE, [(t, (t - 1 + 2 * (t % 2)) % count) for t in rang...  6.63 us
    unnamed x31, local copies, waits for them, and re-layouts  5.78 us
  transfers between devices with their start and end apart: 29, of which 8 were waited for; matrix products, arithmetic and copies ran while one was open for 1% of the time, Pallas kernels for 5%

profile of v4, /device:TPU:1, one launch (start us, length us, event | category | flops | bytes accessed | tf_op | source)
XLA Modules:
  0.0 168.4 jit_solution(3975917862893434852)
XLA Ops:
  0.0 1.6 copy.57
  1.8 0.8 shard_map.164.mine_ref
  2.6 3.8 %collective-permute-start = (bf16[144,128]{1,0:T(8,128)(2,1)S(1)}, bf16[144,128]{1,0:T(8,128)(2,1)S(1)}, u32[]{:S(2)}, u32[]{:S(2)}) collective-permute-start(bf16[144,128]{1,0:T(8,128)(2,1)S(1)} %shard_map.164.mine_ref), channel_id=1, source_target_pairs={{0,1},{1,0},{2,3},{3,2},{4,5},{5,4},{6,7},{7,6},{8,9},{9,8},{10,11... | collective-permute-start | bytes 110600 | tf_op jit(solution)/shard_map/ppermute | solution.py:589
  7.1 0.6 copy-done.1
  7.8 1.2 shard_map.163.sc
  9.0 0.8 shard_map.165
  10.0 1.7 %collective-permute-start.1 = (bf16[48,128]{1,0:T(8,128)(2,1)S(1)}, bf16[48,128]{1,0:T(8,128)(2,1)S(1)}, u32[]{:S(2)}, u32[]{:S(2)}) collective-permute-start(bf16[48,128]{1,0:T(8,128)(2,1)S(1)} %get-tuple-element.79), channel_id=1, source_target_pairs={{0,8},{1,121},{2,10},{3,123},{4,12},{5,125},{6,14},{7,127},{8,16},... | collective-permute-start | bytes 36872 | tf_op jit(solution)/shard_map/ppermute | solution.py:585
  11.7 1.2 collective-permute-start.2
  13.0 0.9 collective-permute-start.3
  14.0 0.3 fusion.bias_ref.rest_0_
  14.2 0.6 copy-done.8
  15.1 0.8 copy-done.10
  16.0 1.1 collective-permute-done.1.ns_ref
  17.2 2.9 %shard_map.166 = (bf16[64,48,128]{2,1,0:T(8,128)(2,1)S(1)}, bf16[144,128]{1,0:T(8,128)(2,1)S(1)}, f32[128,128]{1,0:T(8,128)}) custom-call(s32[8]{0:T(128)S(1)} %shard_map.163.sc, bf16[64,48,128]{2,1,0:T(8,128)(2,1)S(1)} %pad_bitcast_fusion.image_ref, bf16[144,128]{1,0:T(8,128)(2,1)S(1)} %collective-permute-done.their_ref.partner_ref, ...), custom_call_target="tpu_custom_call" | custom-call | tf_op jit(solution)/shard_map/pallas_call | solution.py:198
  20.1 6.0 %collective-permute-start.4 = (bf16[144,128]{1,0:T(8,128)(2,1)S(1)}, bf16[144,128]{1,0:T(8,128)(2,1)S(1)}, u32[]{:S(2)}, u32[]{:S(2)}) collective-permute-start(bf16[144,128]{1,0:T(8,128)(2,1)S(1)} %get-tuple-element.96.mine_ref), channel_id=1, source_target_pairs={{0,1},{1,0},{2,3},{3,2},{4,5},{5,4},{6,7},{7,6},{8,9},{9,8},{10,11... | collective-permute-start | bytes 110600 | tf_op jit(solution)/shard_map/ppermute | solution.py:589
  26.1 0.5 shard_map.168.param_ref
  26.6 7.9 %all-to-all-start = ((f32[128,1,128]{2,1,0:T(1,128)}), f32[128,1,128]{2,1,0:T(1,128)S(1)}, u32[]{:S(2)}, u32[]{:S(2)}) async-start(f32[128,1,128]{2,1,0:T(1,128)} %bitcast.13), calls=%async_computation | async-start | bytes 131072 | tf_op jit(solution)/shard_map/all_to_all | solution.py:601
  34.5 0.8 shard_map.167
  35.5 1.7 %collective-permute-start.5 = (bf16[48,128]{1,0:T(8,128)(2,1)S(1)}, bf16[48,128]{1,0:T(8,128)(2,1)S(1)}, u32[]{:S(2)}, u32[]{:S(2)}) collective-permute-start(bf16[48,128]{1,0:T(8,128)(2,1)S(1)} %get-tuple-element.100), channel_id=1, source_target_pairs={{0,8},{1,121},{2,10},{3,123},{4,12},{5,125},{6,14},{7,127},{8,16},... | collective-permute-start | bytes 36872 | tf_op jit(solution)/shard_map/ppermute | solution.py:585
  37.2 0.7 collective-permute-start.6
  37.8 1.1 collective-permute-start.7
  39.1 0.6 copy-done.14
  40.0 0.8 copy-done.11
  41.3 0.7 copy-done.6
  42.1 0.3 collective-permute-done.5.ns_ref
  42.5 2.0 %all-to-all-done = f32[128,1,128]{2,1,0:T(1,128)S(1)} async-done(((f32[128,1,128]{2,1,0:T(1,128)}), f32[128,1,128]{2,1,0:T(1,128)S(1)}, u32[]{:S(2)}, u32[]{:S(2)}) %all-to-all-start) | async-done | bytes 65568 | tf_op jit(solution)/shard_map/all_to_all | solution.py:601
  44.4 3.2 %shard_map.169 = (bf16[64,48,128]{2,1,0:T(8,128)(2,1)S(1)}, f32[128,128]{1,0:T(8,128)}, bf16[288,128]{1,0:T(8,128)(2,1)S(1)}) custom-call(s32[8]{0:T(128)S(1)} %shard_map.163.sc, bf16[64,48,128]{2,1,0:T(8,128)(2,1)S(1)} %get-tuple-element.94.raw_in, f32[128,128]{1,0:T(8,128)S(1)} %bitcast.62, ...), custom_call_target="tpu_custom_call" | custom-call | tf_op jit(solution)/shard_map/pallas_call | solution.py:198
  47.6 4.3 %collective-permute-start.8 = (bf16[288,128]{1,0:T(8,128)(2,1)S(1)}, bf16[288,128]{1,0:T(8,128)(2,1)S(1)}, u32[]{:S(2)}, u32[]{:S(2)}) collective-permute-start(bf16[288,128]{1,0:T(8,128)(2,1)S(1)} %get-tuple-element.115.mine_ref), channel_id=1, source_target_pairs={{0,1},{1,0},{2,3},{3,2},{4,5},{5,4},{6,7},{7,6},{8,9},{9,8},{10,11... | collective-permute-start | bytes 221192 | tf_op jit(solution)/shard_map/ppermute | solution.py:589
  51.9 7.1 %all-to-all-start.1 = ((f32[128,1,128]{2,1,0:T(1,128)}), f32[128,1,128]{2,1,0:T(1,128)S(1)}, u32[]{:S(2)}, u32[]{:S(2)}) async-start(f32[128,1,128]{2,1,0:T(1,128)} %bitcast.25), calls=%async_computation.1 | async-start | bytes 131072 | tf_op jit(solution)/shard_map/all_to_all | solution.py:601
  59.0 0.8 shard_map.170
  59.8 1.7 %collective-permute-start.9 = (bf16[96,128]{1,0:T(8,128)(2,1)S(1)}, bf16[96,128]{1,0:T(8,128)(2,1)S(1)}, u32[]{:S(2)}, u32[]{:S(2)}) collective-permute-start(bf16[96,128]{1,0:T(8,128)(2,1)S(1)} %get-tuple-element.116), channel_id=1, source_target_pairs={{0,8},{1,121},{2,10},{3,123},{4,12},{5,125},{6,14},{7,127},{8,16},... | collective-permute-start | bytes 73736 | tf_op jit(solution)/shard_map/ppermute | solution.py:585
  61.5 0.7 collective-permute-start.10
  62.1 1.1 collective-permute-start.11
  63.4 5.5 %all-to-all-done.1 = f32[128,1,128]{2,1,0:T(1,128)S(1)} async-done(((f32[128,1,128]{2,1,0:T(1,128)}), f32[128,1,128]{2,1,0:T(1,128)S(1)}, u32[]{:S(2)}, u32[]{:S(2)}) %all-to-all-start.1) | async-done | bytes 65568 | tf_op jit(solution)/shard_map/all_to_all | solution.py:601
  68.9 3.1 %shard_map.171 = (bf16[64,48,128]{2,1,0:T(8,128)(2,1)S(1)}, bf16[4,48,128]{2,1,0:T(8,128)(2,1)S(1)}, bf16[32,96,128]{2,1,0:T(8,128)(2,1)S(1)}, bf16[288,128]{1,0:T(8,128)(2,1)S(1)}, f32[128,128]{1,0:T(8,128)}) custom-call(s32[8]{0:T(128)S(1)} %shard_map.163.sc, bf16[64,48,128]{2,1,0:T(8,128)(2,1)S(1)} %get-tuple-element.113.raw_in, f32[128,128]{1,0:T(8,128)S(1)} %bitcast.64, ...), custom_call_target="tpu_custom_call" | custom-call | tf_op jit(solution)/shard_map/pallas_call | solution.py:198
  72.0 3.3 %collective-permute-start.12 = (bf16[288,128]{1,0:T(8,128)(2,1)S(1)}, bf16[288,128]{1,0:T(8,128)(2,1)S(1)}, u32[]{:S(2)}, u32[]{:S(2)}) collective-permute-start(bf16[288,128]{1,0:T(8,128)(2,1)S(1)} %get-tuple-element.122.mine_ref), channel_id=1, source_target_pairs={{0,1},{1,0},{2,3},{3,2},{4,5},{5,4},{6,7},{7,6},{8,9},{9,8},{10,11... | collective-permute-start | bytes 221192 | tf_op jit(solution)/shard_map/ppermute | solution.py:589
  75.3 7.9 %all-to-all-start.2 = ((f32[128,1,128]{2,1,0:T(1,128)}), f32[128,1,128]{2,1,0:T(1,128)S(1)}, u32[]{:S(2)}, u32[]{:S(2)}) async-start(f32[128,1,128]{2,1,0:T(1,128)} %bitcast.28), calls=%async_computation.2 | async-start | bytes 131072 | tf_op jit(solution)/shard_map/all_to_all | solution.py:601
  83.2 0.8 shard_map.172
  84.0 1.7 %collective-permute-start.13 = (bf16[96,128]{1,0:T(8,128)(2,1)S(1)}, bf16[96,128]{1,0:T(8,128)(2,1)S(1)}, u32[]{:S(2)}, u32[]{:S(2)}) collective-permute-start(bf16[96,128]{1,0:T(8,128)(2,1)S(1)} %get-tuple-element.123), channel_id=1, source_target_pairs={{0,8},{1,121},{2,10},{3,123},{4,12},{5,125},{6,14},{7,127},{8,16},... | collective-permute-start | bytes 73736 | tf_op jit(solution)/shard_map/ppermute | solution.py:585
  85.7 0.7 collective-permute-start.14
  86.3 1.1 collective-permute-start.15
  87.6 5.5 %all-to-all-done.2 = f32[128,1,128]{2,1,0:T(1,128)S(1)} async-done(((f32[128,1,128]{2,1,0:T(1,128)}), f32[128,1,128]{2,1,0:T(1,128)S(1)}, u32[]{:S(2)}, u32[]{:S(2)}) %all-to-all-start.2) | async-done | bytes 65568 | tf_op jit(solution)/shard_map/all_to_all | solution.py:601
  93.1 3.3 %shard_map.173 = (bf16[32,96,128]{2,1,0:T(8,128)(2,1)S(1)}, f32[128,128]{1,0:T(8,128)}, bf16[288,128]{1,0:T(8,128)(2,1)S(1)}) custom-call(s32[8]{0:T(128)S(1)} %shard_map.163.sc, bf16[32,96,128]{2,1,0:T(8,128)(2,1)S(1)} %get-tuple-element.120.raw_in, f32[128,128]{1,0:T(8,128)S(1)} %bitcast.66, ...), custom_call_target="tpu_custom_call" | custom-call | tf_op jit(solution)/shard_map/pallas_call | solution.py:198
  96.4 3.3 %collective-permute-start.16 = (bf16[288,128]{1,0:T(8,128)(2,1)S(1)}, bf16[288,128]{1,0:T(8,128)(2,1)S(1)}, u32[]{:S(2)}, u32[]{:S(2)}) collective-permute-start(bf16[288,128]{1,0:T(8,128)(2,1)S(1)} %get-tuple-element.129.mine_ref), channel_id=1, source_target_pairs={{0,1},{1,0},{2,3},{3,2},{4,5},{5,4},{6,7},{7,6},{8,9},{9,8},{10,11... | collective-permute-start | bytes 221192 | tf_op jit(solution)/shard_map/ppermute | solution.py:589
  99.7 7.9 %all-to-all-start.3 = ((f32[128,1,128]{2,1,0:T(1,128)}), f32[128,1,128]{2,1,0:T(1,128)S(1)}, u32[]{:S(2)}, u32[]{:S(2)}) async-start(f32[128,1,128]{2,1,0:T(1,128)} %bitcast.31), calls=%async_computation.3 | async-start | bytes 131072 | tf_op jit(solution)/shard_map/all_to_all | solution.py:601
  107.6 0.8 shard_map.174
  108.4 1.7 %collective-permute-start.17 = (bf16[96,128]{1,0:T(8,128)(2,1)S(1)}, bf16[96,128]{1,0:T(8,128)(2,1)S(1)}, u32[]{:S(2)}, u32[]{:S(2)}) collective-permute-start(bf16[96,128]{1,0:T(8,128)(2,1)S(1)} %get-tuple-element.130), channel_id=1, source_target_pairs={{0,8},{1,121},{2,10},{3,123},{4,12},{5,125},{6,14},{7,127},{8,16},... | collective-permute-start | bytes 73736 | tf_op jit(solution)/shard_map/ppermute | solution.py:585
  110.1 0.7 collective-permute-start.18
  110.7 1.1 collective-permute-start.19
  111.9 2.1 %shard_map.175.part_ref = bf16[64,48,128]{2,1,0:T(8,128)(2,1)S(1)} custom-call(s32[8]{0:T(128)S(1)} %shard_map.163.sc, bf16[64,48,128]{2,1,0:T(8,128)(2,1)S(1)} %get-tuple-element.133.skip_ref, bf16[4,48,128]{2,1,0:T(8,128)(2,1)S(1)} %get-tuple-element.134.side_ref, bf16[48,432]{1,0:T(8,128)(2,1)S(1)} %reshape.75.weight_ref), custom_call_target="tpu_custom_call" | custom-call | tf_op jit(solution)/shard_map/pallas_call | solution.py:198
  114.0 3.5 %all-to-all-done.3 = f32[128,1,128]{2,1,0:T(1,128)S(1)} async-done(((f32[128,1,128]{2,1,0:T(1,128)}), f32[128,1,128]{2,1,0:T(1,128)S(1)}, u32[]{:S(2)}, u32[]{:S(2)}) %all-to-all-start.3) | async-done | bytes 65568 | tf_op jit(solution)/shard_map/all_to_all | solution.py:601
  117.5 3.7 %shard_map.176 = (bf16[64,48,128]{2,1,0:T(8,128)(2,1)S(1)}, bf16[144,128]{1,0:T(8,128)(2,1)S(1)}, f32[128,128]{1,0:T(8,128)}) custom-call(s32[8]{0:T(128)S(1)} %shard_map.163.sc, bf16[32,96,128]{2,1,0:T(8,128)(2,1)S(1)} %get-tuple-element.127.raw_in, f32[128,128]{1,0:T(8,128)S(1)} %bitcast.63, ...), custom_call_target="tpu_custom_call" | custom-call | tf_op jit(solution)/shard_map/pallas_call | solution.py:198
  121.2 8.6 %all-to-all-start.4 = ((f32[128,1,128]{2,1,0:T(1,128)}), f32[128,1,128]{2,1,0:T(1,128)S(1)}, u32[]{:S(2)}, u32[]{:S(2)}) async-start(f32[128,1,128]{2,1,0:T(1,128)} %bitcast.34), calls=%async_computation.4 | async-start | bytes 131072 | tf_op jit(solution)/shard_map/all_to_all | solution.py:601
  129.8 3.2 %collective-permute-start.20 = (bf16[144,128]{1,0:T(8,128)(2,1)S(1)}, bf16[144,128]{1,0:T(8,128)(2,1)S(1)}, u32[]{:S(2)}, u32[]{:S(2)}) collective-permute-start(bf16[144,128]{1,0:T(8,128)(2,1)S(1)} %get-tuple-element.139.mine_ref), channel_id=1, source_target_pairs={{0,1},{1,0},{2,3},{3,2},{4,5},{5,4},{6,7},{7,6},{8,9},{9,8},{10,11... | collective-permute-start | bytes 110600 | tf_op jit(solution)/shard_map/ppermute | solution.py:589
  133.0 1.8 %collective-permute-done.20.their_ref.partner_ref = bf16[144,128]{1,0:T(8,128)(2,1)S(1)} collective-permute-done((bf16[144,128]{1,0:T(8,128)(2,1)S(1)}, bf16[144,128]{1,0:T(8,128)(2,1)S(1)}, u32[]{:S(2)}, u32[]{:S(2)}) %collective-permute-start.20) | collective-permute-done | bytes 36896 | tf_op jit(solution)/shard_map/ppermute | solution.py:589
  134.8 0.8 shard_map.177
  135.5 1.5 collective-permute-start.21
  137.1 1.5 collective-permute-start.22
  138.6 1.2 collective-permute-start.23
  139.8 2.4 %collective-permute-done.21.ns_ref = bf16[48,128]{1,0:T(8,128)(2,1)S(1)} collective-permute-done((bf16[48,128]{1,0:T(8,128)(2,1)S(1)}, bf16[48,128]{1,0:T(8,128)(2,1)S(1)}, u32[]{:S(2)}, u32[]{:S(2)}) %collective-permute-start.21) | collective-permute-done | bytes 12320 | tf_op jit(solution)/shard_map/ppermute | solution.py:585
  142.2 2.6 %shard_map.178 = (bf16[64,48,128]{2,1,0:T(8,128)(2,1)S(1)}, f32[128,128]{1,0:T(8,128)S(1)}) custom-call(s32[8]{0:T(128)S(1)} %shard_map.163.sc, bf16[64,48,128]{2,1,0:T(8,128)(2,1)S(1)} %get-tuple-element.137.raw_in, f32[128,128]{1,0:T(8,128)S(1)} %bitcast.65, bf16[144,128]{1,0:T(8,128)(2,1)S(1)} %collective-permute-done.20.their_ref.partner_ref, ...), custom_call_target="tpu_custom_call" | custom-call | tf_op jit(solution)/shard_map/pallas_call | solution.py:198
  144.8 21.2 %all_to_all.30 = f32[128,1,128]{2,1,0:T(1,128)S(1)} all-to-all(f32[128,1,128]{2,1,0:T(1,128)S(1)} %bitcast.68), channel_id=1, replica_groups=mesh['tile_0'=4,'tile_1'=4,'tile_2'=2,'tile_3'=2,'split'=2] {'tile_0','t..., dimensions={0} | all-to-all | bytes 131072 | tf_op jit(solution)/shard_map/all_to_all | solution.py:601
  166.0 1.3 shard_map.179
  167.3 1.1 copy.55
  (73 shorter events, 2.4 us)
Async XLA Ops:
  0.0 9.8 %copy-start = (f32[48,192]{1,0:T(8,128)S(1)}, f32[48,192]{1,0:T(8,128)}, u32[]{:S(2)}) copy-start(f32[48,192]{1,0:T(8,128)} %param.20) | copy-start | bytes 110596
  2.6 6.4 %collective-permute-start = (bf16[144,128]{1,0:T(8,128)(2,1)S(1)}, bf16[144,128]{1,0:T(8,128)(2,1)S(1)}, u32[]{:S(2)}, u32[]{:S(2)}) collective-permute-start(bf16[144,128]{1,0:T(8,128)(2,1)S(1)} %shard_map.164.mine_ref), channel_id=1, source_target_pairs={{0,1},{1,0},{2,3},{3,2},{4,5},{5,4},{6,7},{7,6},{8,9},{9,8},{10,11... | collective-permute-start | bytes 110600 | tf_op jit(solution)/shard_map/ppermute | solution.py:589
  7.1 0.7 copy-start.1
  9.8 4.1 %copy-start.13 = (f32[192,48]{0,1:T(8,128)S(1)}, f32[192,48]{0,1:T(8,128)}, u32[]{:S(2)}) copy-start(f32[192,48]{0,1:T(8,128)} %param.21) | copy-start | bytes 110596
  9.8 4.2 %copy-start.12 = (f32[192,96]{1,0:T(8,128)S(1)}, f32[192,96]{1,0:T(8,128)}, u32[]{:S(2)}) copy-start(f32[192,96]{1,0:T(8,128)} %param.22) | copy-start | bytes 221188
  10.0 7.1 %collective-permute-start.1 = (bf16[48,128]{1,0:T(8,128)(2,1)S(1)}, bf16[48,128]{1,0:T(8,128)(2,1)S(1)}, u32[]{:S(2)}, u32[]{:S(2)}) collective-permute-start(bf16[48,128]{1,0:T(8,128)(2,1)S(1)} %get-tuple-element.79), channel_id=1, source_target_pairs={{0,8},{1,121},{2,10},{3,123},{4,12},{5,125},{6,14},{7,127},{8,16},... | collective-permute-start | bytes 36872 | tf_op jit(solution)/shard_map/ppermute | solution.py:585
  11.7 5.4 %collective-permute-start.2 = (bf16[48,128]{1,0:T(8,128)(2,1)S(1)}, bf16[48,128]{1,0:T(8,128)(2,1)S(1)}, u32[]{:S(2)}, u32[]{:S(2)}) collective-permute-start(bf16[48,128]{1,0:T(8,128)(2,1)S(1)} %get-tuple-element.80), channel_id=1, source_target_pairs={{0,2},{2,0},{4,6},{6,4},{8,10},{10,8},{12,14},{14,12},{16,18},{18,... | collective-permute-start | bytes 36872 | tf_op jit(solution)/shard_map/ppermute | solution.py:594
  13.0 4.2 %collective-permute-start.3 = (bf16[48,128]{1,0:T(8,128)(2,1)S(1)}, bf16[48,128]{1,0:T(8,128)(2,1)S(1)}, u32[]{:S(2)}, u32[]{:S(2)}) collective-permute-start(bf16[48,128]{1,0:T(8,128)(2,1)S(1)} %get-tuple-element.81), channel_id=1, source_target_pairs={{0,126},{2,4},{4,2},{6,8},{8,6},{10,12},{12,10},{14,16},{16,14},{1... | collective-permute-start | bytes 36872 | tf_op jit(solution)/shard_map/ppermute | solution.py:593
  13.9 0.9 copy-start.8
  14.9 0.9 copy-start.10
  17.1 8.9 %copy-start.2 = (f32[4,48]{1,0:T(4,128)S(1)}, f32[4,48]{1,0:T(4,128)}, u32[]{:S(2)}) copy-start(f32[4,48]{1,0:T(4,128)} %rest_0_.1) | copy-start | bytes 2308
  17.1 8.9 %copy-start.3 = (f32[4,48]{1,0:T(4,128)S(1)}, f32[4,48]{1,0:T(4,128)}, u32[]{:S(2)}) copy-start(f32[4,48]{1,0:T(4,128)} %rest_1_.1) | copy-start | bytes 2308
  17.1 8.9 %copy-start.5 = (f32[2,96]{1,0:T(2,128)S(1)}, f32[2,96]{1,0:T(2,128)}, u32[]{:S(2)}) copy-start(f32[2,96]{1,0:T(2,128)} %rest_3_.1) | copy-start | bytes 2308
  20.1 6.0 %copy-start.4 = (f32[2,96]{1,0:T(2,128)S(1)}, f32[2,96]{1,0:T(2,128)}, u32[]{:S(2)}) copy-start(f32[2,96]{1,0:T(2,128)} %rest_2_.1) | copy-start | bytes 2308
  20.1 15.2 %copy-start.7 = (bf16[3,3,48,144]{3,2,1,0:T(8,128)(2,1)S(1)}, bf16[3,3,48,144]{3,2,1,0:T(8,128)(2,1)}, u32[]{:S(2)}) copy-start(bf16[3,3,48,144]{3,2,1,0:T(8,128)(2,1)} %param.27) | copy-start | bytes 373252
  20.1 14.4 %collective-permute-start.4 = (bf16[144,128]{1,0:T(8,128)(2,1)S(1)}, bf16[144,128]{1,0:T(8,128)(2,1)S(1)}, u32[]{:S(2)}, u32[]{:S(2)}) collective-permute-start(bf16[144,128]{1,0:T(8,128)(2,1)S(1)} %get-tuple-element.96.mine_ref), channel_id=1, source_target_pairs={{0,1},{1,0},{2,3},{3,2},{4,5},{5,4},{6,7},{7,6},{8,9},{9,8},{10,11... | collective-permute-start | bytes 110600 | tf_op jit(solution)/shard_map/ppermute | solution.py:589
  26.6 17.8 %all-to-all-start = ((f32[128,1,128]{2,1,0:T(1,128)}), f32[128,1,128]{2,1,0:T(1,128)S(1)}, u32[]{:S(2)}, u32[]{:S(2)}) async-start(f32[128,1,128]{2,1,0:T(1,128)} %bitcast.13), calls=%async_computation | async-start | bytes 131072 | tf_op jit(solution)/shard_map/all_to_all | solution.py:601
  35.5 7.0 %collective-permute-start.5 = (bf16[48,128]{1,0:T(8,128)(2,1)S(1)}, bf16[48,128]{1,0:T(8,128)(2,1)S(1)}, u32[]{:S(2)}, u32[]{:S(2)}) collective-permute-start(bf16[48,128]{1,0:T(8,128)(2,1)S(1)} %get-tuple-element.100), channel_id=1, source_target_pairs={{0,8},{1,121},{2,10},{3,123},{4,12},{5,125},{6,14},{7,127},{8,16},... | collective-permute-start | bytes 36872 | tf_op jit(solution)/shard_map/ppermute | solution.py:585
  37.2 5.3 %collective-permute-start.6 = (bf16[48,128]{1,0:T(8,128)(2,1)S(1)}, bf16[48,128]{1,0:T(8,128)(2,1)S(1)}, u32[]{:S(2)}, u32[]{:S(2)}) collective-permute-start(bf16[48,128]{1,0:T(8,128)(2,1)S(1)} %get-tuple-element.101), channel_id=1, source_target_pairs={{0,2},{2,0},{4,6},{6,4},{8,10},{10,8},{12,14},{14,12},{16,18},{18,... | collective-permute-start | bytes 36872 | tf_op jit(solution)/shard_map/ppermute | solution.py:594
  37.8 4.6 %collective-permute-start.7 = (bf16[48,128]{1,0:T(8,128)(2,1)S(1)}, bf16[48,128]{1,0:T(8,128)(2,1)S(1)}, u32[]{:S(2)}, u32[]{:S(2)}) collective-permute-start(bf16[48,128]{1,0:T(8,128)(2,1)S(1)} %get-tuple-element.102), channel_id=1, source_target_pairs={{0,126},{2,4},{4,2},{6,8},{8,6},{10,12},{12,10},{14,16},{16,14},{1... | collective-permute-start | bytes 36872 | tf_op jit(solution)/shard_map/ppermute | solution.py:593
  39.0 0.7 copy-start.14
  39.8 0.9 copy-start.11
  41.0 0.9 copy-start.6
  47.6 11.4 %collective-permute-start.8 = (bf16[288,128]{1,0:T(8,128)(2,1)S(1)}, bf16[288,128]{1,0:T(8,128)(2,1)S(1)}, u32[]{:S(2)}, u32[]{:S(2)}) collective-permute-start(bf16[288,128]{1,0:T(8,128)(2,1)S(1)} %get-tuple-element.115.mine_ref), channel_id=1, source_target_pairs={{0,1},{1,0},{2,3},{3,2},{4,5},{5,4},{6,7},{7,6},{8,9},{9,8},{10,11... | collective-permute-start | bytes 221192 | tf_op jit(solution)/shard_map/ppermute | solution.py:589
  51.9 11.4 %copy-start.9 = (bf16[3,3,96,48]{2,3,1,0:T(8,128)(2,1)S(1)}, bf16[3,3,96,48]{2,3,1,0:T(8,128)(2,1)}, u32[]{:S(2)}) copy-start(bf16[3,3,96,48]{2,3,1,0:T(8,128)(2,1)} %param.25) | copy-start | bytes 248836
  51.9 17.0 %all-to-all-start.1 = ((f32[128,1,128]{2,1,0:T(1,128)}), f32[128,1,128]{2,1,0:T(1,128)S(1)}, u32[]{:S(2)}, u32[]{:S(2)}) async-start(f32[128,1,128]{2,1,0:T(1,128)} %bitcast.25), calls=%async_computation.1 | async-start | bytes 131072 | tf_op jit(solution)/shard_map/all_to_all | solution.py:601
  59.8 9.1 %collective-permute-start.9 = (bf16[96,128]{1,0:T(8,128)(2,1)S(1)}, bf16[96,128]{1,0:T(8,128)(2,1)S(1)}, u32[]{:S(2)}, u32[]{:S(2)}) collective-permute-start(bf16[96,128]{1,0:T(8,128)(2,1)S(1)} %get-tuple-element.116), channel_id=1, source_target_pairs={{0,8},{1,121},{2,10},{3,123},{4,12},{5,125},{6,14},{7,127},{8,16},... | collective-permute-start | bytes 73736 | tf_op jit(solution)/shard_map/ppermute | solution.py:585
  61.5 7.4 %collective-permute-start.10 = (bf16[96,128]{1,0:T(8,128)(2,1)S(1)}, bf16[96,128]{1,0:T(8,128)(2,1)S(1)}, u32[]{:S(2)}, u32[]{:S(2)}) collective-permute-start(bf16[96,128]{1,0:T(8,128)(2,1)S(1)} %get-tuple-element.117), channel_id=1, source_target_pairs={{0,2},{2,0},{4,6},{6,4},{8,10},{10,8},{12,14},{14,12},{16,18},{18,... | collective-permute-start | bytes 73736 | tf_op jit(solution)/shard_map/ppermute | solution.py:594
  62.1 6.8 %collective-permute-start.11 = (bf16[96,128]{1,0:T(8,128)(2,1)S(1)}, bf16[96,128]{1,0:T(8,128)(2,1)S(1)}, u32[]{:S(2)}, u32[]{:S(2)}) collective-permute-start(bf16[96,128]{1,0:T(8,128)(2,1)S(1)} %get-tuple-element.118), channel_id=1, source_target_pairs={{0,126},{2,4},{4,2},{6,8},{8,6},{10,12},{12,10},{14,16},{16,14},{1... | collective-permute-start | bytes 73736 | tf_op jit(solution)/shard_map/ppermute | solution.py:593
  72.0 11.2 %collective-permute-start.12 = (bf16[288,128]{1,0:T(8,128)(2,1)S(1)}, bf16[288,128]{1,0:T(8,128)(2,1)S(1)}, u32[]{:S(2)}, u32[]{:S(2)}) collective-permute-start(bf16[288,128]{1,0:T(8,128)(2,1)S(1)} %get-tuple-element.122.mine_ref), channel_id=1, source_target_pairs={{0,1},{1,0},{2,3},{3,2},{4,5},{5,4},{6,7},{7,6},{8,9},{9,8},{10,11... | collective-permute-start | bytes 221192 | tf_op jit(solution)/shard_map/ppermute | solution.py:589
  75.3 17.8 %all-to-all-start.2 = ((f32[128,1,128]{2,1,0:T(1,128)}), f32[128,1,128]{2,1,0:T(1,128)S(1)}, u32[]{:S(2)}, u32[]{:S(2)}) async-start(f32[128,1,128]{2,1,0:T(1,128)} %bitcast.28), calls=%async_computation.2 | async-start | bytes 131072 | tf_op jit(solution)/shard_map/all_to_all | solution.py:601
  84.0 9.1 %collective-permute-start.13 = (bf16[96,128]{1,0:T(8,128)(2,1)S(1)}, bf16[96,128]{1,0:T(8,128)(2,1)S(1)}, u32[]{:S(2)}, u32[]{:S(2)}) collective-permute-start(bf16[96,128]{1,0:T(8,128)(2,1)S(1)} %get-tuple-element.123), channel_id=1, source_target_pairs={{0,8},{1,121},{2,10},{3,123},{4,12},{5,125},{6,14},{7,127},{8,16},... | collective-permute-start | bytes 73736 | tf_op jit(solution)/shard_map/ppermute | solution.py:585
  85.7 7.4 %collective-permute-start.14 = (bf16[96,128]{1,0:T(8,128)(2,1)S(1)}, bf16[96,128]{1,0:T(8,128)(2,1)S(1)}, u32[]{:S(2)}, u32[]{:S(2)}) collective-permute-start(bf16[96,128]{1,0:T(8,128)(2,1)S(1)} %get-tuple-element.124), channel_id=1, source_target_pairs={{0,2},{2,0},{4,6},{6,4},{8,10},{10,8},{12,14},{14,12},{16,18},{18,... | collective-permute-start | bytes 73736 | tf_op jit(solution)/shard_map/ppermute | solution.py:594
  86.3 6.8 %collective-permute-start.15 = (bf16[96,128]{1,0:T(8,128)(2,1)S(1)}, bf16[96,128]{1,0:T(8,128)(2,1)S(1)}, u32[]{:S(2)}, u32[]{:S(2)}) collective-permute-start(bf16[96,128]{1,0:T(8,128)(2,1)S(1)} %get-tuple-element.125), channel_id=1, source_target_pairs={{0,126},{2,4},{4,2},{6,8},{8,6},{10,12},{12,10},{14,16},{16,14},{1... | collective-permute-start | bytes 73736 | tf_op jit(solution)/shard_map/ppermute | solution.py:593
  96.4 11.2 %collective-permute-start.16 = (bf16[288,128]{1,0:T(8,128)(2,1)S(1)}, bf16[288,128]{1,0:T(8,128)(2,1)S(1)}, u32[]{:S(2)}, u32[]{:S(2)}) collective-permute-start(bf16[288,128]{1,0:T(8,128)(2,1)S(1)} %get-tuple-element.129.mine_ref), channel_id=1, source_target_pairs={{0,1},{1,0},{2,3},{3,2},{4,5},{5,4},{6,7},{7,6},{8,9},{9,8},{10,11... | collective-permute-start | bytes 221192 | tf_op jit(solution)/shard_map/ppermute | solution.py:589
  99.7 17.8 %all-to-all-start.3 = ((f32[128,1,128]{2,1,0:T(1,128)}), f32[128,1,128]{2,1,0:T(1,128)S(1)}, u32[]{:S(2)}, u32[]{:S(2)}) async-start(f32[128,1,128]{2,1,0:T(1,128)} %bitcast.31), calls=%async_computation.3 | async-start | bytes 131072 | tf_op jit(solution)/shard_map/all_to_all | solution.py:601
  108.4 9.1 %collective-permute-start.17 = (bf16[96,128]{1,0:T(8,128)(2,1)S(1)}, bf16[96,128]{1,0:T(8,128)(2,1)S(1)}, u32[]{:S(2)}, u32[]{:S(2)}) collective-permute-start(bf16[96,128]{1,0:T(8,128)(2,1)S(1)} %get-tuple-element.130), channel_id=1, source_target_pairs={{0,8},{1,121},{2,10},{3,123},{4,12},{5,125},{6,14},{7,127},{8,16},... | collective-permute-start | bytes 73736 | tf_op jit(solution)/shard_map/ppermute | solution.py:585
  110.1 7.4 %collective-permute-start.18 = (bf16[96,128]{1,0:T(8,128)(2,1)S(1)}, bf16[96,128]{1,0:T(8,128)(2,1)S(1)}, u32[]{:S(2)}, u32[]{:S(2)}) collective-permute-start(bf16[96,128]{1,0:T(8,128)(2,1)S(1)} %get-tuple-element.131), channel_id=1, source_target_pairs={{0,2},{2,0},{4,6},{6,4},{8,10},{10,8},{12,14},{14,12},{16,18},{18,... | collective-permute-start | bytes 73736 | tf_op jit(solution)/shard_map/ppermute | solution.py:594
  110.7 6.8 %collective-permute-start.19 = (bf16[96,128]{1,0:T(8,128)(2,1)S(1)}, bf16[96,128]{1,0:T(8,128)(2,1)S(1)}, u32[]{:S(2)}, u32[]{:S(2)}) collective-permute-start(bf16[96,128]{1,0:T(8,128)(2,1)S(1)} %get-tuple-element.132), channel_id=1, source_target_pairs={{0,126},{2,4},{4,2},{6,8},{8,6},{10,12},{12,10},{14,16},{16,14},{1... | collective-permute-start | bytes 73736 | tf_op jit(solution)/shard_map/ppermute | solution.py:593
  121.2 21.0 %all-to-all-start.4 = ((f32[128,1,128]{2,1,0:T(1,128)}), f32[128,1,128]{2,1,0:T(1,128)S(1)}, u32[]{:S(2)}, u32[]{:S(2)}) async-start(f32[128,1,128]{2,1,0:T(1,128)} %bitcast.34), calls=%async_computation.4 | async-start | bytes 131072 | tf_op jit(solution)/shard_map/all_to_all | solution.py:601
  129.8 5.0 %collective-permute-start.20 = (bf16[144,128]{1,0:T(8,128)(2,1)S(1)}, bf16[144,128]{1,0:T(8,128)(2,1)S(1)}, u32[]{:S(2)}, u32[]{:S(2)}) collective-permute-start(bf16[144,128]{1,0:T(8,128)(2,1)S(1)} %get-tuple-element.139.mine_ref), channel_id=1, source_target_pairs={{0,1},{1,0},{2,3},{3,2},{4,5},{5,4},{6,7},{7,6},{8,9},{9,8},{10,11... | collective-permute-start | bytes 110600 | tf_op jit(solution)/shard_map/ppermute | solution.py:589
  135.5 6.7 %collective-permute-start.21 = (bf16[48,128]{1,0:T(8,128)(2,1)S(1)}, bf16[48,128]{1,0:T(8,128)(2,1)S(1)}, u32[]{:S(2)}, u32[]{:S(2)}) collective-permute-start(bf16[48,128]{1,0:T(8,128)(2,1)S(1)} %get-tuple-element.140), channel_id=1, source_target_pairs={{0,8},{1,121},{2,10},{3,123},{4,12},{5,125},{6,14},{7,127},{8,16},... | collective-permute-start | bytes 36872 | tf_op jit(solution)/shard_map/ppermute | solution.py:585
  137.1 5.1 %collective-permute-start.22 = (bf16[48,128]{1,0:T(8,128)(2,1)S(1)}, bf16[48,128]{1,0:T(8,128)(2,1)S(1)}, u32[]{:S(2)}, u32[]{:S(2)}) collective-permute-start(bf16[48,128]{1,0:T(8,128)(2,1)S(1)} %get-tuple-element.141), channel_id=1, source_target_pairs={{0,2},{2,0},{4,6},{6,4},{8,10},{10,8},{12,14},{14,12},{16,18},{18,... | collective-permute-start | bytes 36872 | tf_op jit(solution)/shard_map/ppermute | solution.py:594
  138.6 3.6 %collective-permute-start.23 = (bf16[48,128]{1,0:T(8,128)(2,1)S(1)}, bf16[48,128]{1,0:T(8,128)(2,1)S(1)}, u32[]{:S(2)}, u32[]{:S(2)}) collective-permute-start(bf16[48,128]{1,0:T(8,128)(2,1)S(1)} %get-tuple-element.142), channel_id=1, source_target_pairs={{0,126},{2,4},{4,2},{6,8},{8,6},{10,12},{12,10},{14,16},{16,14},{1... | collective-permute-start | bytes 36872 | tf_op jit(solution)/shard_map/ppermute | solution.py:593

commit v5 on v4

--- a/solution.py
+++ b/solution.py
@@ -299,6 +299,17 @@
     return jnp.where(place == 0, facing, inner), jnp.where(place == 0, inner, facing)
 
 
+def coef_stage(scalars, stats, params, line, bias, first, channels, pixels):
+    def body(sc, stats_ref, param_ref, *rest):
+        bias_at = (rest[0], first) if bias is not None else None
+        slope, offset = coefficients(stats_ref[...], *norm_lines(param_ref, line), bias_at, channels, float(pixels))
+        rest[-1][0] = slope
+        rest[-1][1] = offset
+
+    operands = (scalars, stats, params) + ((bias,) if bias is not None else ())
+    return call(body, operands, [((2, channels, LANES), F32)])[0]
+
+
 def first_stage(scalars, image, partner, ns, near, far, weight, bias):
     block_rows, channels, width = image.shape
     outputs = weight.shape[0]
@@ -323,24 +334,21 @@
     )
 
 
-def plain_stage(scalars, raw, stats, partner, ns, near, far, weight, params, line, bias, first, width, depth):
+def plain_stage(scalars, raw, stats, partner, ns, near, far, weight, params, bias, width, depth):
     block_rows, channels, _ = raw.shape
     outputs = weight.shape[0]
     biased = bias is not None
 
     def body(sc, raw_in, stats_ref, partner_ref, ns_ref, near_ref, far_ref, weight_ref, param_ref, *rest):
-        bias_row = None
         if biased:
-            bias_row, rest = (rest[0], first), rest[1:]
+            rest = rest[1:]
         if depth:
             raw_ref, stat_ref, pack_ref, taps, held, sent = rest
         else:
             raw_ref, stat_ref, taps, held, sent = rest
             pack_ref = None
         place = sc[0]
-        coef = coefficients(
-            stats_ref[...], *norm_lines(param_ref, line), bias_row, channels, float(block_rows * width)
-        )
+        coef = (stats_ref[0], stats_ref[1])
         lane = lane_index((channels, LANES))
         clear = jnp.zeros((channels, LANES), BF16)
 
@@ -385,7 +393,7 @@
         skip_ref, side_ref, raw_ref, pack_ref, stat_ref, taps, pooled, held, sent,
     ):
         place = sc[0]
-        coef = coefficients(stats_ref[...], *norm_lines(param_ref, 1), None, channels, float(block_rows * width))
+        coef = (stats_ref[0], stats_ref[1])
         shape = (2 * LANES, LANES)
         row, column = lax.broadcasted_iota(jnp.int32, shape, 0), lane_index(shape)
         gather = jnp.where(((row & (LANES - 1)) >> 1) == column, 0.25, 0.0).astype(BF16)
@@ -489,9 +497,7 @@
         raw_ref, pack_ref, stat_ref, deep_taps, wide, held, sent,
     ):
         place = sc[0]
-        coef = coefficients(
-            stats_ref[...], *norm_lines(param_ref, 9), None, channels, float(low_rows * low_width)
-        )
+        coef = (stats_ref[0], stats_ref[1])
         shape = (LANES, LANES)
         row, column = lax.broadcasted_iota(jnp.int32, shape, 0), lane_index(shape)
         spread = jnp.where(row == column >> 1, 1.0, 0.0).astype(BF16)
@@ -651,7 +657,7 @@
     shifts_lower,
 ):
     here = jnp.stack([lax.axis_index(TILE), lax.axis_index("split")]).astype(jnp.int32)
-    channels, _, width = noisy_image.shape[1:]
+    channels, block_rows, width = noisy_image.shape[1:]
     padding = kernel_upper_first.shape[2] - channels
     image = jnp.transpose(jnp.pad(noisy_image[0], ((0, padding), (0, 0), (0, 0))), (1, 0, 2))
     low_width = width // 2
@@ -686,31 +692,32 @@
     )
     received, weights = lax.optimization_barrier((received, weights))
     lower_first, lower_second, decode_skip, decode_deep, decode_second, project = weights
-    raw, stat, pack = plain_stage(
-        scalars, raw, stats, *received, upper_second, params, 0, biases, 0, width, 2
-    )
+    stats = coef_stage(scalars, stats, params, 0, biases, 0, width_one, block_rows * width)
+    raw, stat, pack = plain_stage(scalars, raw, stats, *received, upper_second, params, biases, width, 2)
 
     stats, received = meet(scalars, pack, stat, width)
+    stats = coef_stage(scalars, stats, params, 1, None, 0, width_one, block_rows * width)
     skip, sides, raw, pack, stat = pool_stage(
         scalars, raw, stats, *received, lower_first, params, biases
     )
 
     stats, received = meet(scalars, pack, stat, low_width)
     part = skip_stage(scalars, skip, sides, decode_skip)
+    stats = coef_stage(scalars, stats, params, 8, biases, width_one, 2 * width_one, block_rows * width // 4)
     raw, stat, pack = plain_stage(
-        scalars, raw, stats, *received, lower_second, params, 8, biases, width_one,
+        scalars, raw, stats, *received, lower_second, params, biases,
         low_width, 1,
     )
 
     stats, received = meet(scalars, pack, stat, low_width)
+    stats = coef_stage(scalars, stats, params, 9, None, 0, 2 * width_one, block_rows * width // 4)
     raw, pack, stat = decode_stage(
         scalars, raw, stats, *received, part, decode_deep, params
     )
 
     stats, received = meet(scalars, pack, stat, width)
-    raw, stat = plain_stage(
-        scalars, raw, stats, *received, decode_second, params, 2, None, 0, width, 0
-    )
+    stats = coef_stage(scalars, stats, params, 2, None, 0, width_one, block_rows * width)
+    raw, stat = plain_stage(scalars, raw, stats, *received, decode_second, params, None, width, 0)
 
     stats, _ = meet(scalars, None, stat, width)
     result = project_stage(scalars, raw, stats, project, params, channels)

time: 169 us -> 169 us (level)
  Pallas kernels: 29.3 us -> 31.9 us
  starting transfers between devices: 85.2 us -> 83.1 us
    pallas_call x16 -> x21, Pallas kernels: 28.1 us -> 30.7 us  [call(): pl.pallas_call(body, in_specs=[SCALARS] + [WHOLE] * (len(operands) - 1),...]
  transfers between devices with their start and end apart: 29 -> 29, of which waited for: 8 -> 8; matrix products, arithmetic and copies ran while one was open for 1% -> 1% of each run, Pallas kernels for 5% -> 6%
where the time goes in v5:
time: 169 us; the launch traced here: 168 us
  starting transfers between devices  83.1 us (49%)
  Pallas kernels  31.9 us (19%)
  waiting for transfers between devices  21.4 us (13%)
  blocking collectives  21.1 us (12%)
  local copies, waits for them, and re-layouts  8.69 us (5%)
    all_to_all x5, starting transfers between devices, share(): return lax.all_to_all(copies, TILE_SPLIT, 0, 0).reshape(DEVICES, LANES)  38.6 us
    pallas_call x21, Pallas kernels, call(): pl.pallas_call(body, in_specs=[SCALARS] + [WHOLE] * (len(operands) - 1),...  30.7 us
    ppermute x6, starting transfers between devices, exchange(): partner = lax.ppermute(pack, 'split', [(0, 1), (1, 0)])  22.2 us
    all_to_all x1, blocking collectives, share(): return lax.all_to_all(copies, TILE_SPLIT, 0, 0).reshape(DEVICES, LANES)  21.1 us
    all_to_all x5, waiting for transfers between devices, share(): return lax.all_to_all(copies, TILE_SPLIT, 0, 0).reshape(DEVICES, LANES)  16.4 us
    ppermute x6, starting transfers between devices, vertical(): return lax.ppermute(value, TILE_SPLIT, pairs)  10.2 us
    ppermute x6, starting transfers between devices, exchange(): lax.ppermute(far, TILE, [(t, (t - 1 + 2 * (t % 2)) % count) for t in rang...  6.73 us
    unnamed x31, local copies, waits for them, and re-layouts  5.79 us
  transfers between devices with their start and end apart: 29, of which 8 were waited for; matrix products, arithmetic and copies ran while one was open for 1% of the time, Pallas kernels for 6%

profile of v5, /device:TPU:1, one launch (start us, length us, event | category | flops | bytes accessed | tf_op | source)
XLA Modules:
  0.0 168.2 jit_solution(4996049503838346711)
XLA Ops:
  0.0 1.6 copy.57
  1.8 0.8 shard_map.164.mine_ref
  2.6 3.8 %collective-permute-start = (bf16[144,128]{1,0:T(8,128)(2,1)S(1)}, bf16[144,128]{1,0:T(8,128)(2,1)S(1)}, u32[]{:S(2)}, u32[]{:S(2)}) collective-permute-start(bf16[144,128]{1,0:T(8,128)(2,1)S(1)} %shard_map.164.mine_ref), channel_id=1, source_target_pairs={{0,1},{1,0},{2,3},{3,2},{4,5},{5,4},{6,7},{7,6},{8,9},{9,8},{10,11... | collective-permute-start | bytes 110600 | tf_op jit(solution)/shard_map/ppermute | solution.py:595
  7.8 1.2 shard_map.163.sc
  9.0 0.8 shard_map.165
  10.0 1.7 %collective-permute-start.1 = (bf16[48,128]{1,0:T(8,128)(2,1)S(1)}, bf16[48,128]{1,0:T(8,128)(2,1)S(1)}, u32[]{:S(2)}, u32[]{:S(2)}) collective-permute-start(bf16[48,128]{1,0:T(8,128)(2,1)S(1)} %get-tuple-element.79), channel_id=1, source_target_pairs={{0,8},{1,121},{2,10},{3,123},{4,12},{5,125},{6,14},{7,127},{8,16},... | collective-permute-start | bytes 36872 | tf_op jit(solution)/shard_map/ppermute | solution.py:591
  11.7 1.2 collective-permute-start.2
  13.0 0.9 collective-permute-start.3
  15.1 0.8 copy-done.10
  16.0 1.1 collective-permute-done.1.ns_ref
  17.2 2.9 %shard_map.166 = (bf16[64,48,128]{2,1,0:T(8,128)(2,1)S(1)}, bf16[144,128]{1,0:T(8,128)(2,1)S(1)}, f32[128,128]{1,0:T(8,128)}) custom-call(s32[8]{0:T(128)S(1)} %shard_map.163.sc, bf16[64,48,128]{2,1,0:T(8,128)(2,1)S(1)} %pad_bitcast_fusion.image_ref, bf16[144,128]{1,0:T(8,128)(2,1)S(1)} %collective-permute-done.their_ref.partner_ref, ...), custom_call_target="tpu_custom_call" | custom-call | tf_op jit(solution)/shard_map/pallas_call | solution.py:198
  20.1 6.0 %collective-permute-start.4 = (bf16[144,128]{1,0:T(8,128)(2,1)S(1)}, bf16[144,128]{1,0:T(8,128)(2,1)S(1)}, u32[]{:S(2)}, u32[]{:S(2)}) collective-permute-start(bf16[144,128]{1,0:T(8,128)(2,1)S(1)} %get-tuple-element.96.mine_ref), channel_id=1, source_target_pairs={{0,1},{1,0},{2,3},{3,2},{4,5},{5,4},{6,7},{7,6},{8,9},{9,8},{10,11... | collective-permute-start | bytes 110600 | tf_op jit(solution)/shard_map/ppermute | solution.py:595
  26.6 7.9 %all-to-all-start = ((f32[128,1,128]{2,1,0:T(1,128)}), f32[128,1,128]{2,1,0:T(1,128)S(1)}, u32[]{:S(2)}, u32[]{:S(2)}) async-start(f32[128,1,128]{2,1,0:T(1,128)} %bitcast.13), calls=%async_computation | async-start | bytes 131072 | tf_op jit(solution)/shard_map/all_to_all | solution.py:607
  34.5 0.8 shard_map.169
  35.5 1.7 %collective-permute-start.5 = (bf16[48,128]{1,0:T(8,128)(2,1)S(1)}, bf16[48,128]{1,0:T(8,128)(2,1)S(1)}, u32[]{:S(2)}, u32[]{:S(2)}) collective-permute-start(bf16[48,128]{1,0:T(8,128)(2,1)S(1)} %get-tuple-element.100), channel_id=1, source_target_pairs={{0,8},{1,121},{2,10},{3,123},{4,12},{5,125},{6,14},{7,127},{8,16},... | collective-permute-start | bytes 36872 | tf_op jit(solution)/shard_map/ppermute | solution.py:591
  37.2 0.7 collective-permute-start.6
  37.8 1.1 collective-permute-start.7
  39.1 0.6 copy-done.14
  40.0 0.8 copy-done.11
  41.3 0.7 copy-done.6
  42.5 2.0 %all-to-all-done = f32[128,1,128]{2,1,0:T(1,128)S(1)} async-done(((f32[128,1,128]{2,1,0:T(1,128)}), f32[128,1,128]{2,1,0:T(1,128)S(1)}, u32[]{:S(2)}, u32[]{:S(2)}) %all-to-all-start) | async-done | bytes 65568 | tf_op jit(solution)/shard_map/all_to_all | solution.py:607
  44.4 0.7 shard_map.168.stats_ref
  45.1 3.1 %shard_map.170 = (bf16[64,48,128]{2,1,0:T(8,128)(2,1)S(1)}, f32[128,128]{1,0:T(8,128)}, bf16[288,128]{1,0:T(8,128)(2,1)S(1)}) custom-call(s32[8]{0:T(128)S(1)} %shard_map.163.sc, bf16[64,48,128]{2,1,0:T(8,128)(2,1)S(1)} %get-tuple-element.94.raw_in, f32[2,48,128]{2,1,0:T(8,128)S(1)} %shard_map.168.stats_ref, ...), custom_call_target="tpu_custom_call" | custom-call | tf_op jit(solution)/shard_map/pallas_call | solution.py:198
  48.2 4.3 %collective-permute-start.8 = (bf16[288,128]{1,0:T(8,128)(2,1)S(1)}, bf16[288,128]{1,0:T(8,128)(2,1)S(1)}, u32[]{:S(2)}, u32[]{:S(2)}) collective-permute-start(bf16[288,128]{1,0:T(8,128)(2,1)S(1)} %get-tuple-element.115.mine_ref), channel_id=1, source_target_pairs={{0,1},{1,0},{2,3},{3,2},{4,5},{5,4},{6,7},{7,6},{8,9},{9,8},{10,11... | collective-permute-start | bytes 221192 | tf_op jit(solution)/shard_map/ppermute | solution.py:595
  52.5 7.1 %all-to-all-start.1 = ((f32[128,1,128]{2,1,0:T(1,128)}), f32[128,1,128]{2,1,0:T(1,128)S(1)}, u32[]{:S(2)}, u32[]{:S(2)}) async-start(f32[128,1,128]{2,1,0:T(1,128)} %bitcast.25), calls=%async_computation.1 | async-start | bytes 131072 | tf_op jit(solution)/shard_map/all_to_all | solution.py:607
  59.6 0.8 shard_map.172
  60.4 1.7 %collective-permute-start.9 = (bf16[96,128]{1,0:T(8,128)(2,1)S(1)}, bf16[96,128]{1,0:T(8,128)(2,1)S(1)}, u32[]{:S(2)}, u32[]{:S(2)}) collective-permute-start(bf16[96,128]{1,0:T(8,128)(2,1)S(1)} %get-tuple-element.116), channel_id=1, source_target_pairs={{0,8},{1,121},{2,10},{3,123},{4,12},{5,125},{6,14},{7,127},{8,16},... | collective-permute-start | bytes 73736 | tf_op jit(solution)/shard_map/ppermute | solution.py:591
  62.1 0.7 collective-permute-start.10
  62.8 1.1 collective-permute-start.11
  64.0 5.5 %all-to-all-done.1 = f32[128,1,128]{2,1,0:T(1,128)S(1)} async-done(((f32[128,1,128]{2,1,0:T(1,128)}), f32[128,1,128]{2,1,0:T(1,128)S(1)}, u32[]{:S(2)}, u32[]{:S(2)}) %all-to-all-start.1) | async-done | bytes 65568 | tf_op jit(solution)/shard_map/all_to_all | solution.py:607
  69.5 0.7 shard_map.171.stats_ref
  70.2 2.9 %shard_map.173 = (bf16[64,48,128]{2,1,0:T(8,128)(2,1)S(1)}, bf16[4,48,128]{2,1,0:T(8,128)(2,1)S(1)}, bf16[32,96,128]{2,1,0:T(8,128)(2,1)S(1)}, bf16[288,128]{1,0:T(8,128)(2,1)S(1)}, f32[128,128]{1,0:T(8,128)}) custom-call(s32[8]{0:T(128)S(1)} %shard_map.163.sc, bf16[64,48,128]{2,1,0:T(8,128)(2,1)S(1)} %get-tuple-element.113.raw_in, ...), custom_call_target="tpu_custom_call" | custom-call | tf_op jit(solution)/shard_map/pallas_call | solution.py:198
  73.1 2.6 %collective-permute-start.12 = (bf16[288,128]{1,0:T(8,128)(2,1)S(1)}, bf16[288,128]{1,0:T(8,128)(2,1)S(1)}, u32[]{:S(2)}, u32[]{:S(2)}) collective-permute-start(bf16[288,128]{1,0:T(8,128)(2,1)S(1)} %get-tuple-element.122.mine_ref), channel_id=1, source_target_pairs={{0,1},{1,0},{2,3},{3,2},{4,5},{5,4},{6,7},{7,6},{8,9},{9,8},{10,11... | collective-permute-start | bytes 221192 | tf_op jit(solution)/shard_map/ppermute | solution.py:595
  75.7 7.9 %all-to-all-start.2 = ((f32[128,1,128]{2,1,0:T(1,128)}), f32[128,1,128]{2,1,0:T(1,128)S(1)}, u32[]{:S(2)}, u32[]{:S(2)}) async-start(f32[128,1,128]{2,1,0:T(1,128)} %bitcast.28), calls=%async_computation.2 | async-start | bytes 131072 | tf_op jit(solution)/shard_map/all_to_all | solution.py:607
  83.6 0.8 shard_map.175
  84.4 1.7 %collective-permute-start.13 = (bf16[96,128]{1,0:T(8,128)(2,1)S(1)}, bf16[96,128]{1,0:T(8,128)(2,1)S(1)}, u32[]{:S(2)}, u32[]{:S(2)}) collective-permute-start(bf16[96,128]{1,0:T(8,128)(2,1)S(1)} %get-tuple-element.123), channel_id=1, source_target_pairs={{0,8},{1,121},{2,10},{3,123},{4,12},{5,125},{6,14},{7,127},{8,16},... | collective-permute-start | bytes 73736 | tf_op jit(solution)/shard_map/ppermute | solution.py:591
  86.1 0.7 collective-permute-start.14
  86.8 1.1 collective-permute-start.15
  88.0 5.5 %all-to-all-done.2 = f32[128,1,128]{2,1,0:T(1,128)S(1)} async-done(((f32[128,1,128]{2,1,0:T(1,128)}), f32[128,1,128]{2,1,0:T(1,128)S(1)}, u32[]{:S(2)}, u32[]{:S(2)}) %all-to-all-start.2) | async-done | bytes 65568 | tf_op jit(solution)/shard_map/all_to_all | solution.py:607
  93.5 0.7 shard_map.174.stats_ref
  94.3 3.0 %shard_map.176 = (bf16[32,96,128]{2,1,0:T(8,128)(2,1)S(1)}, f32[128,128]{1,0:T(8,128)}, bf16[288,128]{1,0:T(8,128)(2,1)S(1)}) custom-call(s32[8]{0:T(128)S(1)} %shard_map.163.sc, bf16[32,96,128]{2,1,0:T(8,128)(2,1)S(1)} %get-tuple-element.120.raw_in, f32[2,96,128]{2,1,0:T(8,128)S(1)} %shard_map.174.stats_ref, ...), custom_call_target="tpu_custom_call" | custom-call | tf_op jit(solution)/shard_map/pallas_call | solution.py:198
  97.3 2.6 %collective-permute-start.16 = (bf16[288,128]{1,0:T(8,128)(2,1)S(1)}, bf16[288,128]{1,0:T(8,128)(2,1)S(1)}, u32[]{:S(2)}, u32[]{:S(2)}) collective-permute-start(bf16[288,128]{1,0:T(8,128)(2,1)S(1)} %get-tuple-element.129.mine_ref), channel_id=1, source_target_pairs={{0,1},{1,0},{2,3},{3,2},{4,5},{5,4},{6,7},{7,6},{8,9},{9,8},{10,11... | collective-permute-start | bytes 221192 | tf_op jit(solution)/shard_map/ppermute | solution.py:595
  99.9 7.9 %all-to-all-start.3 = ((f32[128,1,128]{2,1,0:T(1,128)}), f32[128,1,128]{2,1,0:T(1,128)S(1)}, u32[]{:S(2)}, u32[]{:S(2)}) async-start(f32[128,1,128]{2,1,0:T(1,128)} %bitcast.31), calls=%async_computation.3 | async-start | bytes 131072 | tf_op jit(solution)/shard_map/all_to_all | solution.py:607
  107.8 0.8 shard_map.178
  108.6 1.7 %collective-permute-start.17 = (bf16[96,128]{1,0:T(8,128)(2,1)S(1)}, bf16[96,128]{1,0:T(8,128)(2,1)S(1)}, u32[]{:S(2)}, u32[]{:S(2)}) collective-permute-start(bf16[96,128]{1,0:T(8,128)(2,1)S(1)} %get-tuple-element.130), channel_id=1, source_target_pairs={{0,8},{1,121},{2,10},{3,123},{4,12},{5,125},{6,14},{7,127},{8,16},... | collective-permute-start | bytes 73736 | tf_op jit(solution)/shard_map/ppermute | solution.py:591
  110.3 0.7 collective-permute-start.18
  110.9 1.1 collective-permute-start.19
  112.1 2.1 %shard_map.179.part_ref = bf16[64,48,128]{2,1,0:T(8,128)(2,1)S(1)} custom-call(s32[8]{0:T(128)S(1)} %shard_map.163.sc, bf16[64,48,128]{2,1,0:T(8,128)(2,1)S(1)} %get-tuple-element.133.skip_ref, bf16[4,48,128]{2,1,0:T(8,128)(2,1)S(1)} %get-tuple-element.134.side_ref, bf16[48,432]{1,0:T(8,128)(2,1)S(1)} %reshape.75.weight_ref), custom_call_target="tpu_custom_call" | custom-call | tf_op jit(solution)/shard_map/pallas_call | solution.py:198
  114.2 3.5 %all-to-all-done.3 = f32[128,1,128]{2,1,0:T(1,128)S(1)} async-done(((f32[128,1,128]{2,1,0:T(1,128)}), f32[128,1,128]{2,1,0:T(1,128)S(1)}, u32[]{:S(2)}, u32[]{:S(2)}) %all-to-all-start.3) | async-done | bytes 65568 | tf_op jit(solution)/shard_map/all_to_all | solution.py:607
  117.7 0.7 shard_map.177.stats_ref
  118.4 3.6 %shard_map.180 = (bf16[64,48,128]{2,1,0:T(8,128)(2,1)S(1)}, bf16[144,128]{1,0:T(8,128)(2,1)S(1)}, f32[128,128]{1,0:T(8,128)}) custom-call(s32[8]{0:T(128)S(1)} %shard_map.163.sc, bf16[32,96,128]{2,1,0:T(8,128)(2,1)S(1)} %get-tuple-element.127.raw_in, f32[2,96,128]{2,1,0:T(8,128)S(1)} %shard_map.177.stats_ref, ...), custom_call_target="tpu_custom_call" | custom-call | tf_op jit(solution)/shard_map/pallas_call | solution.py:198
  122.0 7.9 %all-to-all-start.4 = ((f32[128,1,128]{2,1,0:T(1,128)}), f32[128,1,128]{2,1,0:T(1,128)S(1)}, u32[]{:S(2)}, u32[]{:S(2)}) async-start(f32[128,1,128]{2,1,0:T(1,128)} %bitcast.34), calls=%async_computation.4 | async-start | bytes 131072 | tf_op jit(solution)/shard_map/all_to_all | solution.py:607
  129.9 2.9 %collective-permute-start.20 = (bf16[144,128]{1,0:T(8,128)(2,1)S(1)}, bf16[144,128]{1,0:T(8,128)(2,1)S(1)}, u32[]{:S(2)}, u32[]{:S(2)}) collective-permute-start(bf16[144,128]{1,0:T(8,128)(2,1)S(1)} %get-tuple-element.139.mine_ref), channel_id=1, source_target_pairs={{0,1},{1,0},{2,3},{3,2},{4,5},{5,4},{6,7},{7,6},{8,9},{9,8},{10,11... | collective-permute-start | bytes 110600 | tf_op jit(solution)/shard_map/ppermute | solution.py:595
  132.8 1.8 %collective-permute-done.20.their_ref.partner_ref = bf16[144,128]{1,0:T(8,128)(2,1)S(1)} collective-permute-done((bf16[144,128]{1,0:T(8,128)(2,1)S(1)}, bf16[144,128]{1,0:T(8,128)(2,1)S(1)}, u32[]{:S(2)}, u32[]{:S(2)}) %collective-permute-start.20) | collective-permute-done | bytes 36896 | tf_op jit(solution)/shard_map/ppermute | solution.py:595
  134.6 0.8 shard_map.182
  135.4 1.8 %collective-permute-start.21 = (bf16[48,128]{1,0:T(8,128)(2,1)S(1)}, bf16[48,128]{1,0:T(8,128)(2,1)S(1)}, u32[]{:S(2)}, u32[]{:S(2)}) collective-permute-start(bf16[48,128]{1,0:T(8,128)(2,1)S(1)} %get-tuple-element.140), channel_id=1, source_target_pairs={{0,8},{1,121},{2,10},{3,123},{4,12},{5,125},{6,14},{7,127},{8,16},... | collective-permute-start | bytes 36872 | tf_op jit(solution)/shard_map/ppermute | solution.py:591
  137.2 1.5 collective-permute-start.22
  138.7 1.3 collective-permute-start.23
  140.0 0.7 shard_map.181.stats_ref
  140.6 1.7 %collective-permute-done.21.ns_ref = bf16[48,128]{1,0:T(8,128)(2,1)S(1)} collective-permute-done((bf16[48,128]{1,0:T(8,128)(2,1)S(1)}, bf16[48,128]{1,0:T(8,128)(2,1)S(1)}, u32[]{:S(2)}, u32[]{:S(2)}) %collective-permute-start.21) | collective-permute-done | bytes 12320 | tf_op jit(solution)/shard_map/ppermute | solution.py:591
  142.4 2.3 %shard_map.183 = (bf16[64,48,128]{2,1,0:T(8,128)(2,1)S(1)}, f32[128,128]{1,0:T(8,128)S(1)}) custom-call(s32[8]{0:T(128)S(1)} %shard_map.163.sc, bf16[64,48,128]{2,1,0:T(8,128)(2,1)S(1)} %get-tuple-element.137.raw_in, f32[2,48,128]{2,1,0:T(8,128)S(1)} %shard_map.181.stats_ref, bf16[144,128]{1,0:T(8,128)(2,1)S(1)} %collective-permute-done.20.their_ref.partner_ref, ...), custom_call_target="tpu_custom_call" | custom-call | tf_op jit(solution)/shard_map/pallas_call | solution.py:198
  144.7 21.1 %all_to_all.30 = f32[128,1,128]{2,1,0:T(1,128)S(1)} all-to-all(f32[128,1,128]{2,1,0:T(1,128)S(1)} %bitcast.68), channel_id=1, replica_groups=mesh['tile_0'=4,'tile_1'=4,'tile_2'=2,'tile_3'=2,'split'=2] {'tile_0','t..., dimensions={0} | all-to-all | bytes 131072 | tf_op jit(solution)/shard_map/all_to_all | solution.py:607
  165.8 1.3 shard_map.184
  167.2 1.1 copy.55
  (78 shorter events, 4.8 us)
Async XLA Ops:
  0.0 9.8 %copy-start = (f32[48,192]{1,0:T(8,128)S(1)}, f32[48,192]{1,0:T(8,128)}, u32[]{:S(2)}) copy-start(f32[48,192]{1,0:T(8,128)} %param.20) | copy-start | bytes 110596
  2.6 6.4 %collective-permute-start = (bf16[144,128]{1,0:T(8,128)(2,1)S(1)}, bf16[144,128]{1,0:T(8,128)(2,1)S(1)}, u32[]{:S(2)}, u32[]{:S(2)}) collective-permute-start(bf16[144,128]{1,0:T(8,128)(2,1)S(1)} %shard_map.164.mine_ref), channel_id=1, source_target_pairs={{0,1},{1,0},{2,3},{3,2},{4,5},{5,4},{6,7},{7,6},{8,9},{9,8},{10,11... | collective-permute-start | bytes 110600 | tf_op jit(solution)/shard_map/ppermute | solution.py:595
  7.1 0.7 copy-start.1
  9.8 4.1 %copy-start.13 = (f32[192,48]{0,1:T(8,128)S(1)}, f32[192,48]{0,1:T(8,128)}, u32[]{:S(2)}) copy-start(f32[192,48]{0,1:T(8,128)} %param.21) | copy-start | bytes 110596
  9.8 4.2 %copy-start.12 = (f32[192,96]{1,0:T(8,128)S(1)}, f32[192,96]{1,0:T(8,128)}, u32[]{:S(2)}) copy-start(f32[192,96]{1,0:T(8,128)} %param.22) | copy-start | bytes 221188
  10.0 7.1 %collective-permute-start.1 = (bf16[48,128]{1,0:T(8,128)(2,1)S(1)}, bf16[48,128]{1,0:T(8,128)(2,1)S(1)}, u32[]{:S(2)}, u32[]{:S(2)}) collective-permute-start(bf16[48,128]{1,0:T(8,128)(2,1)S(1)} %get-tuple-element.79), channel_id=1, source_target_pairs={{0,8},{1,121},{2,10},{3,123},{4,12},{5,125},{6,14},{7,127},{8,16},... | collective-permute-start | bytes 36872 | tf_op jit(solution)/shard_map/ppermute | solution.py:591
  11.7 5.4 %collective-permute-start.2 = (bf16[48,128]{1,0:T(8,128)(2,1)S(1)}, bf16[48,128]{1,0:T(8,128)(2,1)S(1)}, u32[]{:S(2)}, u32[]{:S(2)}) collective-permute-start(bf16[48,128]{1,0:T(8,128)(2,1)S(1)} %get-tuple-element.80), channel_id=1, source_target_pairs={{0,2},{2,0},{4,6},{6,4},{8,10},{10,8},{12,14},{14,12},{16,18},{18,... | collective-permute-start | bytes 36872 | tf_op jit(solution)/shard_map/ppermute | solution.py:600
  13.0 4.2 %collective-permute-start.3 = (bf16[48,128]{1,0:T(8,128)(2,1)S(1)}, bf16[48,128]{1,0:T(8,128)(2,1)S(1)}, u32[]{:S(2)}, u32[]{:S(2)}) collective-permute-start(bf16[48,128]{1,0:T(8,128)(2,1)S(1)} %get-tuple-element.81), channel_id=1, source_target_pairs={{0,126},{2,4},{4,2},{6,8},{8,6},{10,12},{12,10},{14,16},{16,14},{1... | collective-permute-start | bytes 36872 | tf_op jit(solution)/shard_map/ppermute | solution.py:599
  13.9 0.9 copy-start.8
  14.9 0.9 copy-start.10
  17.1 8.9 %copy-start.2 = (f32[4,48]{1,0:T(4,128)S(1)}, f32[4,48]{1,0:T(4,128)}, u32[]{:S(2)}) copy-start(f32[4,48]{1,0:T(4,128)} %rest_0_.1) | copy-start | bytes 2308
  17.1 8.9 %copy-start.3 = (f32[4,48]{1,0:T(4,128)S(1)}, f32[4,48]{1,0:T(4,128)}, u32[]{:S(2)}) copy-start(f32[4,48]{1,0:T(4,128)} %rest_1_.1) | copy-start | bytes 2308
  17.1 8.9 %copy-start.5 = (f32[2,96]{1,0:T(2,128)S(1)}, f32[2,96]{1,0:T(2,128)}, u32[]{:S(2)}) copy-start(f32[2,96]{1,0:T(2,128)} %rest_3_.1) | copy-start | bytes 2308
  20.1 6.0 %copy-start.4 = (f32[2,96]{1,0:T(2,128)S(1)}, f32[2,96]{1,0:T(2,128)}, u32[]{:S(2)}) copy-start(f32[2,96]{1,0:T(2,128)} %rest_2_.1) | copy-start | bytes 2308
  20.1 15.2 %copy-start.7 = (bf16[3,3,48,144]{3,2,1,0:T(8,128)(2,1)S(1)}, bf16[3,3,48,144]{3,2,1,0:T(8,128)(2,1)}, u32[]{:S(2)}) copy-start(bf16[3,3,48,144]{3,2,1,0:T(8,128)(2,1)} %param.27) | copy-start | bytes 373252
  20.1 14.4 %collective-permute-start.4 = (bf16[144,128]{1,0:T(8,128)(2,1)S(1)}, bf16[144,128]{1,0:T(8,128)(2,1)S(1)}, u32[]{:S(2)}, u32[]{:S(2)}) collective-permute-start(bf16[144,128]{1,0:T(8,128)(2,1)S(1)} %get-tuple-element.96.mine_ref), channel_id=1, source_target_pairs={{0,1},{1,0},{2,3},{3,2},{4,5},{5,4},{6,7},{7,6},{8,9},{9,8},{10,11... | collective-permute-start | bytes 110600 | tf_op jit(solution)/shard_map/ppermute | solution.py:595
  26.6 17.8 %all-to-all-start = ((f32[128,1,128]{2,1,0:T(1,128)}), f32[128,1,128]{2,1,0:T(1,128)S(1)}, u32[]{:S(2)}, u32[]{:S(2)}) async-start(f32[128,1,128]{2,1,0:T(1,128)} %bitcast.13), calls=%async_computation | async-start | bytes 131072 | tf_op jit(solution)/shard_map/all_to_all | solution.py:607
  35.5 7.0 %collective-permute-start.5 = (bf16[48,128]{1,0:T(8,128)(2,1)S(1)}, bf16[48,128]{1,0:T(8,128)(2,1)S(1)}, u32[]{:S(2)}, u32[]{:S(2)}) collective-permute-start(bf16[48,128]{1,0:T(8,128)(2,1)S(1)} %get-tuple-element.100), channel_id=1, source_target_pairs={{0,8},{1,121},{2,10},{3,123},{4,12},{5,125},{6,14},{7,127},{8,16},... | collective-permute-start | bytes 36872 | tf_op jit(solution)/shard_map/ppermute | solution.py:591
  37.2 5.3 %collective-permute-start.6 = (bf16[48,128]{1,0:T(8,128)(2,1)S(1)}, bf16[48,128]{1,0:T(8,128)(2,1)S(1)}, u32[]{:S(2)}, u32[]{:S(2)}) collective-permute-start(bf16[48,128]{1,0:T(8,128)(2,1)S(1)} %get-tuple-element.101), channel_id=1, source_target_pairs={{0,2},{2,0},{4,6},{6,4},{8,10},{10,8},{12,14},{14,12},{16,18},{18,... | collective-permute-start | bytes 36872 | tf_op jit(solution)/shard_map/ppermute | solution.py:600
  37.8 4.6 %collective-permute-start.7 = (bf16[48,128]{1,0:T(8,128)(2,1)S(1)}, bf16[48,128]{1,0:T(8,128)(2,1)S(1)}, u32[]{:S(2)}, u32[]{:S(2)}) collective-permute-start(bf16[48,128]{1,0:T(8,128)(2,1)S(1)} %get-tuple-element.102), channel_id=1, source_target_pairs={{0,126},{2,4},{4,2},{6,8},{8,6},{10,12},{12,10},{14,16},{16,14},{1... | collective-permute-start | bytes 36872 | tf_op jit(solution)/shard_map/ppermute | solution.py:599
  39.0 0.7 copy-start.14
  39.8 0.9 copy-start.11
  41.0 0.9 copy-start.6
  48.2 11.4 %collective-permute-start.8 = (bf16[288,128]{1,0:T(8,128)(2,1)S(1)}, bf16[288,128]{1,0:T(8,128)(2,1)S(1)}, u32[]{:S(2)}, u32[]{:S(2)}) collective-permute-start(bf16[288,128]{1,0:T(8,128)(2,1)S(1)} %get-tuple-element.115.mine_ref), channel_id=1, source_target_pairs={{0,1},{1,0},{2,3},{3,2},{4,5},{5,4},{6,7},{7,6},{8,9},{9,8},{10,11... | collective-permute-start | bytes 221192 | tf_op jit(solution)/shard_map/ppermute | solution.py:595
  52.5 11.4 %copy-start.9 = (bf16[3,3,96,48]{2,3,1,0:T(8,128)(2,1)S(1)}, bf16[3,3,96,48]{2,3,1,0:T(8,128)(2,1)}, u32[]{:S(2)}) copy-start(bf16[3,3,96,48]{2,3,1,0:T(8,128)(2,1)} %param.25) | copy-start | bytes 248836
  52.5 17.0 %all-to-all-start.1 = ((f32[128,1,128]{2,1,0:T(1,128)}), f32[128,1,128]{2,1,0:T(1,128)S(1)}, u32[]{:S(2)}, u32[]{:S(2)}) async-start(f32[128,1,128]{2,1,0:T(1,128)} %bitcast.25), calls=%async_computation.1 | async-start | bytes 131072 | tf_op jit(solution)/shard_map/all_to_all | solution.py:607
  60.4 9.8 %collective-permute-start.9 = (bf16[96,128]{1,0:T(8,128)(2,1)S(1)}, bf16[96,128]{1,0:T(8,128)(2,1)S(1)}, u32[]{:S(2)}, u32[]{:S(2)}) collective-permute-start(bf16[96,128]{1,0:T(8,128)(2,1)S(1)} %get-tuple-element.116), channel_id=1, source_target_pairs={{0,8},{1,121},{2,10},{3,123},{4,12},{5,125},{6,14},{7,127},{8,16},... | collective-permute-start | bytes 73736 | tf_op jit(solution)/shard_map/ppermute | solution.py:591
  62.1 8.1 %collective-permute-start.10 = (bf16[96,128]{1,0:T(8,128)(2,1)S(1)}, bf16[96,128]{1,0:T(8,128)(2,1)S(1)}, u32[]{:S(2)}, u32[]{:S(2)}) collective-permute-start(bf16[96,128]{1,0:T(8,128)(2,1)S(1)} %get-tuple-element.117), channel_id=1, source_target_pairs={{0,2},{2,0},{4,6},{6,4},{8,10},{10,8},{12,14},{14,12},{16,18},{18,... | collective-permute-start | bytes 73736 | tf_op jit(solution)/shard_map/ppermute | solution.py:600
  62.8 7.5 %collective-permute-start.11 = (bf16[96,128]{1,0:T(8,128)(2,1)S(1)}, bf16[96,128]{1,0:T(8,128)(2,1)S(1)}, u32[]{:S(2)}, u32[]{:S(2)}) collective-permute-start(bf16[96,128]{1,0:T(8,128)(2,1)S(1)} %get-tuple-element.118), channel_id=1, source_target_pairs={{0,126},{2,4},{4,2},{6,8},{8,6},{10,12},{12,10},{14,16},{16,14},{1... | collective-permute-start | bytes 73736 | tf_op jit(solution)/shard_map/ppermute | solution.py:599
  73.1 10.5 %collective-permute-start.12 = (bf16[288,128]{1,0:T(8,128)(2,1)S(1)}, bf16[288,128]{1,0:T(8,128)(2,1)S(1)}, u32[]{:S(2)}, u32[]{:S(2)}) collective-permute-start(bf16[288,128]{1,0:T(8,128)(2,1)S(1)} %get-tuple-element.122.mine_ref), channel_id=1, source_target_pairs={{0,1},{1,0},{2,3},{3,2},{4,5},{5,4},{6,7},{7,6},{8,9},{9,8},{10,11... | collective-permute-start | bytes 221192 | tf_op jit(solution)/shard_map/ppermute | solution.py:595
  75.7 17.8 %all-to-all-start.2 = ((f32[128,1,128]{2,1,0:T(1,128)}), f32[128,1,128]{2,1,0:T(1,128)S(1)}, u32[]{:S(2)}, u32[]{:S(2)}) async-start(f32[128,1,128]{2,1,0:T(1,128)} %bitcast.28), calls=%async_computation.2 | async-start | bytes 131072 | tf_op jit(solution)/shard_map/all_to_all | solution.py:607
  84.4 9.8 %collective-permute-start.13 = (bf16[96,128]{1,0:T(8,128)(2,1)S(1)}, bf16[96,128]{1,0:T(8,128)(2,1)S(1)}, u32[]{:S(2)}, u32[]{:S(2)}) collective-permute-start(bf16[96,128]{1,0:T(8,128)(2,1)S(1)} %get-tuple-element.123), channel_id=1, source_target_pairs={{0,8},{1,121},{2,10},{3,123},{4,12},{5,125},{6,14},{7,127},{8,16},... | collective-permute-start | bytes 73736 | tf_op jit(solution)/shard_map/ppermute | solution.py:591
  86.1 8.2 %collective-permute-start.14 = (bf16[96,128]{1,0:T(8,128)(2,1)S(1)}, bf16[96,128]{1,0:T(8,128)(2,1)S(1)}, u32[]{:S(2)}, u32[]{:S(2)}) collective-permute-start(bf16[96,128]{1,0:T(8,128)(2,1)S(1)} %get-tuple-element.124), channel_id=1, source_target_pairs={{0,2},{2,0},{4,6},{6,4},{8,10},{10,8},{12,14},{14,12},{16,18},{18,... | collective-permute-start | bytes 73736 | tf_op jit(solution)/shard_map/ppermute | solution.py:600
  86.8 7.5 %collective-permute-start.15 = (bf16[96,128]{1,0:T(8,128)(2,1)S(1)}, bf16[96,128]{1,0:T(8,128)(2,1)S(1)}, u32[]{:S(2)}, u32[]{:S(2)}) collective-permute-start(bf16[96,128]{1,0:T(8,128)(2,1)S(1)} %get-tuple-element.125), channel_id=1, source_target_pairs={{0,126},{2,4},{4,2},{6,8},{8,6},{10,12},{12,10},{14,16},{16,14},{1... | collective-permute-start | bytes 73736 | tf_op jit(solution)/shard_map/ppermute | solution.py:599
  97.3 10.5 %collective-permute-start.16 = (bf16[288,128]{1,0:T(8,128)(2,1)S(1)}, bf16[288,128]{1,0:T(8,128)(2,1)S(1)}, u32[]{:S(2)}, u32[]{:S(2)}) collective-permute-start(bf16[288,128]{1,0:T(8,128)(2,1)S(1)} %get-tuple-element.129.mine_ref), channel_id=1, source_target_pairs={{0,1},{1,0},{2,3},{3,2},{4,5},{5,4},{6,7},{7,6},{8,9},{9,8},{10,11... | collective-permute-start | bytes 221192 | tf_op jit(solution)/shard_map/ppermute | solution.py:595
  99.9 17.8 %all-to-all-start.3 = ((f32[128,1,128]{2,1,0:T(1,128)}), f32[128,1,128]{2,1,0:T(1,128)S(1)}, u32[]{:S(2)}, u32[]{:S(2)}) async-start(f32[128,1,128]{2,1,0:T(1,128)} %bitcast.31), calls=%async_computation.3 | async-start | bytes 131072 | tf_op jit(solution)/shard_map/all_to_all | solution.py:607
  108.6 9.8 %collective-permute-start.17 = (bf16[96,128]{1,0:T(8,128)(2,1)S(1)}, bf16[96,128]{1,0:T(8,128)(2,1)S(1)}, u32[]{:S(2)}, u32[]{:S(2)}) collective-permute-start(bf16[96,128]{1,0:T(8,128)(2,1)S(1)} %get-tuple-element.130), channel_id=1, source_target_pairs={{0,8},{1,121},{2,10},{3,123},{4,12},{5,125},{6,14},{7,127},{8,16},... | collective-permute-start | bytes 73736 | tf_op jit(solution)/shard_map/ppermute | solution.py:591
  110.3 8.1 %collective-permute-start.18 = (bf16[96,128]{1,0:T(8,128)(2,1)S(1)}, bf16[96,128]{1,0:T(8,128)(2,1)S(1)}, u32[]{:S(2)}, u32[]{:S(2)}) collective-permute-start(bf16[96,128]{1,0:T(8,128)(2,1)S(1)} %get-tuple-element.131), channel_id=1, source_target_pairs={{0,2},{2,0},{4,6},{6,4},{8,10},{10,8},{12,14},{14,12},{16,18},{18,... | collective-permute-start | bytes 73736 | tf_op jit(solution)/shard_map/ppermute | solution.py:600
  110.9 7.5 %collective-permute-start.19 = (bf16[96,128]{1,0:T(8,128)(2,1)S(1)}, bf16[96,128]{1,0:T(8,128)(2,1)S(1)}, u32[]{:S(2)}, u32[]{:S(2)}) collective-permute-start(bf16[96,128]{1,0:T(8,128)(2,1)S(1)} %get-tuple-element.132), channel_id=1, source_target_pairs={{0,126},{2,4},{4,2},{6,8},{8,6},{10,12},{12,10},{14,16},{16,14},{1... | collective-permute-start | bytes 73736 | tf_op jit(solution)/shard_map/ppermute | solution.py:599
  122.0 18.0 %all-to-all-start.4 = ((f32[128,1,128]{2,1,0:T(1,128)}), f32[128,1,128]{2,1,0:T(1,128)S(1)}, u32[]{:S(2)}, u32[]{:S(2)}) async-start(f32[128,1,128]{2,1,0:T(1,128)} %bitcast.34), calls=%async_computation.4 | async-start | bytes 131072 | tf_op jit(solution)/shard_map/all_to_all | solution.py:607
  129.9 4.8 %collective-permute-start.20 = (bf16[144,128]{1,0:T(8,128)(2,1)S(1)}, bf16[144,128]{1,0:T(8,128)(2,1)S(1)}, u32[]{:S(2)}, u32[]{:S(2)}) collective-permute-start(bf16[144,128]{1,0:T(8,128)(2,1)S(1)} %get-tuple-element.139.mine_ref), channel_id=1, source_target_pairs={{0,1},{1,0},{2,3},{3,2},{4,5},{5,4},{6,7},{7,6},{8,9},{9,8},{10,11... | collective-permute-start | bytes 110600 | tf_op jit(solution)/shard_map/ppermute | solution.py:595
  135.4 6.9 %collective-permute-start.21 = (bf16[48,128]{1,0:T(8,128)(2,1)S(1)}, bf16[48,128]{1,0:T(8,128)(2,1)S(1)}, u32[]{:S(2)}, u32[]{:S(2)}) collective-permute-start(bf16[48,128]{1,0:T(8,128)(2,1)S(1)} %get-tuple-element.140), channel_id=1, source_target_pairs={{0,8},{1,121},{2,10},{3,123},{4,12},{5,125},{6,14},{7,127},{8,16},... | collective-permute-start | bytes 36872 | tf_op jit(solution)/shard_map/ppermute | solution.py:591
  137.2 5.2 %collective-permute-start.22 = (bf16[48,128]{1,0:T(8,128)(2,1)S(1)}, bf16[48,128]{1,0:T(8,128)(2,1)S(1)}, u32[]{:S(2)}, u32[]{:S(2)}) collective-permute-start(bf16[48,128]{1,0:T(8,128)(2,1)S(1)} %get-tuple-element.141), channel_id=1, source_target_pairs={{0,2},{2,0},{4,6},{6,4},{8,10},{10,8},{12,14},{14,12},{16,18},{18,... | collective-permute-start | bytes 36872 | tf_op jit(solution)/shard_map/ppermute | solution.py:600
  138.7 3.7 %collective-permute-start.23 = (bf16[48,128]{1,0:T(8,128)(2,1)S(1)}, bf16[48,128]{1,0:T(8,128)(2,1)S(1)}, u32[]{:S(2)}, u32[]{:S(2)}) collective-permute-start(bf16[48,128]{1,0:T(8,128)(2,1)S(1)} %get-tuple-element.142), channel_id=1, source_target_pairs={{0,126},{2,4},{4,2},{6,8},{8,6},{10,12},{12,10},{14,16},{16,14},{1... | collective-permute-start | bytes 36872 | tf_op jit(solution)/shard_map/ppermute | solution.py:599
